TPU v7x, 256 devices: a whole 4x4x8 slice. The times are simulated.
256 devices in a mesh: row: 8 (over x, core), col: 32 (over y, z).
Axes of the slice: x: 4, y: 4, z: 8, core: 2. Of those that a mesh axis runs over, the one named last changes fastest.
Arguments:
- tensor: float32 [1024, 64, 4096], P(None, 'row', 'col'), may hold values from -60 to 60, as said below
- factor_two: float32 [64, 32], P('row'), may hold values from -0.75 to 0.75
- factor_three: float32 [128, 32], P('col'), may hold values from -0.5 to 0.5
- factor_four: float32 [32, 16], replicated, may hold values from -1 to 1
- factor_init: float32 [1024, 64], replicated, may hold values from -6 to 6
Outputs:
- factor_new: float32 [1024, 64], replicated
- core: float32 [64, 32, 32, 16], P(None, 'row', 'col')
Inputs may be any that keep to these rules, and one draw needn't show every extreme that they name: `tensor`: scales vary from slab to slab.
All inputs are finite; a program needn't handle non-finite values.
Results may differ from a plain program's by a relative error of at most 0.00013.
Values sent between devices are 32-bit elements; how exact they have to be, the bound alone decides.
No kernel may reach another device: no remote copies, remote signals or barrier semaphores. Data moves between devices by JAX's collectives and lax.ppermute only.
A program may use at most 128 MiB of HBM per device.

v0:
```python
import jax
import jax.numpy as jnp
from jax import lax
from jax.sharding import Mesh
from jax.sharding import PartitionSpec as P

ROW = ("row_0", "row_1")
COL = ("col_0", "col_1")


def from_everyone(array, axis):
    copies = jnp.broadcast_to(array, (lax.axis_size(axis), *array.shape))
    return lax.all_to_all(copies, axis, split_axis=0, concat_axis=0, tiled=True)


def joined_along(tiles, dim):
    shape = list(tiles.shape[1:])
    shape[dim] *= tiles.shape[0]
    return jnp.moveaxis(tiles, 0, dim).reshape(shape)


def gathered_copies(array, axis, dim):
    tiles = from_everyone(array, axis)
    return joined_along(tiles, dim)


def split_up(array, dim, length):
    shape = array.shape
    tiles = array.reshape(*shape[:dim], length, shape[dim] // length, *shape[dim + 1 :])
    return jnp.moveaxis(tiles, dim, 0)


def sent_and_summed(array, axis, dim):
    tiles = split_up(array, dim, lax.axis_size(axis))
    arrived = lax.all_to_all(tiles, axis, split_axis=0, concat_axis=0, tiled=True)
    return arrived.sum(axis=0)


def sum_by_axis(array, axes, dim):
    far, near = axes
    tiles = split_up(array, dim, lax.axis_size(far))
    nearer = sent_and_summed(tiles, near, dim + 1)
    arrived = lax.all_to_all(nearer, far, split_axis=0, concat_axis=0, tiled=True)
    return arrived.sum(axis=0)


def rows_for(lines, length):
    spare = -lines.shape[0] % length
    if not spare:
        return lines
    return jnp.concatenate([lines, jnp.zeros((spare, *lines.shape[1:]), lines.dtype)])


def gathered_by_axis(array, axes, dim):
    far, near = axes
    leading = from_everyone(array, far)
    tiles = jnp.swapaxes(from_everyone(leading, near), 0, 1)
    return joined_along(tiles.reshape(-1, *array.shape), dim)


def nested_sum(array, axes):
    lines = array.reshape(-1, array.shape[-1])
    own = sum_by_axis(rows_for(lines, lax.axis_size(axes[0]) * lax.axis_size(axes[1])), axes, 0)
    whole = gathered_by_axis(own, axes, 0)
    return whole[: len(lines)].reshape(array.shape)


def shards(tensor, factor_two, factor_three, factor_four, factor_init):
    highest = lax.Precision.HIGHEST
    first_len = tensor.shape[0]
    local_two = tensor.shape[1]
    fourth_len = factor_four.shape[0]
    local_three = tensor.shape[2] // fourth_len
    rank_one = factor_init.shape[1]
    data = tensor.reshape(first_len, local_two, local_three, fourth_len)
    fourth = jnp.einsum("abcd,de->abce", data, factor_four, precision=highest)
    whole_two = gathered_copies(factor_two, ROW, 0)
    spread_two = lax.all_to_all(fourth, ROW, split_axis=0, concat_axis=1, tiled=True)
    projected_two = jnp.einsum("abce,bg->agce", spread_two, whole_two, precision=highest)
    partial_two = lax.all_to_all(projected_two, ROW, split_axis=1, concat_axis=0, tiled=True)
    whole_three = gathered_copies(factor_three, COL, 0)
    spread_three = lax.all_to_all(partial_two, COL, split_axis=0, concat_axis=2, tiled=True)
    projected_three = jnp.einsum("agce,cf->agfe", spread_three, whole_three, precision=highest)
    block = lax.all_to_all(projected_three, COL, split_axis=2, concat_axis=0, tiled=True)
    columns = block.reshape(first_len, -1)
    basis = factor_init
    inner = jnp.dot(columns.T, basis, precision=highest, preferred_element_type=jnp.float32)
    local_image = jnp.dot(columns, inner, precision=highest, preferred_element_type=jnp.float32)
    image = nested_sum(local_image, (("row_0", "row_1"), ("col_0", "col_1")))
    square = jnp.dot(image.T, image, precision=highest, preferred_element_type=jnp.float32)
    lower = jnp.linalg.cholesky(square)
    basis = jax.scipy.linalg.solve_triangular(lower, image.T, lower=True).T
    core = jnp.dot(basis.T, columns, precision=highest, preferred_element_type=jnp.float32)
    return (basis, core.reshape(rank_one, block.shape[1], block.shape[2], block.shape[3]))


def solution(mesh):
    split = Mesh(mesh.devices.reshape(4, 2, 4, 8), ("row_0", "row_1", "col_0", "col_1"))
    in_specs = (P(None, ROW, COL), P(ROW, None), P(COL, None), P(), P())
    out_specs = (P(), P(None, ROW, COL, None))
    return jax.shard_map(
        shards, mesh=split, in_specs=in_specs, out_specs=out_specs, check_vma=False
    )
```

profile of v0, /device:TPU:32, one launch (start us, length us, event | category | flops | bytes accessed | tf_op | source)
XLA Modules:
  0.0 319.8 jit_solution(13342368360743462871)
XLA Ops:
  2.1 4.3 %all-to-all-start.1 = ((f32[8,1,256]{2,1,0:T(1,128)}), f32[8,1,256]{2,1,0:T(1,128)S(1)}, u32[]{:S(2)}, u32[]{:S(2)}) async-start(f32[8,1,256]{2,1,0:T(1,128)} %reshape.45), calls=%async_computation.1 | async-start | bytes 16384 | tf_op jit(solution)/shard_map/all_to_all | solution.py:13
  6.4 5.4 %copy.77 = f32[1024,8,128]{0,2,1:T(8,128)} copy(f32[1024,8,128]{2,1,0:T(8,128)} %param.5) | data formatting | bytes 8388608 | tf_op args[0]
  11.8 4.2 %fusion.18 = f32[1024,8,4,16]{0,3,2,1:T(8,128)S(1)} fusion(f32[1024,8,4,32]{0,3,2,1:T(8,128)} %bitcast.92, f32[32,16]{0,1:T(8,128)S(1)} %copy-done.2), kind=kOutput, calls=%fused_computation.24 | convolution fusion | flops 201326592 | bytes 6293504 | tf_op jit(solution)/shard_map/abcd,de->abce/dot_general | solution.py:76
  16.0 12.2 %copy.78 = f32[1024,8,4,16]{3,2,1,0:T(4,128)} copy(f32[1024,8,4,16]{0,3,2,1:T(8,128)S(1)} %fusion.18) | data formatting | bytes 4194304 | tf_op jit(solution)/shard_map/abcd,de->abce/dot_general | solution.py:76
  28.1 15.4 %reshape.43 = f32[8,1,65536]{2,1,0:T(1,128)} reshape(f32[1024,8,4,16]{3,2,1,0:T(4,128)} %copy.78) | data formatting | bytes 4194304
  43.5 5.0 %all-to-all-start = ((f32[8,1,65536]{2,1,0:T(1,128)}), f32[8,1,65536]{2,1,0:T(1,128)}, u32[]{:S(2)}, u32[]{:S(2)}) async-start(f32[8,1,65536]{2,1,0:T(1,128)} %reshape.43), calls=%async_computation | async-start | bytes 4194304 | tf_op jit(solution)/shard_map/all_to_all | solution.py:78
  49.8 25.8 %all-to-all-done = f32[8,1,65536]{2,1,0:T(1,128)} async-done(((f32[8,1,65536]{2,1,0:T(1,128)}), f32[8,1,65536]{2,1,0:T(1,128)}, u32[]{:S(2)}, u32[]{:S(2)}) %all-to-all-start) | async-done | bytes 2097184 | tf_op jit(solution)/shard_map/all_to_all | solution.py:78
  75.6 7.2 %reduce.6 = f32[8,65536]{1,0:T(8,128)S(1)} reduce(f32[8,1,65536]{2,1,0:T(1,128)} %all-to-all-done, f32[]{:T(128)} %broadcast.53), dimensions={1}, to_apply=%all_to_all.64.reduce_sub_computation | reduce | bytes 4194308 | tf_op jit(solution)/shard_map/all_to_all | solution.py:78
  82.8 17.4 %reshape.44 = f32[1024,8,4,16]{3,2,1,0:T(4,128)} reshape(f32[8,65536]{1,0:T(8,128)S(1)} %reduce.6) | data formatting | bytes 4194304
  100.2 10.0 %copy.106 = f32[8,128,8,4,16]{1,0,3,4,2:T(8,128)S(1)} copy(f32[8,128,8,4,16]{4,3,2,1,0:T(4,128)} %bitcast.89) | data formatting | bytes 4194304 | tf_op jit(solution)/shard_map/all_to_all | solution.py:78
  111.5 1.6 copy.81
  113.1 3.6 %all-to-all-start.2 = ((f32[128,32,4,16]{0,3,2,1:T(8,128)}), f32[128,32,4,16]{0,3,2,1:T(8,128)S(1)}, u32[]{:S(2)}, u32[]{:S(2)}) async-start(f32[128,32,4,16]{0,3,2,1:T(8,128)} %copy.81), calls=%async_computation.2 | async-start | bytes 2097152 | tf_op jit(solution)/shard_map/all_to_all | solution.py:80
  117.5 15.1 %all-to-all-done.2 = f32[128,32,4,16]{0,3,2,1:T(8,128)S(1)} async-done(((f32[128,32,4,16]{0,3,2,1:T(8,128)}), f32[128,32,4,16]{0,3,2,1:T(8,128)S(1)}, u32[]{:S(2)}, u32[]{:S(2)}) %all-to-all-start.2) | async-done | bytes 1048608 | tf_op jit(solution)/shard_map/all_to_all | solution.py:80
  132.6 11.4 %all-to-all-start.4 = ((f32[32,1,128]{2,1,0:T(1,128)}), f32[32,1,128]{2,1,0:T(1,128)S(1)}, u32[]{:S(2)}, u32[]{:S(2)}) async-start(f32[32,1,128]{2,1,0:T(1,128)} %reshape.49), calls=%async_computation.4 | async-start | bytes 32768 | tf_op jit(solution)/shard_map/all_to_all | solution.py:13
  143.9 6.1 %copy.110 = f32[8,128,4,4,16]{4,3,2,1,0:T(4,128)} copy(f32[8,128,4,4,16]{1,4,3,2,0:T(8,128)S(1)} %bitcast.93) | data formatting | bytes 2097152 | tf_op jit(solution)/shard_map/all_to_all | solution.py:80
  150.0 8.9 %reshape.47 = f32[32,1,8192]{2,1,0:T(1,128)} reshape(f32[1024,4,4,16]{3,2,1,0:T(4,128)} %bitcast.90) | data formatting | bytes 2097152
  159.0 10.4 %all-to-all-start.3 = ((f32[32,1,8192]{2,1,0:T(1,128)}), f32[32,1,8192]{2,1,0:T(1,128)S(1)}, u32[]{:S(2)}, u32[]{:S(2)}) async-start(f32[32,1,8192]{2,1,0:T(1,128)} %reshape.47), calls=%async_computation.3 | async-start | bytes 2097152 | tf_op jit(solution)/shard_map/all_to_all | solution.py:82
  170.1 26.8 %all-to-all-done.3 = f32[32,1,8192]{2,1,0:T(1,128)S(1)} async-done(((f32[32,1,8192]{2,1,0:T(1,128)}), f32[32,1,8192]{2,1,0:T(1,128)S(1)}, u32[]{:S(2)}, u32[]{:S(2)}) %all-to-all-start.3) | async-done | bytes 1048608 | tf_op jit(solution)/shard_map/all_to_all | solution.py:82
  196.9 3.2 %reduce.8 = f32[32,8192]{1,0:T(8,128)S(1)} reduce(f32[32,1,8192]{2,1,0:T(1,128)S(1)} %all-to-all-done.3, f32[]{:T(128)} %broadcast.53), dimensions={1}, to_apply=%all_to_all.72.reduce_sub_computation | reduce | bytes 2097156 | tf_op jit(solution)/shard_map/all_to_all | solution.py:82
  200.2 7.2 %reshape.48 = f32[1024,4,4,16]{3,2,1,0:T(4,128)} reshape(f32[32,8192]{1,0:T(8,128)S(1)} %reduce.8) | data formatting | bytes 2097152
  207.4 10.0 %copy.85 = f32[32,32,4,4,16]{0,1,3,4,2:T(8,128)} copy(f32[32,32,4,4,16]{4,3,2,1,0:T(4,128)} %bitcast.91) | data formatting | bytes 2097152 | tf_op jit(solution)/shard_map/all_to_all | solution.py:82
  217.4 5.6 %fusion.7 = f32[32,4,32,16]{2,0,3,1:T(8,128)S(1)} fusion(f32[32,32,4,4,16]{0,1,3,4,2:T(8,128)} %copy.85, f32[32,4,32,1,1]{2,1,0,4,3:T(4,128)S(1)} %bitcast.99), kind=kOutput, calls=%fused_computation.5 | convolution fusion | flops 100663296 | bytes 1327104 | tf_op jit(solution)/shard_map/agce,cf->agfe/dot_general | solution.py:83
  224.4 16.7 %all_to_all.93 = f32[32,1,2048]{2,1,0:T(1,128)S(1)} all-to-all(f32[32,1,2048]{2,1,0:T(1,128)S(1)} %reshape.51), channel_id=1, replica_groups=mesh['row_0'=4,'row_1'=2,'col_0'=4,'col_1'=8] {'col_0','col_1'}, dimensions={0} | all-to-all | bytes 524288 | tf_op jit(solution)/shard_map/all_to_all | solution.py:84
  242.8 1.6 copy.89
  245.4 1.7 reshape.33
  249.9 15.8 %all_to_all.94 = f32[32,1,2048]{2,1,0:T(1,128)S(1)} all-to-all(f32[32,1,2048]{2,1,0:T(1,128)S(1)} %reshape.53), channel_id=1, replica_groups=mesh['row_0'=4,'row_1'=2,'col_0'=4,'col_1'=8] {'col_0','col_1'}, dimensions={0} | all-to-all | bytes 524288 | tf_op jit(solution)/shard_map/all_to_all | solution.py:35
  267.6 7.7 %all_to_all.95 = f32[8,1,256]{2,1,0:T(1,128)S(1)} all-to-all(f32[8,1,256]{2,1,0:T(1,128)S(1)} %reshape.55), channel_id=1, replica_groups=mesh['row_0'=4,'row_1'=2,'col_0'=4,'col_1'=8] {'row_0','row_1'}, dimensions={0} | all-to-all | bytes 16384 | tf_op jit(solution)/shard_map/all_to_all | solution.py:43
  276.1 7.7 %all_to_all.96 = f32[8,1,256]{2,1,0:T(1,128)S(1)} all-to-all(f32[8,1,256]{2,1,0:T(1,128)S(1)} %reshape.57), channel_id=1, replica_groups=mesh['row_0'=4,'row_1'=2,'col_0'=4,'col_1'=8] {'row_0','row_1'}, dimensions={0} | all-to-all | bytes 16384 | tf_op jit(solution)/shard_map/all_to_all | solution.py:13
  285.2 16.8 %all_to_all.97 = f32[32,1,2048]{2,1,0:T(1,128)S(1)} all-to-all(f32[32,1,2048]{2,1,0:T(1,128)S(1)} %reshape.59), channel_id=1, replica_groups=mesh['row_0'=4,'row_1'=2,'col_0'=4,'col_1'=8] {'col_0','col_1'}, dimensions={0} | all-to-all | bytes 524288 | tf_op jit(solution)/shard_map/all_to_all | solution.py:13
  303.6 1.4 convolution_bitcast_fusion.1
  305.4 5.8 %cholesky.16 = f32[64,64]{1,0:T(8,128)S(1)} custom-call(f32[64,64]{1,0:T(8,128)S(1)} %fusion.16), custom_call_target="Cholesky" | custom-call | tf_op jit(solution)/shard_map/jit(cholesky)/cholesky | solution.py:91
  312.6 4.9 %custom-call.7 = f32[1,64,64]{1,2,0:T(8,128)S(1)} custom-call(f32[1,64,64]{2,1,0:T(8,128)S(1)} %fusion.13), custom_call_target="InvertDiagBlocksLowerTriangular" | custom-call | tf_op jit(solution)/shard_map/jit(_solve_triangular)/triangular_solve | solution.py:92
  (55 shorter events, 21.7 us)
Async XLA Ops:
  0.6 247.5 %copy-start = (f32[1024,64]{0,1:T(8,128)S(1)}, f32[1024,64]{0,1:T(8,128)}, u32[]{:S(2)}) copy-start(f32[1024,64]{0,1:T(8,128)} %param.9) | copy-start | bytes 786436
  2.1 41.5 %all-to-all-start.1 = ((f32[8,1,256]{2,1,0:T(1,128)}), f32[8,1,256]{2,1,0:T(1,128)S(1)}, u32[]{:S(2)}, u32[]{:S(2)}) async-start(f32[8,1,256]{2,1,0:T(1,128)} %reshape.45), calls=%async_computation.1 | async-start | bytes 16384 | tf_op jit(solution)/shard_map/all_to_all | solution.py:13
  6.4 5.4 %copy-start.2 = (f32[32,16]{0,1:T(8,128)S(1)}, f32[32,16]{0,1:T(8,128)}, u32[]{:S(2)}) copy-start(f32[32,16]{0,1:T(8,128)} %param.8) | copy-start | bytes 6148
  43.5 32.1 %all-to-all-start = ((f32[8,1,65536]{2,1,0:T(1,128)}), f32[8,1,65536]{2,1,0:T(1,128)}, u32[]{:S(2)}, u32[]{:S(2)}) async-start(f32[8,1,65536]{2,1,0:T(1,128)} %reshape.43), calls=%async_computation | async-start | bytes 4194304 | tf_op jit(solution)/shard_map/all_to_all | solution.py:78
  110.2 6.5 %copy-start.3 = (f32[4,32]{1,0:T(4,128)S(1)}, f32[4,32]{1,0:T(4,128)}, u32[]{:S(2)}) copy-start(f32[4,32]{1,0:T(4,128)} %param.7) | copy-start | bytes 1540
  113.1 19.4 %all-to-all-start.2 = ((f32[128,32,4,16]{0,3,2,1:T(8,128)}), f32[128,32,4,16]{0,3,2,1:T(8,128)S(1)}, u32[]{:S(2)}, u32[]{:S(2)}) async-start(f32[128,32,4,16]{0,3,2,1:T(8,128)} %copy.81), calls=%async_computation.2 | async-start | bytes 2097152 | tf_op jit(solution)/shard_map/all_to_all | solution.py:80
  132.6 26.4 %all-to-all-start.4 = ((f32[32,1,128]{2,1,0:T(1,128)}), f32[32,1,128]{2,1,0:T(1,128)S(1)}, u32[]{:S(2)}, u32[]{:S(2)}) async-start(f32[32,1,128]{2,1,0:T(1,128)} %reshape.49), calls=%async_computation.4 | async-start | bytes 32768 | tf_op jit(solution)/shard_map/all_to_all | solution.py:13
  159.0 38.0 %all-to-all-start.3 = ((f32[32,1,8192]{2,1,0:T(1,128)}), f32[32,1,8192]{2,1,0:T(1,128)S(1)}, u32[]{:S(2)}, u32[]{:S(2)}) async-start(f32[32,1,8192]{2,1,0:T(1,128)} %reshape.47), calls=%async_computation.3 | async-start | bytes 2097152 | tf_op jit(solution)/shard_map/all_to_all | solution.py:82
  318.6 1.0 copy-start.1
where the time goes:
time: 325 us; the launch traced here: 320 us
  local copies, waits for them, and re-layouts  107 us (33%)
  waiting for transfers between devices  67.8 us (21%)
  blocking collectives  64.7 us (20%)
  starting transfers between devices  34.6 us (11%)
  other arithmetic  29.1 us (9%)
  matrix products  15.2 us (5%)
    unnamed x27, local copies, waits for them, and re-layouts  58.7 us
    all_to_all x1, waiting for transfers between devices, shards(): lax.all_to_all(partial_two, COL, split_axis=0, concat_axis=2, tiled=True)  26.8 us
    all_to_all x1, waiting for transfers between devices, shards(): lax.all_to_all(fourth, ROW, split_axis=0, concat_axis=1, tiled=True)  25.8 us
    all_to_all x2, blocking collectives, from_everyone(): return lax.all_to_all(copies, axis, split_axis=0, concat_axis=0, tiled=True)  24.5 us
    all_to_all x1, blocking collectives, shards(): lax.all_to_all(projected_three, COL, split_axis=2, concat_axis=0, tiled=T...  16.7 us
    all_to_all x1, blocking collectives, sent_and_summed(): lax.all_to_all(tiles, axis, split_axis=0, concat_axis=0, tiled=True)  15.8 us
    all_to_all x2, starting transfers between devices, from_everyone(): return lax.all_to_all(copies, axis, split_axis=0, concat_axis=0, tiled=True)  15.7 us
    all_to_all x1, waiting for transfers between devices, shards(): lax.all_to_all(projected_two, ROW, split_axis=1, concat_axis=0, tiled=True)  15.1 us
  transfers between devices with their start and end apart: 5, of which 3 were waited for; matrix products, arithmetic and copies ran while one was open for 17% of the time, Pallas kernels for 0%

commit v1 on v0

v1 whole, which is shorter than its diff:
```python
import functools

import jax
import jax.numpy as jnp
from jax import lax
from jax.experimental import pallas as pl
from jax.experimental.pallas import tpu as pltpu
from jax.sharding import Mesh
from jax.sharding import PartitionSpec as P

ROW = ("x", "k")
COL = ("y", "z")
PLANE = ("x", "k", "y")
F32 = jnp.float32


def mm(a, b, left=1, right=0):
    return lax.dot_general(
        a, b, (((left,), (right,)), ((), ())),
        precision=lax.Precision.HIGHEST, preferred_element_type=F32,
    )


def call(body, outs, smem=(), n_in=0, flops=0):
    vm = pl.BlockSpec(memory_space=pltpu.VMEM)
    sm = pl.BlockSpec(memory_space=pltpu.SMEM)
    return pl.pallas_call(
        body,
        out_shape=[jax.ShapeDtypeStruct(s, F32) for s in outs],
        in_specs=[sm if i in smem else vm for i in range(n_in)],
        out_specs=[vm] * len(outs),
        cost_estimate=pl.CostEstimate(flops=flops, bytes_accessed=1 << 20, transcendentals=0),
    )


def first_mode(bt, x_ref, k4t):
    combs = []
    for b in range(0, 8, 2):
        pair = jnp.concatenate(
            [x_ref[pl.ds(b, 1024, stride=8), :], x_ref[pl.ds(b + 1, 1024, stride=8), :]], axis=1
        )
        z = mm(bt, pair)
        for h in range(2):
            m = mm(k4t, z[:, h * 128 : (h + 1) * 128], 1, 1)
            combs.append(jnp.concatenate([m[:32], m[32:]], axis=1))
    return combs


def start_body(x_ref, bt_ref, k4t_ref, f2_ref, out_ref):
    combs = first_mode(bt_ref[...], x_ref, k4t_ref[...])
    for b, comb in enumerate(combs):
        for c in range(4):
            out_ref[pl.ds(c * 8 + b, 8, stride=40), :] = comb[c * 8 : (c + 1) * 8]
    tail = jnp.concatenate([f2_ref[...], jnp.zeros((8, 96), F32)], axis=1)
    for i in range(8):
        out_ref[i * 40 + 32 : i * 40 + 40, :] = tail


def second_body(r_ref, f3_ref, out_ref, f2_ref):
    f2 = r_ref[:, 32:40, :].reshape(64, 128)[:, :32]
    f2_ref[...] = f2
    data = jnp.concatenate([r_ref[:, c * 8 : (c + 1) * 8, :].reshape(64, 128) for c in range(4)], axis=1)
    y = mm(f2, data, 0, 0)
    f3 = jnp.concatenate([f3_ref[...], jnp.zeros((4, 96), F32)], axis=1)
    for c in range(4):
        out_ref[pl.ds(c, 32, stride=8), :] = y[:, c * 128 : (c + 1) * 128]
        out_ref[pl.ds(4 + c, 32, stride=8), :] = jnp.broadcast_to(f3[c : c + 1], (32, 128))


def third_body(r_ref, out_ref):
    data = jnp.concatenate([r_ref[pl.ds(c, 32, stride=8), :] for c in range(4)], axis=0)
    f3 = jnp.concatenate([r_ref[pl.ds(4 + c, 32, stride=8), :] for c in range(4)], axis=0)[:, :32]
    q = mm(f3, mm(f3, data, 0, 0))
    for c in range(4):
        out_ref[pl.ds(c, 32, stride=4), :] = q[c * 32 : (c + 1) * 32]


def back_body(r_ref, f2_ref, out_ref):
    data = jnp.concatenate([r_ref[pl.ds(c, 32, stride=4), :] for c in range(4)], axis=1)
    y = mm(f2_ref[...], data)
    for c in range(4):
        out_ref[:, c * 8 : (c + 1) * 8, :] = y[:, c * 128 : (c + 1) * 128].reshape(8, 8, 128)


def image_body(r_ref, k4t_ref, x_ref, out_ref):
    top = jnp.zeros((512, 64), F32)
    low = jnp.zeros((512, 64), F32)
    for b in range(0, 8, 2):
        ws = []
        for h in range(2):
            w4 = jnp.concatenate([r_ref[pl.ds(c * 8 + b + h, 8, stride=32), :] for c in range(4)], axis=0)
            w4 = jnp.concatenate([w4[:, :64], w4[:, 64:]], axis=0)
            ws.append(mm(k4t_ref[...], w4, 0, 0))
        w = jnp.concatenate(ws, axis=0)
        pair = jnp.concatenate(
            [x_ref[pl.ds(b, 1024, stride=8), :], x_ref[pl.ds(b + 1, 1024, stride=8), :]], axis=1
        )
        full = mm(pair, w)
        top, low = top + full[:512], low + full[512:]
    out_ref[...] = jnp.concatenate([top, low], axis=1)


def sum_body(r_ref, out_ref):
    total = r_ref[0]
    for i in range(1, r_ref.shape[0]):
        total = total + r_ref[i]
    for i in range(out_ref.shape[0]):
        out_ref[i] = total


def core_two_body(image_ref, x_ref, k4t_ref, f2_ref, out_ref, turned_ref):
    flat = image_ref[...].T
    bt = jnp.concatenate([flat[:64], flat[64:]], axis=1)
    turned_ref[...] = bt
    combs = first_mode(bt, x_ref, k4t_ref[...])
    for g in range(32):
        total = f2_ref[0, g] * combs[0]
        for b in range(1, 8):
            total = total + f2_ref[b, g] * combs[b]
        out_ref[g * 32 : (g + 1) * 32, :] = total


def core_three_body(r_ref, f3_ref, out_ref):
    total = r_ref[0]
    for i in range(1, 8):
        total = total + r_ref[i]
    for f in range(32):
        for g in range(4):
            piece = f3_ref[0, f] * total[g * 32 : g * 32 + 8]
            for c in range(1, 4):
                piece = piece + f3_ref[c, f] * total[g * 32 + c * 8 : g * 32 + c * 8 + 8]
            out_ref[(f * 4 + g) * 8 : (f * 4 + g + 1) * 8, :] = piece


def core_body(r_ref, linv_ref, out_ref):
    total = r_ref[0]
    for i in range(1, 32):
        total = total + r_ref[i]
    parts = []
    for g in range(4):
        parts += [total[g * 8 : g * 8 + 8, :64], total[g * 8 : g * 8 + 8, 64:]]
    out_ref[...] = mm(jnp.concatenate(parts, axis=0), linv_ref[...], 1, 1)


def trade(block, axis):
    return lax.all_to_all(block, axis, split_axis=0, concat_axis=0, tiled=True)


def shards(tensor, factor_two, factor_three, factor_four, factor_init):
    x = tensor.reshape(8192, 128)
    k4t = (
        factor_four.T.reshape(2, 1, 8, 1, 32) * jnp.eye(4, dtype=F32).reshape(1, 4, 1, 4, 1)
    ).reshape(64, 128)
    (block,) = call(start_body, [(320, 128)], n_in=4, flops=10**9)(x, factor_init.T, k4t, factor_two)
    block = trade(block.reshape(8, 40, 128), ROW)
    block, whole_two = call(second_body, [(256, 128), (64, 32)], n_in=2, flops=10**7)(block, factor_three)
    block = trade(block.reshape(32, 8, 128), COL)
    (block,) = call(third_body, [(128, 128)], n_in=1, flops=10**7)(block.reshape(256, 128))
    block = trade(block.reshape(32, 4, 128), COL)
    (block,) = call(back_body, [(8, 32, 128)], n_in=2, flops=10**7)(block.reshape(128, 128), whole_two)
    block = trade(block, ROW)
    (image,) = call(image_body, [(512, 128)], n_in=3, flops=10**9)(block.reshape(256, 128), k4t, x)
    image = trade(image.reshape(32, 16, 128), PLANE)
    (image,) = call(sum_body, [(8, 16, 128)], n_in=1, flops=10**6)(image)
    image = trade(image, "z")
    (image,) = call(sum_body, [(32, 16, 128)], n_in=1, flops=10**6)(image)
    image = trade(image, PLANE)
    block, turned = call(core_two_body, [(1024, 128), (64, 1024)], smem=(3,), n_in=4, flops=10**9)(
        image.reshape(512, 128), x, k4t, factor_two
    )
    block = trade(block.reshape(8, 128, 128), ROW)
    square = mm(turned, turned, 1, 1)
    lower = jnp.linalg.cholesky(square)
    linv = jax.scipy.linalg.solve_triangular(lower, jnp.eye(64, dtype=F32), lower=True)
    basis = mm(linv, turned)
    (block,) = call(core_three_body, [(1024, 128)], smem=(1,), n_in=2, flops=10**7)(block, factor_three)
    block = trade(block.reshape(32, 32, 128), COL)
    (core,) = call(core_body, [(64, 64)], n_in=2, flops=10**7)(block, linv)
    return basis.T, core.reshape(4, 1, 16, 64).transpose(3, 0, 1, 2)


def solution(mesh):
    split = Mesh(mesh.devices.reshape(4, 2, 4, 8), ("x", "k", "y", "z"))
    in_specs = (P(None, ROW, COL), P(ROW, None), P(COL, None), P(), P())
    out_specs = (P(), P(None, ROW, COL, None))
    return jax.shard_map(shards, mesh=split, in_specs=in_specs, out_specs=out_specs, check_vma=False)
```

time: 325 us -> 176 us (0.54); the launches traced: 320 us -> 175 us
  local copies, waits for them, and re-layouts: 107 us -> 2.41 us
  waiting for transfers between devices: 67.8 us -> 13 us
  Pallas kernels: 0 us -> 39.1 us
  blocking collectives: 64.7 us -> 95.7 us
  starting transfers between devices: 34.6 us -> 8.62 us
  other arithmetic: 29.1 us -> 12.9 us
  matrix products: 15.2 us -> 2.73 us
    unnamed x27 -> x8, local copies, waits for them, and re-layouts: 58.7 us -> 1.6 us
    all_to_all x5 -> x2, waiting for transfers between devices: 67.8 us -> 13 us  [trade(): return lax.all_to_all(block, axis, split_axis=0, concat_axis=0, tiled=True)]
    pallas_call x0 -> x10, Pallas kernels: none -> 39.1 us  [the longest x1 10.4 us: shards(): call(image_body, [(512, 128)], n_in=3, flops=10 ** 9)]
    all_to_all x5 -> x7, blocking collectives: 64.7 us -> 95.7 us  [trade(): return lax.all_to_all(block, axis, split_axis=0, concat_axis=0, tiled=True)]
    all_to_all x8 -> x0, local copies, waits for them, and re-layouts: 29.6 us -> none  [the longest x2 10.5 us: shards(): lax.all_to_all(fourth, ROW, split_axis=0, concat_axis=1, tiled=True)]
    all_to_all x5 -> x2, starting transfers between devices: 34.6 us -> 8.62 us  [trade(): return lax.all_to_all(block, axis, split_axis=0, concat_axis=0, tiled=True)]
    all_to_all x9 -> x0, other arithmetic: 16.9 us -> none  [the longest x1 7.22 us: shards(): lax.all_to_all(fourth, ROW, split_axis=0, concat_axis=1, tiled=True)]
    dot_general x3 -> x1, local copies, waits for them, and re-layouts: 13.3 us -> 0.07 us  [mm(): lax.dot_general(a, b, (((left,), (right,)), ((), ())), precision=lax.Prec...]
  transfers between devices with their start and end apart: 5 -> 2, of which waited for: 3 -> 2; matrix products, arithmetic and copies ran while one was open for 17% -> 8% of each run, Pallas kernels for 0% -> 0%
where the time goes in v1:
time: 176 us; the launch traced here: 175 us
  blocking collectives  95.7 us (54%)
  Pallas kernels  39.1 us (22%)
  waiting for transfers between devices  13 us (7%)
  other arithmetic  12.9 us (7%)
  starting transfers between devices  8.62 us (5%)
  matrix products  2.73 us (2%)
  local copies, waits for them, and re-layouts  2.41 us (1%)
    all_to_all x7, blocking collectives, trade(): return lax.all_to_all(block, axis, split_axis=0, concat_axis=0, tiled=True)  95.7 us
    all_to_all x2, waiting for transfers between devices, trade(): return lax.all_to_all(block, axis, split_axis=0, concat_axis=0, tiled=True)  13 us
    pallas_call x1, Pallas kernels, shards(): call(image_body, [(512, 128)], n_in=3, flops=10 ** 9)  10.4 us
    all_to_all x2, starting transfers between devices, trade(): return lax.all_to_all(block, axis, split_axis=0, concat_axis=0, tiled=True)  8.62 us
    pallas_call x1, Pallas kernels, shards(): call(core_two_body, [(1024, 128), (64, 1024)], smem=(3,), n_in=4, flops=1...  8.11 us
    pallas_call x1, Pallas kernels, shards(): call(start_body, [(320, 128)], n_in=4, flops=10 ** 9)  7.89 us
    another operation x3, other arithmetic, shards(): lower = jnp.linalg.cholesky(square)  6.52 us
    another operation x2, other arithmetic, shards(): jax.scipy.linalg.solve_triangular(lower, jnp.eye(64, dtype=F32), lower=True)  5.55 us
  transfers between devices with their start and end apart: 2, of which 2 were waited for; matrix products, arithmetic and copies ran while one was open for 8% of the time, Pallas kernels for 0%

profile of v1, /device:TPU:32, one launch (start us, length us, event | category | flops | bytes accessed | tf_op | source)
XLA Modules:
  0.0 175.1 jit_solution(3112644731027999572)
XLA Ops:
  0.6 0.8 broadcast_multiply_fusion
  1.4 0.7 mul.23.k4t_ref
  2.2 7.9 %shard_map.68 = f32[320,128]{1,0:T(8,128)} custom-call(f32[8192,128]{1,0:T(8,128)} %bitcast.33, f32[64,1024]{1,0:T(8,128)} %bitcast.45, f32[64,128]{1,0:T(8,128)} %mul.23.k4t_ref, f32[8,32]{1,0:T(8,128)} %f2_ref.3), custom_call_target="tpu_custom_call" | custom-call | flops 1000000000 | bytes 1048576 | tf_op jit(solution)/shard_map/pallas_call | solution.py:154
  10.0 10.8 %all_to_all.45.r_ref = f32[8,40,128]{2,1,0:T(8,128)} all-to-all(f32[8,40,128]{2,1,0:T(8,128)} %bitcast.39), channel_id=1, replica_groups=mesh['x'=4,'k'=2,'y'=4,'z'=8] {'x','k'}, dimensions={0} | all-to-all | bytes 327680 | tf_op jit(solution)/shard_map/all_to_all | solution.py:146
  20.9 1.8 %shard_map.69 = (f32[256,128]{1,0:T(8,128)}, f32[64,32]{1,0:T(8,128)}) custom-call(f32[8,40,128]{2,1,0:T(8,128)} %all_to_all.45.r_ref, f32[4,32]{1,0:T(4,128)} %f3_ref.3), custom_call_target="tpu_custom_call" | custom-call | flops 10000000 | bytes 1048576 | tf_op jit(solution)/shard_map/pallas_call | solution.py:156
  22.7 21.1 %all_to_all.46 = f32[32,8,128]{2,1,0:T(8,128)} all-to-all(f32[32,8,128]{2,1,0:T(8,128)} %bitcast.46), channel_id=1, replica_groups=mesh['x'=4,'k'=2,'y'=4,'z'=8] {'y','z'}, dimensions={0} | all-to-all | bytes 262144 | tf_op jit(solution)/shard_map/all_to_all | solution.py:146
  43.9 2.0 %shard_map.70 = f32[128,128]{1,0:T(8,128)} custom-call(f32[256,128]{1,0:T(8,128)} %bitcast.42), custom_call_target="tpu_custom_call" | custom-call | flops 10000000 | bytes 1048576 | tf_op jit(solution)/shard_map/pallas_call | solution.py:158
  45.9 14.2 %all_to_all.47 = f32[32,4,128]{2,1,0:T(4,128)} all-to-all(f32[32,4,128]{2,1,0:T(4,128)} %bitcast.44), channel_id=1, replica_groups=mesh['x'=4,'k'=2,'y'=4,'z'=8] {'y','z'}, dimensions={0} | all-to-all | bytes 131072 | tf_op jit(solution)/shard_map/all_to_all | solution.py:146
  60.1 1.7 shard_map.71
  61.9 10.1 %all_to_all.48 = f32[8,32,128]{2,1,0:T(8,128)} all-to-all(f32[8,32,128]{2,1,0:T(8,128)} %shard_map.71), channel_id=1, replica_groups=mesh['x'=4,'k'=2,'y'=4,'z'=8] {'x','k'}, dimensions={0} | all-to-all | bytes 262144 | tf_op jit(solution)/shard_map/all_to_all | solution.py:146
  72.0 10.4 %shard_map.72 = f32[512,128]{1,0:T(8,128)} custom-call(f32[256,128]{1,0:T(8,128)} %bitcast.40, f32[64,128]{1,0:T(8,128)} %mul.23.k4t_ref, f32[8192,128]{1,0:T(8,128)} %bitcast.34), custom_call_target="tpu_custom_call" | custom-call | flops 1000000000 | bytes 1048576 | tf_op jit(solution)/shard_map/pallas_call | solution.py:162
  82.3 13.7 %all_to_all.49.r_ref = f32[32,16,128]{2,1,0:T(8,128)} all-to-all(f32[32,16,128]{2,1,0:T(8,128)} %bitcast.38), channel_id=1, replica_groups=mesh['x'=4,'k'=2,'y'=4,'z'=8] {'x','k','y'}, dimensions={0} | all-to-all | bytes 524288 | tf_op jit(solution)/shard_map/all_to_all | solution.py:146
  96.0 1.6 shard_map.73
  97.7 12.0 %all_to_all.50.r_ref = f32[8,16,128]{2,1,0:T(8,128)} all-to-all(f32[8,16,128]{2,1,0:T(8,128)} %shard_map.73), channel_id=1, replica_groups=mesh['x'=4,'k'=2,'y'=4,'z'=8] {'z'}, dimensions={0} | all-to-all | bytes 131072 | tf_op jit(solution)/shard_map/all_to_all | solution.py:146
  109.7 1.6 shard_map.74
  111.2 13.7 %all_to_all.51 = f32[32,16,128]{2,1,0:T(8,128)} all-to-all(f32[32,16,128]{2,1,0:T(8,128)} %shard_map.74), channel_id=1, replica_groups=mesh['x'=4,'k'=2,'y'=4,'z'=8] {'x','k','y'}, dimensions={0} | all-to-all | bytes 524288 | tf_op jit(solution)/shard_map/all_to_all | solution.py:146
  124.9 8.1 %shard_map.75 = (f32[1024,128]{1,0:T(8,128)}, f32[64,1024]{1,0:T(8,128)}) custom-call(f32[512,128]{1,0:T(8,128)} %bitcast.37, f32[8192,128]{1,0:T(8,128)} %bitcast.35, f32[64,128]{1,0:T(8,128)} %mul.23.k4t_ref, f32[8,32]{1,0:T(8,128)} %f2_ref.3), custom_call_target="tpu_custom_call" | custom-call | flops 1000000000 | bytes 1048576 | tf_op jit(solution)/shard_map/pallas_call | solution.py:168
  133.0 3.6 %all-to-all-start.7 = ((f32[8,128,128]{2,1,0:T(8,128)}), f32[8,128,128]{2,1,0:T(8,128)S(1)}, u32[]{:S(2)}, u32[]{:S(2)}) async-start(f32[8,128,128]{2,1,0:T(8,128)} %bitcast.41), calls=%async_computation.7 | async-start | bytes 1048576 | tf_op jit(solution)/shard_map/all_to_all | solution.py:146
  136.7 1.4 fusion.5
  138.2 8.7 %all-to-all-done.7.r_ref = f32[8,128,128]{2,1,0:T(8,128)S(1)} async-done(((f32[8,128,128]{2,1,0:T(8,128)}), f32[8,128,128]{2,1,0:T(8,128)S(1)}, u32[]{:S(2)}, u32[]{:S(2)}) %all-to-all-start.7) | async-done | bytes 524320 | tf_op jit(solution)/shard_map/all_to_all | solution.py:146
  146.9 0.8 copy-done.2
  147.7 2.0 %shard_map.76 = f32[1024,128]{1,0:T(8,128)} custom-call(f32[8,128,128]{2,1,0:T(8,128)} %copy-done.2, f32[4,32]{1,0:T(4,128)} %f3_ref.3), custom_call_target="tpu_custom_call" | custom-call | flops 10000000 | bytes 1048576 | tf_op jit(solution)/shard_map/pallas_call | solution.py:176
  149.7 5.0 %all-to-all-start.8 = ((f32[32,32,128]{2,1,0:T(8,128)}), f32[32,32,128]{2,1,0:T(8,128)S(1)}, u32[]{:S(2)}, u32[]{:S(2)}) async-start(f32[32,32,128]{2,1,0:T(8,128)} %bitcast.36), calls=%async_computation.8 | async-start | bytes 1048576 | tf_op jit(solution)/shard_map/all_to_all | solution.py:146
  154.7 5.8 %cholesky.17 = f32[64,64]{1,0:T(8,128)S(1)} custom-call(f32[64,64]{1,0:T(8,128)S(1)} %fusion.3), custom_call_target="Cholesky" | custom-call | tf_op jit(solution)/shard_map/jit(cholesky)/cholesky | solution.py:173
  160.6 0.6 compare_reduce_fusion
  161.3 0.7 fusion
  161.9 4.9 %custom-call.7 = f32[1,64,64]{1,2,0:T(8,128)S(1)} custom-call(f32[1,64,64]{2,1,0:T(8,128)S(1)} %fusion), custom_call_target="InvertDiagBlocksLowerTriangular" | custom-call | tf_op jit(solution)/shard_map/jit(_solve_triangular)/triangular_solve | solution.py:174
  166.8 0.2 fusion.1.linv_ref
  167.1 1.1 fusion.6
  168.2 4.3 %all-to-all-done.8.r_ref = f32[32,32,128]{2,1,0:T(8,128)S(1)} async-done(((f32[32,32,128]{2,1,0:T(8,128)}), f32[32,32,128]{2,1,0:T(8,128)S(1)}, u32[]{:S(2)}, u32[]{:S(2)}) %all-to-all-start.8) | async-done | bytes 524320 | tf_op jit(solution)/shard_map/all_to_all | solution.py:146
  172.4 0.8 copy-done.1
  173.2 1.9 %shard_map.77 = f32[64,64]{1,0:T(8,128)} custom-call(f32[32,32,128]{2,1,0:T(8,128)} %copy-done.1, f32[64,64]{1,0:T(8,128)} %copy-done.3), custom_call_target="tpu_custom_call" | custom-call | flops 10000000 | bytes 1048576 | tf_op jit(solution)/shard_map/pallas_call | solution.py:178
  (10 shorter events, 0.1 us)
Async XLA Ops:
  133.0 34.0 %copy-start = (f32[64,1024]{1,0:T(8,128)S(1)}, f32[64,1024]{1,0:T(8,128)}, u32[]{:S(2)}) copy-start(f32[64,1024]{1,0:T(8,128)} %get-tuple-element.8) | copy-start | bytes 786436
  133.0 13.9 %all-to-all-start.7 = ((f32[8,128,128]{2,1,0:T(8,128)}), f32[8,128,128]{2,1,0:T(8,128)S(1)}, u32[]{:S(2)}, u32[]{:S(2)}) async-start(f32[8,128,128]{2,1,0:T(8,128)} %bitcast.41), calls=%async_computation.7 | async-start | bytes 1048576 | tf_op jit(solution)/shard_map/all_to_all | solution.py:146
  146.9 0.8 copy-start.2
  149.7 22.7 %all-to-all-start.8 = ((f32[32,32,128]{2,1,0:T(8,128)}), f32[32,32,128]{2,1,0:T(8,128)S(1)}, u32[]{:S(2)}, u32[]{:S(2)}) async-start(f32[32,32,128]{2,1,0:T(8,128)} %bitcast.36), calls=%async_computation.8 | async-start | bytes 1048576 | tf_op jit(solution)/shard_map/all_to_all | solution.py:146
  167.1 5.4 %copy-start.3 = (f32[64,64]{1,0:T(8,128)}, f32[64,64]{1,0:T(8,128)S(1)}, u32[]{:S(2)}) copy-start(f32[64,64]{1,0:T(8,128)S(1)} %fusion.1.linv_ref) | copy-start | bytes 49156
  172.4 0.8 copy-start.1

commit v2 on v1

v2 whole, which is shorter than its diff:
```python
import jax
import jax.numpy as jnp
from jax import lax
from jax.experimental import pallas as pl
from jax.experimental.pallas import tpu as pltpu
from jax.sharding import Mesh
from jax.sharding import PartitionSpec as P

ROW = ("x", "k")
COL = ("y", "z")
PLANE = ("x", "k", "y")
F32 = jnp.float32
BF16 = jnp.bfloat16
HBM = pltpu.HBM
VMEM = pltpu.VMEM
SMEM = pltpu.SMEM


def mm(a, b, left=1, right=0):
    return lax.dot_general(
        a, b, (((left,), (right,)), ((), ())),
        precision=lax.Precision.HIGHEST, preferred_element_type=F32,
    )


def mm16(a, b):
    return jnp.dot(a, b, preferred_element_type=F32)


def halves(a):
    high = a.astype(BF16)
    return high, (a - high.astype(F32)).astype(BF16)


def call(body, outs, spaces, scratch=(), mib=4, flops=0):
    vmem = pl.BlockSpec(memory_space=pltpu.VMEM)
    specs = [pl.BlockSpec(memory_space=s) for s in spaces]
    return pl.pallas_call(
        body,
        out_shape=[jax.ShapeDtypeStruct(s, d) for s, d in outs],
        in_specs=specs,
        out_specs=[vmem] * len(outs),
        scratch_shapes=list(scratch),
        compiler_params=pltpu.CompilerParams(vmem_limit_bytes=mib << 20),
        cost_estimate=pl.CostEstimate(flops=flops, bytes_accessed=1 << 20, transcendentals=0),
    )


def fourth_matrix(f4t):
    wide = jnp.concatenate([f4t] * 4, axis=1)
    owner = lax.broadcasted_iota(jnp.int32, (8, 128), 1) // 32
    rows = [
        jnp.where(owner == c, wide[lo * 8 : lo * 8 + 8], 0.0) for lo in range(2) for c in range(4)
    ]
    return jnp.concatenate(rows, axis=0)


def fourth_mode(z, k4t):
    stack = jnp.concatenate([z[:, b * 128 : (b + 1) * 128] for b in range(8)], axis=0)
    m = mm(k4t, stack, 1, 1)
    return [
        jnp.concatenate([m[:32, b * 64 : b * 64 + 64], m[32:, b * 64 : b * 64 + 64]], axis=1)
        for b in range(8)
    ]


def start_body(x_ref, bt_ref, f4t_ref, f2_ref, out_ref, high_ref, low_ref, k4t_ref, held, sems):
    def copy(i):
        part = pl.ds(i * 2048, 2048)
        return pltpu.make_async_copy(x_ref.at[part], held.at[part], sems.at[i])

    for i in range(4):
        copy(i).start()
    k4t = fourth_matrix(f4t_ref[...])
    k4t_ref[...] = k4t
    tail = jnp.concatenate([f2_ref[...], jnp.zeros((8, 96), F32)], axis=1)
    for i in range(8):
        out_ref[i * 40 + 32 : i * 40 + 40, :] = tail
    bt_high, bt_low = halves(bt_ref[...])
    both = jnp.concatenate([bt_high, bt_low], axis=0)
    z = jnp.zeros((64, 1024), F32)
    for i in range(4):
        copy(i).wait()
        rows = slice(i * 256, i * 256 + 256)
        for b in range(8):
            high, low = halves(held[pl.ds(i * 2048 + b, 256, stride=8), :])
            high_ref[rows, b * 128 : b * 128 + 128] = high
            low_ref[rows, b * 128 : b * 128 + 128] = low
        major = mm16(both[:, rows], high_ref[rows, :])
        z = z + major[:64] + major[64:] + mm16(bt_high[:, rows], low_ref[rows, :])
    for b, comb in enumerate(fourth_mode(z, k4t)):
        for c in range(4):
            out_ref[pl.ds(c * 8 + b, 8, stride=40), :] = comb[c * 8 : (c + 1) * 8]


def second_body(r_ref, f3_ref, out_ref, f2_ref):
    f2 = r_ref[:, 32:40, :].reshape(64, 128)[:, :32]
    f2_ref[...] = f2
    data = jnp.concatenate([r_ref[:, c * 8 : (c + 1) * 8, :].reshape(64, 128) for c in range(4)], axis=1)
    y = mm(f2, data, 0, 0)
    f3 = jnp.concatenate([f3_ref[...], jnp.zeros((4, 96), F32)], axis=1)
    for c in range(4):
        out_ref[pl.ds(c, 32, stride=8), :] = y[:, c * 128 : (c + 1) * 128]
        out_ref[pl.ds(4 + c, 32, stride=8), :] = jnp.broadcast_to(f3[c : c + 1], (32, 128))


def third_body(r_ref, out_ref):
    data = jnp.concatenate([r_ref[pl.ds(c, 32, stride=8), :] for c in range(4)], axis=0)
    f3 = jnp.concatenate([r_ref[pl.ds(4 + c, 32, stride=8), :] for c in range(4)], axis=0)[:, :32]
    q = mm(f3, mm(f3, data, 0, 0))
    for c in range(4):
        out_ref[pl.ds(c, 32, stride=4), :] = q[c * 32 : (c + 1) * 32]


def back_body(r_ref, f2_ref, out_ref):
    data = jnp.concatenate([r_ref[pl.ds(c, 32, stride=4), :] for c in range(4)], axis=1)
    y = mm(f2_ref[...], data)
    for c in range(4):
        out_ref[:, c * 8 : (c + 1) * 8, :] = y[:, c * 128 : (c + 1) * 128].reshape(8, 8, 128)


def image_body(r_ref, k4t_ref, high_ref, low_ref, out_ref):
    ws = []
    for b in range(8):
        w4 = jnp.concatenate([r_ref[pl.ds(c * 8 + b, 8, stride=32), :] for c in range(4)], axis=0)
        ws.append(jnp.concatenate([w4[:, :64], w4[:, 64:]], axis=0))
    w = mm(k4t_ref[...], jnp.concatenate(ws, axis=1), 0, 0)
    w = jnp.concatenate([w[:, b * 64 : b * 64 + 64] for b in range(8)], axis=0)
    w_high, w_low = halves(w)
    none = jnp.zeros((1024, 64), BF16)
    first = jnp.concatenate([w_high, w_low], axis=1)
    second = jnp.concatenate([w_low, w_high], axis=1)
    left = jnp.concatenate([w_high, none], axis=1)
    right = jnp.concatenate([none, w_high], axis=1)
    half = lax.broadcasted_iota(jnp.int32, (128, 128), 1) < 64
    for i in range(4):
        top = slice(i * 128, i * 128 + 128)
        low = slice(512 + i * 128, 512 + i * 128 + 128)
        t = mm16(high_ref[top, :], first)
        u = mm16(high_ref[low, :], second)
        rest = mm16(low_ref[top, :], left) + mm16(low_ref[low, :], right)
        out_ref[top, :] = jnp.where(half, t, u) + pltpu.roll(jnp.where(half, u, t), 64, 1) + rest


def sum_body(r_ref, out_ref):
    total = r_ref[0]
    for i in range(1, r_ref.shape[0]):
        total = total + r_ref[i]
    for i in range(out_ref.shape[0]):
        out_ref[i] = total


def core_two_body(image_ref, high_ref, low_ref, k4t_ref, f2_ref, out_ref, turned_ref):
    flat = image_ref[...].T
    bt = jnp.concatenate([flat[:64], flat[64:]], axis=1)
    turned_ref[...] = bt
    bt_high, bt_low = halves(bt)
    major = mm16(jnp.concatenate([bt_high, bt_low], axis=0), high_ref[...])
    z = major[:64] + major[64:] + mm16(bt_high, low_ref[...])
    combs = fourth_mode(z, k4t_ref[...])
    for g in range(32):
        total = f2_ref[0, g] * combs[0]
        for b in range(1, 8):
            total = total + f2_ref[b, g] * combs[b]
        out_ref[g * 32 : (g + 1) * 32, :] = total


def core_three_body(r_ref, f3_ref, out_ref):
    total = r_ref[0]
    for i in range(1, 8):
        total = total + r_ref[i]
    for f in range(32):
        for g in range(4):
            piece = f3_ref[0, f] * total[g * 32 : g * 32 + 8]
            for c in range(1, 4):
                piece = piece + f3_ref[c, f] * total[g * 32 + c * 8 : g * 32 + c * 8 + 8]
            out_ref[(f * 4 + g) * 8 : (f * 4 + g + 1) * 8, :] = piece


def core_body(r_ref, linv_ref, out_ref):
    total = r_ref[0]
    for i in range(1, 32):
        total = total + r_ref[i]
    parts = []
    for g in range(4):
        parts += [total[g * 8 : g * 8 + 8, :64], total[g * 8 : g * 8 + 8, 64:]]
    out_ref[...] = mm(jnp.concatenate(parts, axis=0), linv_ref[...], 1, 1)


def trade(block, axis):
    return lax.all_to_all(block, axis, split_axis=0, concat_axis=0, tiled=True)


def shards(tensor, factor_two, factor_three, factor_four, factor_init):
    x = tensor.reshape(8192, 128)
    block, high, low, k4t = call(
        start_body,
        [((320, 128), F32), ((1024, 1024), BF16), ((1024, 1024), BF16), ((64, 128), F32)],
        (HBM, VMEM, VMEM, VMEM),
        scratch=(pltpu.VMEM((8192, 128), F32), pltpu.SemaphoreType.DMA((4,))),
        mib=48, flops=10**9,
    )(x, factor_init.T, factor_four.T, factor_two)
    block = trade(block.reshape(8, 40, 128), ROW)
    block, whole_two = call(second_body, [((256, 128), F32), ((64, 32), F32)], (VMEM, VMEM), flops=10**7)(
        block, factor_three
    )
    block = trade(block.reshape(32, 8, 128), COL)
    (block,) = call(third_body, [((128, 128), F32)], (VMEM,), flops=10**7)(block.reshape(256, 128))
    block = trade(block.reshape(32, 4, 128), COL)
    (block,) = call(back_body, [((8, 32, 128), F32)], (VMEM, VMEM), flops=10**7)(block.reshape(128, 128), whole_two)
    block = trade(block, ROW)
    (image,) = call(image_body, [((512, 128), F32)], (VMEM,) * 4, mib=12, flops=10**9)(
        block.reshape(256, 128), k4t, high, low
    )
    image = trade(image.reshape(32, 16, 128), PLANE)
    (image,) = call(sum_body, [((8, 16, 128), F32)], (VMEM,), flops=10**6)(image)
    image = trade(image, "z")
    (image,) = call(sum_body, [((32, 16, 128), F32)], (VMEM,), flops=10**6)(image)
    image = trade(image, PLANE)
    block, turned = call(
        core_two_body, [((1024, 128), F32), ((64, 1024), F32)], (VMEM,) * 4 + (SMEM,), mib=12, flops=10**9
    )(image.reshape(512, 128), high, low, k4t, factor_two)
    block = trade(block.reshape(8, 128, 128), ROW)
    square = mm(turned, turned, 1, 1)
    lower = jnp.linalg.cholesky(square)
    linv = jax.scipy.linalg.solve_triangular(lower, jnp.eye(64, dtype=F32), lower=True)
    basis = mm(linv, turned)
    (block,) = call(core_three_body, [((1024, 128), F32)], (VMEM, SMEM), flops=10**7)(block, factor_three)
    block = trade(block.reshape(32, 32, 128), COL)
    (core,) = call(core_body, [((64, 64), F32)], (VMEM, VMEM), flops=10**7)(block, linv)
    return basis.T, core.reshape(4, 1, 16, 64).transpose(3, 0, 1, 2)


def solution(mesh):
    split = Mesh(mesh.devices.reshape(4, 2, 4, 8), ("x", "k", "y", "z"))
    in_specs = (P(None, ROW, COL), P(ROW, None), P(COL, None), P(), P())
    out_specs = (P(), P(None, ROW, COL, None))
    return jax.shard_map(shards, mesh=split, in_specs=in_specs, out_specs=out_specs, check_vma=False)
```

time: 176 us -> 141 us (0.80)
  Pallas kernels: 39.1 us -> 12 us
  blocking collectives: 95.7 us -> 88.8 us
    pallas_call x10, Pallas kernels: 39.1 us -> 12 us  [the longest x1 3.81 us: shards(): call(start_body, [((320, 128), F32), ((1024, 1024), BF16), ((1024, 1024),...]
    all_to_all x7, blocking collectives: 95.7 us -> 88.8 us  [trade(): return lax.all_to_all(block, axis, split_axis=0, concat_axis=0, tiled=True)]
  transfers between devices with their start and end apart: 2 -> 2, of which waited for: 2 -> 2; matrix products, arithmetic and copies ran while one was open for 8% -> 10% of each run, Pallas kernels for 0% -> 0%
where the time goes in v2:
time: 141 us; the launch traced here: 140 us
  blocking collectives  88.8 us (63%)
  waiting for transfers between devices  14.1 us (10%)
  other arithmetic  12.1 us (9%)
  Pallas kernels  12 us (9%)
  starting transfers between devices  8.49 us (6%)
  local copies, waits for them, and re-layouts  2.4 us (2%)
  matrix products  1.66 us (1%)
    all_to_all x7, blocking collectives, trade(): return lax.all_to_all(block, axis, split_axis=0, concat_axis=0, tiled=True)  88.8 us
    all_to_all x2, waiting for transfers between devices, trade(): return lax.all_to_all(block, axis, split_axis=0, concat_axis=0, tiled=True)  14.1 us
    all_to_all x2, starting transfers between devices, trade(): return lax.all_to_all(block, axis, split_axis=0, concat_axis=0, tiled=True)  8.49 us
    another operation x3, other arithmetic, shards(): lower = jnp.linalg.cholesky(square)  6.52 us
    another operation x2, other arithmetic, shards(): jax.scipy.linalg.solve_triangular(lower, jnp.eye(64, dtype=F32), lower=True)  5.55 us
    pallas_call x1, Pallas kernels, shards(): call(start_body, [((320, 128), F32), ((1024, 1024), BF16), ((1024, 1024),...  3.81 us
  transfers between devices with their start and end apart: 2, of which 2 were waited for; matrix products, arithmetic and copies ran while one was open for 10% of the time, Pallas kernels for 0%

profile of v2, /device:TPU:32, one launch (start us, length us, event | category | flops | bytes accessed | tf_op | source)
XLA Modules:
  0.0 140.3 jit_solution(15890829313000110088)
XLA Ops:
  0.6 0.0 copy-start
  0.6 0.9 copy-done
  1.6 0.7 copy-done.1
  2.3 0.7 copy-done.2
  3.0 3.8 %shard_map.68 = (f32[320,128]{1,0:T(8,128)S(1)}, bf16[1024,1024]{1,0:T(8,128)(2,1)S(1)}, bf16[1024,1024]{1,0:T(8,128)(2,1)S(1)}, f32[64,128]{1,0:T(8,128)S(1)}) custom-call(f32[8192,128]{1,0:T(8,128)} %bitcast.41, f32[64,1024]{1,0:T(8,128)S(1)} %bitcast.35, f32[16,32]{1,0:T(8,128)S(1)} %bitcast.40, f32[8,32]{1,0:T(8,128)S(1)} %copy-done.1), custom_call_target="tpu_custom_call" | custom-call | flops 1000000000 | bytes 1048576 | tf_op jit(solution)/shard_map/pallas_call | solution.py:196
  6.8 10.6 %all_to_all.45.r_ref = f32[8,40,128]{2,1,0:T(8,128)S(1)} all-to-all(f32[8,40,128]{2,1,0:T(8,128)S(1)} %bitcast.38), channel_id=1, replica_groups=mesh['x'=4,'k'=2,'y'=4,'z'=8] {'x','k'}, dimensions={0} | all-to-all | bytes 327680 | tf_op jit(solution)/shard_map/all_to_all | solution.py:191
  17.3 0.0 copy-done.3
  17.3 0.3 shard_map.69
  17.6 20.8 %all_to_all.46 = f32[32,8,128]{2,1,0:T(8,128)S(1)} all-to-all(f32[32,8,128]{2,1,0:T(8,128)S(1)} %bitcast.39), channel_id=1, replica_groups=mesh['x'=4,'k'=2,'y'=4,'z'=8] {'y','z'}, dimensions={0} | all-to-all | bytes 262144 | tf_op jit(solution)/shard_map/all_to_all | solution.py:191
  38.4 0.5 shard_map.70
  38.9 13.3 %all_to_all.47 = f32[32,4,128]{2,1,0:T(4,128)S(1)} all-to-all(f32[32,4,128]{2,1,0:T(4,128)S(1)} %bitcast.37), channel_id=1, replica_groups=mesh['x'=4,'k'=2,'y'=4,'z'=8] {'y','z'}, dimensions={0} | all-to-all | bytes 131072 | tf_op jit(solution)/shard_map/all_to_all | solution.py:191
  52.2 0.2 shard_map.71
  52.5 8.5 %all_to_all.48 = f32[8,32,128]{2,1,0:T(8,128)S(1)} all-to-all(f32[8,32,128]{2,1,0:T(8,128)S(1)} %shard_map.71), channel_id=1, replica_groups=mesh['x'=4,'k'=2,'y'=4,'z'=8] {'x','k'}, dimensions={0} | all-to-all | bytes 262144 | tf_op jit(solution)/shard_map/all_to_all | solution.py:191
  61.0 2.0 %shard_map.72 = f32[512,128]{1,0:T(8,128)S(1)} custom-call(f32[256,128]{1,0:T(8,128)S(1)} %bitcast.33, f32[64,128]{1,0:T(8,128)S(1)} %get-tuple-element.13.k4t_ref, bf16[1024,1024]{1,0:T(8,128)(2,1)S(1)} %get-tuple-element.14.high_ref, bf16[1024,1024]{1,0:T(8,128)(2,1)S(1)} %get-tuple-element.15.low_ref), custom_call_target="tpu_custom_call" | custom-call | flops 1000000000 | bytes 1048576 | tf_op jit(solution)/shard_map/pallas_call | solution.py:212
  63.0 12.5 %all_to_all.49.r_ref = f32[32,16,128]{2,1,0:T(8,128)S(1)} all-to-all(f32[32,16,128]{2,1,0:T(8,128)S(1)} %bitcast.32), channel_id=1, replica_groups=mesh['x'=4,'k'=2,'y'=4,'z'=8] {'x','k','y'}, dimensions={0} | all-to-all | bytes 524288 | tf_op jit(solution)/shard_map/all_to_all | solution.py:191
  75.5 10.5 %all_to_all.50.r_ref = f32[8,16,128]{2,1,0:T(8,128)S(1)} all-to-all(f32[8,16,128]{2,1,0:T(8,128)S(1)} %shard_map.73), channel_id=1, replica_groups=mesh['x'=4,'k'=2,'y'=4,'z'=8] {'z'}, dimensions={0} | all-to-all | bytes 131072 | tf_op jit(solution)/shard_map/all_to_all | solution.py:191
  86.0 12.7 %all_to_all.51 = f32[32,16,128]{2,1,0:T(8,128)S(1)} all-to-all(f32[32,16,128]{2,1,0:T(8,128)S(1)} %shard_map.74), channel_id=1, replica_groups=mesh['x'=4,'k'=2,'y'=4,'z'=8] {'x','k','y'}, dimensions={0} | all-to-all | bytes 524288 | tf_op jit(solution)/shard_map/all_to_all | solution.py:191
  98.7 2.8 %shard_map.75 = (f32[1024,128]{1,0:T(8,128)}, f32[64,1024]{1,0:T(8,128)S(1)}) custom-call(f32[512,128]{1,0:T(8,128)S(1)} %bitcast.31, bf16[1024,1024]{1,0:T(8,128)(2,1)S(1)} %get-tuple-element.14.high_ref, bf16[1024,1024]{1,0:T(8,128)(2,1)S(1)} %get-tuple-element.15.low_ref, f32[64,128]{1,0:T(8,128)S(1)} %get-tuple-element.13.k4t_ref, f32[8,32]{1,0:T(8,128)S(1)} %copy-done.1), custom_call_target="tpu_custom_call" | custom-call | flops 1000000000 | bytes 1048576 | tf_op jit(solution)/shard_map/pallas_call | solution.py:220
  101.5 3.5 %all-to-all-start.7 = ((f32[8,128,128]{2,1,0:T(8,128)}), f32[8,128,128]{2,1,0:T(8,128)S(1)}, u32[]{:S(2)}, u32[]{:S(2)}) async-start(f32[8,128,128]{2,1,0:T(8,128)} %bitcast.14), calls=%async_computation.7 | async-start | bytes 1048576 | tf_op jit(solution)/shard_map/all_to_all | solution.py:191
  105.0 0.4 fusion.4
  105.4 0.1 copy.7
  105.5 9.8 %all-to-all-done.7.r_ref = f32[8,128,128]{2,1,0:T(8,128)S(1)} async-done(((f32[8,128,128]{2,1,0:T(8,128)}), f32[8,128,128]{2,1,0:T(8,128)S(1)}, u32[]{:S(2)}, u32[]{:S(2)}) %all-to-all-start.7) | async-done | bytes 524320 | tf_op jit(solution)/shard_map/all_to_all | solution.py:191
  115.3 1.5 %shard_map.76 = f32[1024,128]{1,0:T(8,128)} custom-call(f32[8,128,128]{2,1,0:T(8,128)S(1)} %all-to-all-done.7.r_ref, f32[4,32]{1,0:T(4,128)S(1)} %copy-done.3), custom_call_target="tpu_custom_call" | custom-call | flops 10000000 | bytes 1048576 | tf_op jit(solution)/shard_map/pallas_call | solution.py:228
  116.8 5.0 %all-to-all-start.8 = ((f32[32,32,128]{2,1,0:T(8,128)}), f32[32,32,128]{2,1,0:T(8,128)S(1)}, u32[]{:S(2)}, u32[]{:S(2)}) async-start(f32[32,32,128]{2,1,0:T(8,128)} %bitcast.15), calls=%async_computation.8 | async-start | bytes 1048576 | tf_op jit(solution)/shard_map/all_to_all | solution.py:191
  121.8 5.8 %cholesky.17 = f32[64,64]{1,0:T(8,128)S(1)} custom-call(f32[64,64]{1,0:T(8,128)S(1)} %fusion.3), custom_call_target="Cholesky" | custom-call | tf_op jit(solution)/shard_map/jit(cholesky)/cholesky | solution.py:225
  127.7 0.6 compare_reduce_fusion
  128.3 0.7 fusion
  129.0 4.9 %custom-call.7 = f32[1,64,64]{1,2,0:T(8,128)S(1)} custom-call(f32[1,64,64]{2,1,0:T(8,128)S(1)} %fusion), custom_call_target="InvertDiagBlocksLowerTriangular" | custom-call | tf_op jit(solution)/shard_map/jit(_solve_triangular)/triangular_solve | solution.py:226
  133.9 0.2 fusion.1.linv_ref
  134.1 1.1 fusion.5
  135.2 4.3 %all-to-all-done.8.r_ref = f32[32,32,128]{2,1,0:T(8,128)S(1)} async-done(((f32[32,32,128]{2,1,0:T(8,128)}), f32[32,32,128]{2,1,0:T(8,128)S(1)}, u32[]{:S(2)}, u32[]{:S(2)}) %all-to-all-start.8) | async-done | bytes 524320 | tf_op jit(solution)/shard_map/all_to_all | solution.py:191
  139.5 0.9 shard_map.77
  (7 shorter events, 0.1 us)
Async XLA Ops:
  0.6 1.0 copy-start
  1.6 0.7 copy-start.1
  2.3 0.7 copy-start.2
  3.0 14.4 %copy-start.3 = (f32[4,32]{1,0:T(4,128)S(1)}, f32[4,32]{1,0:T(4,128)}, u32[]{:S(2)}) copy-start(f32[4,32]{1,0:T(4,128)} %f3_ref.3) | copy-start | bytes 1540
  101.5 13.7 %all-to-all-start.7 = ((f32[8,128,128]{2,1,0:T(8,128)}), f32[8,128,128]{2,1,0:T(8,128)S(1)}, u32[]{:S(2)}, u32[]{:S(2)}) async-start(f32[8,128,128]{2,1,0:T(8,128)} %bitcast.14), calls=%async_computation.7 | async-start | bytes 1048576 | tf_op jit(solution)/shard_map/all_to_all | solution.py:191
  116.8 22.7 %all-to-all-start.8 = ((f32[32,32,128]{2,1,0:T(8,128)}), f32[32,32,128]{2,1,0:T(8,128)S(1)}, u32[]{:S(2)}, u32[]{:S(2)}) async-start(f32[32,32,128]{2,1,0:T(8,128)} %bitcast.15), calls=%async_computation.8 | async-start | bytes 1048576 | tf_op jit(solution)/shard_map/all_to_all | solution.py:191

commit v3 on v2

--- a/solution.py
+++ b/solution.py
@@ -64,36 +64,41 @@
     ]
 
 
-def start_body(x_ref, bt_ref, f4t_ref, f2_ref, out_ref, high_ref, low_ref, k4t_ref, held, sems):
+def split_body(x_ref, high_ref, low_ref, held, sems):
     def copy(i):
-        part = pl.ds(i * 2048, 2048)
+        part = pl.ds(i * 1024, 1024)
         return pltpu.make_async_copy(x_ref.at[part], held.at[part], sems.at[i])
 
-    for i in range(4):
+    for i in range(8):
         copy(i).start()
+    for i in range(8):
+        copy(i).wait()
+        rows = slice(i * 128, i * 128 + 128)
+        for b in range(8):
+            high, low = halves(held[pl.ds(i * 1024 + b, 128, stride=8), :])
+            high_ref[rows, b * 128 : b * 128 + 128] = high
+            low_ref[rows, b * 128 : b * 128 + 128] = low
+
+
+def first_mode(bt, high_ref, low_ref):
+    bt_high, bt_low = halves(bt)
+    major = mm16(jnp.concatenate([bt_high, bt_low], axis=0), high_ref[...])
+    return major[:64] + major[64:] + mm16(bt_high, low_ref[...])
+
+
+def start_body(high_ref, low_ref, bt_ref, f4t_ref, f2_ref, out_ref, k4t_ref):
     k4t = fourth_matrix(f4t_ref[...])
     k4t_ref[...] = k4t
     tail = jnp.concatenate([f2_ref[...], jnp.zeros((8, 96), F32)], axis=1)
     for i in range(8):
         out_ref[i * 40 + 32 : i * 40 + 40, :] = tail
-    bt_high, bt_low = halves(bt_ref[...])
-    both = jnp.concatenate([bt_high, bt_low], axis=0)
-    z = jnp.zeros((64, 1024), F32)
-    for i in range(4):
-        copy(i).wait()
-        rows = slice(i * 256, i * 256 + 256)
-        for b in range(8):
-            high, low = halves(held[pl.ds(i * 2048 + b, 256, stride=8), :])
-            high_ref[rows, b * 128 : b * 128 + 128] = high
-            low_ref[rows, b * 128 : b * 128 + 128] = low
-        major = mm16(both[:, rows], high_ref[rows, :])
-        z = z + major[:64] + major[64:] + mm16(bt_high[:, rows], low_ref[rows, :])
+    z = first_mode(bt_ref[...], high_ref, low_ref)
     for b, comb in enumerate(fourth_mode(z, k4t)):
         for c in range(4):
             out_ref[pl.ds(c * 8 + b, 8, stride=40), :] = comb[c * 8 : (c + 1) * 8]
 
 
-def second_body(r_ref, f3_ref, out_ref, f2_ref):
+def second_body(r_ref, f3_ref, out_ref, f2_ref, twice_ref):
     f2 = r_ref[:, 32:40, :].reshape(64, 128)[:, :32]
     f2_ref[...] = f2
     data = jnp.concatenate([r_ref[:, c * 8 : (c + 1) * 8, :].reshape(64, 128) for c in range(4)], axis=1)
@@ -102,6 +107,9 @@
     for c in range(4):
         out_ref[pl.ds(c, 32, stride=8), :] = y[:, c * 128 : (c + 1) * 128]
         out_ref[pl.ds(4 + c, 32, stride=8), :] = jnp.broadcast_to(f3[c : c + 1], (32, 128))
+    g = lax.broadcasted_iota(jnp.int32, (32, 64), 0)
+    slot = lax.broadcasted_iota(jnp.int32, (32, 64), 1)
+    twice_ref[...] = mm(f2, jnp.where(slot // 8 * 4 + slot % 4 == g, 1.0, 0.0).astype(F32))
 
 
 def third_body(r_ref, out_ref):
@@ -150,40 +158,39 @@
         out_ref[i] = total
 
 
-def core_two_body(image_ref, high_ref, low_ref, k4t_ref, f2_ref, out_ref, turned_ref):
+def core_two_body(image_ref, high_ref, low_ref, k4t_ref, out_ref, turned_ref):
     flat = image_ref[...].T
     bt = jnp.concatenate([flat[:64], flat[64:]], axis=1)
     turned_ref[...] = bt
-    bt_high, bt_low = halves(bt)
-    major = mm16(jnp.concatenate([bt_high, bt_low], axis=0), high_ref[...])
-    z = major[:64] + major[64:] + mm16(bt_high, low_ref[...])
-    combs = fourth_mode(z, k4t_ref[...])
-    for g in range(32):
-        total = f2_ref[0, g] * combs[0]
-        for b in range(1, 8):
-            total = total + f2_ref[b, g] * combs[b]
-        out_ref[g * 32 : (g + 1) * 32, :] = total
-
-
-def core_three_body(r_ref, f3_ref, out_ref):
-    total = r_ref[0]
-    for i in range(1, 8):
-        total = total + r_ref[i]
-    for f in range(32):
-        for g in range(4):
-            piece = f3_ref[0, f] * total[g * 32 : g * 32 + 8]
+    z = first_mode(bt, high_ref, low_ref)
+    for b, comb in enumerate(fourth_mode(z, k4t_ref[...])):
+        for c in range(4):
+            out_ref[pl.ds(c * 8 + b, 8, stride=32), :] = comb[c * 8 : (c + 1) * 8]
+
+
+def core_three_body(r_ref, twice_ref, f3_ref, out_ref):
+    data = jnp.concatenate([r_ref[:, c * 8 : (c + 1) * 8, :].reshape(64, 128) for c in range(4)], axis=1)
+    y = mm(twice_ref[...], data, 0, 0)
+    upper = lax.broadcasted_iota(jnp.int32, (8, 128), 0) < 4
+    for f in range(0, 32, 2):
+        scale = [jnp.where(upper, f3_ref[c, f], f3_ref[c, f + 1]) for c in range(4)]
+        for i in range(8):
+            piece = scale[0] * y[i * 8 : i * 8 + 8, :128]
             for c in range(1, 4):
-                piece = piece + f3_ref[c, f] * total[g * 32 + c * 8 : g * 32 + c * 8 + 8]
-            out_ref[(f * 4 + g) * 8 : (f * 4 + g + 1) * 8, :] = piece
-
-
-def core_body(r_ref, linv_ref, out_ref):
-    total = r_ref[0]
-    for i in range(1, 32):
-        total = total + r_ref[i]
+                piece = piece + scale[c] * y[i * 8 : i * 8 + 8, c * 128 : c * 128 + 128]
+            out_ref[(i * 32 + f) * 4 : (i * 32 + f) * 4 + 8, :] = piece
+
+
+def core_body(r_ref, linv_ref, out_ref, kept):
+    for i in range(8):
+        total = r_ref[i * 128 : i * 128 + 8, :]
+        for t in range(1, 16):
+            total = total + r_ref[i * 128 + t * 8 : i * 128 + t * 8 + 8, :]
+        kept[i * 8 : i * 8 + 8, :] = total + pltpu.roll(total, 4, 0)
     parts = []
     for g in range(4):
-        parts += [total[g * 8 : g * 8 + 8, :64], total[g * 8 : g * 8 + 8, 64:]]
+        tile = kept[pl.ds(g, 8, stride=8), :]
+        parts += [tile[:, :64], tile[:, 64:]]
     out_ref[...] = mm(jnp.concatenate(parts, axis=0), linv_ref[...], 1, 1)
 
 
@@ -193,17 +200,17 @@
 
 def shards(tensor, factor_two, factor_three, factor_four, factor_init):
     x = tensor.reshape(8192, 128)
-    block, high, low, k4t = call(
-        start_body,
-        [((320, 128), F32), ((1024, 1024), BF16), ((1024, 1024), BF16), ((64, 128), F32)],
-        (HBM, VMEM, VMEM, VMEM),
-        scratch=(pltpu.VMEM((8192, 128), F32), pltpu.SemaphoreType.DMA((4,))),
-        mib=48, flops=10**9,
-    )(x, factor_init.T, factor_four.T, factor_two)
+    high, low = call(
+        split_body, [((1024, 1024), BF16)] * 2, (HBM,),
+        scratch=(pltpu.VMEM((8192, 128), F32), pltpu.SemaphoreType.DMA((8,))), mib=48, flops=10**8,
+    )(x)
+    block, k4t = call(start_body, [((320, 128), F32), ((64, 128), F32)], (VMEM,) * 5, mib=12, flops=10**9)(
+        high, low, factor_init.T, factor_four.T, factor_two
+    )
     block = trade(block.reshape(8, 40, 128), ROW)
-    block, whole_two = call(second_body, [((256, 128), F32), ((64, 32), F32)], (VMEM, VMEM), flops=10**7)(
-        block, factor_three
-    )
+    block, whole_two, twice = call(
+        second_body, [((256, 128), F32), ((64, 32), F32), ((64, 64), F32)], (VMEM, VMEM), flops=10**7
+    )(block, factor_three)
     block = trade(block.reshape(32, 8, 128), COL)
     (block,) = call(third_body, [((128, 128), F32)], (VMEM,), flops=10**7)(block.reshape(256, 128))
     block = trade(block.reshape(32, 4, 128), COL)
@@ -218,16 +225,18 @@
     (image,) = call(sum_body, [((32, 16, 128), F32)], (VMEM,), flops=10**6)(image)
     image = trade(image, PLANE)
     block, turned = call(
-        core_two_body, [((1024, 128), F32), ((64, 1024), F32)], (VMEM,) * 4 + (SMEM,), mib=12, flops=10**9
-    )(image.reshape(512, 128), high, low, k4t, factor_two)
-    block = trade(block.reshape(8, 128, 128), ROW)
+        core_two_body, [((256, 128), F32), ((64, 1024), F32)], (VMEM,) * 4, mib=12, flops=10**9
+    )(image.reshape(512, 128), high, low, k4t)
+    block = trade(block.reshape(8, 32, 128), ROW)
     square = mm(turned, turned, 1, 1)
     lower = jnp.linalg.cholesky(square)
     linv = jax.scipy.linalg.solve_triangular(lower, jnp.eye(64, dtype=F32), lower=True)
     basis = mm(linv, turned)
-    (block,) = call(core_three_body, [((1024, 128), F32)], (VMEM, SMEM), flops=10**7)(block, factor_three)
-    block = trade(block.reshape(32, 32, 128), COL)
-    (core,) = call(core_body, [((64, 64), F32)], (VMEM, VMEM), flops=10**7)(block, linv)
+    (block,) = call(core_three_body, [((1024, 128), F32)], (VMEM, VMEM, SMEM), flops=10**7)(block, twice, factor_three)
+    block = trade(block.reshape(256, 4, 128), ROW + COL)
+    (core,) = call(core_body, [((64, 64), F32)], (VMEM, VMEM), scratch=(pltpu.VMEM((64, 128), F32),), flops=10**7)(
+        block.reshape(1024, 128), linv
+    )
     return basis.T, core.reshape(4, 1, 16, 64).transpose(3, 0, 1, 2)
 
 

time: 141 us -> 140 us (level); the launches traced: 140 us -> 137 us
  local copies, waits for them, and re-layouts: 2.4 us -> 0.09 us
  starting transfers between devices: 8.49 us -> 10.1 us
  waiting for transfers between devices: 14.1 us -> 12.6 us
    unnamed x8, local copies, waits for them, and re-layouts: 2.33 us -> 0.02 us
    all_to_all x2, starting transfers between devices: 8.49 us -> 10.1 us  [trade(): return lax.all_to_all(block, axis, split_axis=0, concat_axis=0, tiled=True)]
    all_to_all x2, waiting for transfers between devices: 14.1 us -> 12.6 us  [trade(): return lax.all_to_all(block, axis, split_axis=0, concat_axis=0, tiled=True)]
    pallas_call x5 -> x6, Pallas kernels: 9.25 us -> 8.48 us  [the longest x1 2.41 us: shards(): call(split_body, [((1024, 1024), BF16)] * 2, (HBM,), scratch=(pltpu.VMEM(...]
where the time goes in v3:
time: 140 us; the launch traced here: 137 us
  blocking collectives  88.8 us (63%)
  waiting for transfers between devices  12.6 us (9%)
  other arithmetic  12.1 us (9%)
  Pallas kernels  11.2 us (8%)
  starting transfers between devices  10.1 us (7%)
  matrix products  1.66 us (1%)
    all_to_all x7, blocking collectives, trade(): return lax.all_to_all(block, axis, split_axis=0, concat_axis=0, tiled=True)  88.8 us
    all_to_all x2, waiting for transfers between devices, trade(): return lax.all_to_all(block, axis, split_axis=0, concat_axis=0, tiled=True)  12.6 us
    all_to_all x2, starting transfers between devices, trade(): return lax.all_to_all(block, axis, split_axis=0, concat_axis=0, tiled=True)  10.1 us
    another operation x3, other arithmetic, shards(): lower = jnp.linalg.cholesky(square)  6.52 us
    another operation x2, other arithmetic, shards(): jax.scipy.linalg.solve_triangular(lower, jnp.eye(64, dtype=F32), lower=True)  5.55 us
  transfers between devices with their start and end apart: 2, of which 2 were waited for; matrix products, arithmetic and copies ran while one was open for 10% of the time, Pallas kernels for 0%

profile of v3, /device:TPU:32, one launch (start us, length us, event | category | flops | bytes accessed | tf_op | source)
XLA Modules:
  0.0 137.4 jit_solution(2655680146314610020)
XLA Ops:
  0.6 0.0 copy-start
  0.6 0.0 copy-start.1
  0.7 2.4 %shard_map.68 = (bf16[1024,1024]{1,0:T(8,128)(2,1)S(1)}, bf16[1024,1024]{1,0:T(8,128)(2,1)S(1)}) custom-call(f32[8192,128]{1,0:T(8,128)} %bitcast.43), custom_call_target="tpu_custom_call" | custom-call | flops 100000000 | bytes 1048576 | tf_op jit(solution)/shard_map/pallas_call | solution.py:203
  3.1 0.0 copy-start.2
  3.1 1.2 shard_map.69
  4.3 10.5 %all_to_all.45.r_ref = f32[8,40,128]{2,1,0:T(8,128)S(1)} all-to-all(f32[8,40,128]{2,1,0:T(8,128)S(1)} %bitcast.40), channel_id=1, replica_groups=mesh['x'=4,'k'=2,'y'=4,'z'=8] {'x','k'}, dimensions={0} | all-to-all | bytes 327680 | tf_op jit(solution)/shard_map/all_to_all | solution.py:198
  14.9 0.0 copy-done.2
  14.9 0.3 shard_map.70
  15.2 20.8 %all_to_all.46 = f32[32,8,128]{2,1,0:T(8,128)S(1)} all-to-all(f32[32,8,128]{2,1,0:T(8,128)S(1)} %bitcast.41), channel_id=1, replica_groups=mesh['x'=4,'k'=2,'y'=4,'z'=8] {'y','z'}, dimensions={0} | all-to-all | bytes 262144 | tf_op jit(solution)/shard_map/all_to_all | solution.py:198
  36.0 0.5 shard_map.71
  36.5 13.3 %all_to_all.47 = f32[32,4,128]{2,1,0:T(4,128)S(1)} all-to-all(f32[32,4,128]{2,1,0:T(4,128)S(1)} %bitcast.39), channel_id=1, replica_groups=mesh['x'=4,'k'=2,'y'=4,'z'=8] {'y','z'}, dimensions={0} | all-to-all | bytes 131072 | tf_op jit(solution)/shard_map/all_to_all | solution.py:198
  49.8 0.2 shard_map.72
  50.0 8.5 %all_to_all.48 = f32[8,32,128]{2,1,0:T(8,128)S(1)} all-to-all(f32[8,32,128]{2,1,0:T(8,128)S(1)} %shard_map.72), channel_id=1, replica_groups=mesh['x'=4,'k'=2,'y'=4,'z'=8] {'x','k'}, dimensions={0} | all-to-all | bytes 262144 | tf_op jit(solution)/shard_map/all_to_all | solution.py:198
  58.5 2.0 %shard_map.73 = f32[512,128]{1,0:T(8,128)S(1)} custom-call(f32[256,128]{1,0:T(8,128)S(1)} %bitcast.35, f32[64,128]{1,0:T(8,128)S(1)} %get-tuple-element.16.k4t_ref, bf16[1024,1024]{1,0:T(8,128)(2,1)S(1)} %get-tuple-element.11.high_ref, bf16[1024,1024]{1,0:T(8,128)(2,1)S(1)} %get-tuple-element.12.low_ref), custom_call_target="tpu_custom_call" | custom-call | flops 1000000000 | bytes 1048576 | tf_op jit(solution)/shard_map/pallas_call | solution.py:219
  60.5 12.5 %all_to_all.49.r_ref = f32[32,16,128]{2,1,0:T(8,128)S(1)} all-to-all(f32[32,16,128]{2,1,0:T(8,128)S(1)} %bitcast.34), channel_id=1, replica_groups=mesh['x'=4,'k'=2,'y'=4,'z'=8] {'x','k','y'}, dimensions={0} | all-to-all | bytes 524288 | tf_op jit(solution)/shard_map/all_to_all | solution.py:198
  73.0 10.5 %all_to_all.50.r_ref = f32[8,16,128]{2,1,0:T(8,128)S(1)} all-to-all(f32[8,16,128]{2,1,0:T(8,128)S(1)} %shard_map.74), channel_id=1, replica_groups=mesh['x'=4,'k'=2,'y'=4,'z'=8] {'z'}, dimensions={0} | all-to-all | bytes 131072 | tf_op jit(solution)/shard_map/all_to_all | solution.py:198
  83.5 12.7 %all_to_all.51 = f32[32,16,128]{2,1,0:T(8,128)S(1)} all-to-all(f32[32,16,128]{2,1,0:T(8,128)S(1)} %shard_map.75), channel_id=1, replica_groups=mesh['x'=4,'k'=2,'y'=4,'z'=8] {'x','k','y'}, dimensions={0} | all-to-all | bytes 524288 | tf_op jit(solution)/shard_map/all_to_all | solution.py:198
  96.2 1.9 %shard_map.76 = (f32[256,128]{1,0:T(8,128)}, f32[64,1024]{1,0:T(8,128)S(1)}) custom-call(f32[512,128]{1,0:T(8,128)S(1)} %bitcast.33, bf16[1024,1024]{1,0:T(8,128)(2,1)S(1)} %get-tuple-element.11.high_ref, bf16[1024,1024]{1,0:T(8,128)(2,1)S(1)} %get-tuple-element.12.low_ref, f32[64,128]{1,0:T(8,128)S(1)} %get-tuple-element.16.k4t_ref), custom_call_target="tpu_custom_call" | custom-call | flops 1000000000 | bytes 1048576 | tf_op jit(solution)/shard_map/pallas_call | solution.py:227
  98.1 3.4 %all-to-all-start.7 = ((f32[8,32,128]{2,1,0:T(8,128)}), f32[8,32,128]{2,1,0:T(8,128)S(1)}, u32[]{:S(2)}, u32[]{:S(2)}) async-start(f32[8,32,128]{2,1,0:T(8,128)} %bitcast.14), calls=%async_computation.7 | async-start | bytes 262144 | tf_op jit(solution)/shard_map/all_to_all | solution.py:198
  101.5 0.4 fusion.4
  101.9 0.1 copy.7
  102.0 5.6 %all-to-all-done.7.r_ref = f32[8,32,128]{2,1,0:T(8,128)S(1)} async-done(((f32[8,32,128]{2,1,0:T(8,128)}), f32[8,32,128]{2,1,0:T(8,128)S(1)}, u32[]{:S(2)}, u32[]{:S(2)}) %all-to-all-start.7) | async-done | bytes 131104 | tf_op jit(solution)/shard_map/all_to_all | solution.py:198
  107.5 1.8 %shard_map.77 = f32[1024,128]{1,0:T(8,128)} custom-call(f32[8,32,128]{2,1,0:T(8,128)S(1)} %all-to-all-done.7.r_ref, f32[64,64]{1,0:T(8,128)S(1)} %get-tuple-element.19.twice_ref, f32[4,32]{1,0:T(4,128)S(1)} %copy-done.2), custom_call_target="tpu_custom_call" | custom-call | flops 10000000 | bytes 1048576 | tf_op jit(solution)/shard_map/pallas_call | solution.py:235
  109.3 6.8 %all-to-all-start.8 = ((f32[256,4,128]{2,1,0:T(4,128)}), f32[256,4,128]{2,1,0:T(4,128)S(1)}, u32[]{:S(2)}, u32[]{:S(2)}) async-start(f32[256,4,128]{2,1,0:T(4,128)} %bitcast.15), calls=%async_computation.8 | async-start | bytes 1048576 | tf_op jit(solution)/shard_map/all_to_all | solution.py:198
  116.1 5.8 %cholesky.17 = f32[64,64]{1,0:T(8,128)S(1)} custom-call(f32[64,64]{1,0:T(8,128)S(1)} %fusion.3), custom_call_target="Cholesky" | custom-call | tf_op jit(solution)/shard_map/jit(cholesky)/cholesky | solution.py:232
  122.0 0.6 compare_reduce_fusion
  122.6 0.7 fusion
  123.3 4.9 %custom-call.7 = f32[1,64,64]{1,2,0:T(8,128)S(1)} custom-call(f32[1,64,64]{2,1,0:T(8,128)S(1)} %fusion), custom_call_target="InvertDiagBlocksLowerTriangular" | custom-call | tf_op jit(solution)/shard_map/jit(_solve_triangular)/triangular_solve | solution.py:233
  128.2 0.2 fusion.1.linv_ref
  128.4 1.1 fusion.5
  129.5 7.0 %all-to-all-done.8 = f32[256,4,128]{2,1,0:T(4,128)S(1)} async-done(((f32[256,4,128]{2,1,0:T(4,128)}), f32[256,4,128]{2,1,0:T(4,128)S(1)}, u32[]{:S(2)}, u32[]{:S(2)}) %all-to-all-start.8) | async-done | bytes 524320 | tf_op jit(solution)/shard_map/all_to_all | solution.py:198
  136.5 0.9 shard_map.78
  (8 shorter events, 0.1 us)
Async XLA Ops:
  0.6 2.4 %copy-start = (f32[1024,64]{0,1:T(8,128)S(1)}, f32[1024,64]{0,1:T(8,128)}, u32[]{:S(2)}) copy-start(f32[1024,64]{0,1:T(8,128)} %param.9) | copy-start | bytes 786436
  0.6 2.4 %copy-start.1 = (f32[32,16]{0,1:T(8,128)S(1)}, f32[32,16]{0,1:T(8,128)}, u32[]{:S(2)}) copy-start(f32[32,16]{0,1:T(8,128)} %param.8) | copy-start | bytes 6148
  0.7 2.4 %copy-start.3 = (f32[8,32]{1,0:T(8,128)S(1)}, f32[8,32]{1,0:T(8,128)}, u32[]{:S(2)}) copy-start(f32[8,32]{1,0:T(8,128)} %f2_ref.1) | copy-start | bytes 3076
  3.1 11.8 %copy-start.2 = (f32[4,32]{1,0:T(4,128)S(1)}, f32[4,32]{1,0:T(4,128)}, u32[]{:S(2)}) copy-start(f32[4,32]{1,0:T(4,128)} %f3_ref.3) | copy-start | bytes 1540
  98.1 9.4 %all-to-all-start.7 = ((f32[8,32,128]{2,1,0:T(8,128)}), f32[8,32,128]{2,1,0:T(8,128)S(1)}, u32[]{:S(2)}, u32[]{:S(2)}) async-start(f32[8,32,128]{2,1,0:T(8,128)} %bitcast.14), calls=%async_computation.7 | async-start | bytes 262144 | tf_op jit(solution)/shard_map/all_to_all | solution.py:198
  109.3 27.2 %all-to-all-start.8 = ((f32[256,4,128]{2,1,0:T(4,128)}), f32[256,4,128]{2,1,0:T(4,128)S(1)}, u32[]{:S(2)}, u32[]{:S(2)}) async-start(f32[256,4,128]{2,1,0:T(4,128)} %bitcast.15), calls=%async_computation.8 | async-start | bytes 1048576 | tf_op jit(solution)/shard_map/all_to_all | solution.py:198

commit v4 on v3

--- a/solution.py
+++ b/solution.py
@@ -86,9 +86,8 @@
     return major[:64] + major[64:] + mm16(bt_high, low_ref[...])
 
 
-def start_body(high_ref, low_ref, bt_ref, f4t_ref, f2_ref, out_ref, k4t_ref):
+def start_body(high_ref, low_ref, bt_ref, f4t_ref, f2_ref, out_ref):
     k4t = fourth_matrix(f4t_ref[...])
-    k4t_ref[...] = k4t
     tail = jnp.concatenate([f2_ref[...], jnp.zeros((8, 96), F32)], axis=1)
     for i in range(8):
         out_ref[i * 40 + 32 : i * 40 + 40, :] = tail
@@ -98,18 +97,45 @@
             out_ref[pl.ds(c * 8 + b, 8, stride=40), :] = comb[c * 8 : (c + 1) * 8]
 
 
-def second_body(r_ref, f3_ref, out_ref, f2_ref, twice_ref):
+def pack_body(high_ref, low_ref, f4t_ref, me_ref, *refs):
+    outs, (mat_high, mat_low) = refs[:8], refs[8:]
+    lane = lax.broadcasted_iota(jnp.int32, (16, 512), 1)
+    index = lax.broadcasted_iota(jnp.int32, (16, 512), 0)
+    owner = lane // 8 % 2 * 8 + (me_ref[0] + lane // 64) % 8
+    wide = mm(f4t_ref[...], jnp.where(index == owner, 1.0, 0.0).astype(F32), 0, 0)
+    lane = lax.broadcasted_iota(jnp.int32, (32, 512), 1)
+    spot = lane % 8 * 4 + lane // 16 % 4
+    wide_high, wide_low = halves(wide)
+    for n in range(32):
+        mat_high[n * 32 : n * 32 + 32, :] = jnp.where(spot == n, wide_high.astype(F32), 0.0).astype(BF16)
+        mat_low[n * 32 : n * 32 + 32, :] = jnp.where(spot == n, wide_low.astype(F32), 0.0).astype(BF16)
+    for t in range(4):
+        parts = []
+        for start in (t * 128, 512 + t * 128):
+            rows = slice(start, start + 128)
+            parts.append(
+                mm16(high_ref[rows, :], mat_high[...])
+                + mm16(high_ref[rows, :], mat_low[...])
+                + mm16(low_ref[rows, :], mat_high[...])
+            )
+        for n, out in enumerate(outs):
+            lanes = slice(n * 64, n * 64 + 64)
+            out[t * 128 : t * 128 + 128, :] = jnp.concatenate([p[:, lanes] for p in parts], axis=1)
+
+
+def second_body(r_ref, f3_ref, me_ref, out_ref, f2_ref, twice_ref):
     f2 = r_ref[:, 32:40, :].reshape(64, 128)[:, :32]
-    f2_ref[...] = f2
     data = jnp.concatenate([r_ref[:, c * 8 : (c + 1) * 8, :].reshape(64, 128) for c in range(4)], axis=1)
     y = mm(f2, data, 0, 0)
     f3 = jnp.concatenate([f3_ref[...], jnp.zeros((4, 96), F32)], axis=1)
     for c in range(4):
         out_ref[pl.ds(c, 32, stride=8), :] = y[:, c * 128 : (c + 1) * 128]
         out_ref[pl.ds(4 + c, 32, stride=8), :] = jnp.broadcast_to(f3[c : c + 1], (32, 128))
+    turned = jnp.concatenate([r_ref[(me_ref[0] - t + 8) % 8, 32:40, :] for t in range(8)], axis=0)[:, :32]
+    f2_ref[...] = turned
     g = lax.broadcasted_iota(jnp.int32, (32, 64), 0)
     slot = lax.broadcasted_iota(jnp.int32, (32, 64), 1)
-    twice_ref[...] = mm(f2, jnp.where(slot // 8 * 4 + slot % 4 == g, 1.0, 0.0).astype(F32))
+    twice_ref[...] = mm(turned, jnp.where(slot // 8 * 4 + slot % 4 == g, 1.0, 0.0).astype(F32))
 
 
 def third_body(r_ref, out_ref):
@@ -120,34 +146,20 @@
         out_ref[pl.ds(c, 32, stride=4), :] = q[c * 32 : (c + 1) * 32]
 
 
-def back_body(r_ref, f2_ref, out_ref):
+def image_body(r_ref, f2_ref, *refs):
+    blocks, (out_ref, high_ref, low_ref) = refs[:8], refs[8:]
+    for t, block in enumerate(blocks):
+        lanes = slice(t * 128, t * 128 + 128)
+        high_ref[:, lanes], low_ref[:, lanes] = halves(block[...])
     data = jnp.concatenate([r_ref[pl.ds(c, 32, stride=4), :] for c in range(4)], axis=1)
     y = mm(f2_ref[...], data)
-    for c in range(4):
-        out_ref[:, c * 8 : (c + 1) * 8, :] = y[:, c * 128 : (c + 1) * 128].reshape(8, 8, 128)
-
-
-def image_body(r_ref, k4t_ref, high_ref, low_ref, out_ref):
-    ws = []
-    for b in range(8):
-        w4 = jnp.concatenate([r_ref[pl.ds(c * 8 + b, 8, stride=32), :] for c in range(4)], axis=0)
-        ws.append(jnp.concatenate([w4[:, :64], w4[:, 64:]], axis=0))
-    w = mm(k4t_ref[...], jnp.concatenate(ws, axis=1), 0, 0)
-    w = jnp.concatenate([w[:, b * 64 : b * 64 + 64] for b in range(8)], axis=0)
-    w_high, w_low = halves(w)
-    none = jnp.zeros((1024, 64), BF16)
-    first = jnp.concatenate([w_high, w_low], axis=1)
-    second = jnp.concatenate([w_low, w_high], axis=1)
-    left = jnp.concatenate([w_high, none], axis=1)
-    right = jnp.concatenate([none, w_high], axis=1)
-    half = lax.broadcasted_iota(jnp.int32, (128, 128), 1) < 64
-    for i in range(4):
-        top = slice(i * 128, i * 128 + 128)
-        low = slice(512 + i * 128, 512 + i * 128 + 128)
-        t = mm16(high_ref[top, :], first)
-        u = mm16(high_ref[low, :], second)
-        rest = mm16(low_ref[top, :], left) + mm16(low_ref[low, :], right)
-        out_ref[top, :] = jnp.where(half, t, u) + pltpu.roll(jnp.where(half, u, t), 64, 1) + rest
+    zero = jnp.zeros((64, 64), F32)
+    rows = []
+    for t in range(8):
+        w = jnp.concatenate([y[t * 8 : t * 8 + 8, n * 64 : n * 64 + 64] for n in range(8)], axis=0)
+        rows += [jnp.concatenate([w, zero], axis=1), jnp.concatenate([zero, w], axis=1)]
+    w_high, w_low = halves(jnp.concatenate(rows, axis=0))
+    out_ref[...] = mm16(high_ref[...], w_high) + mm16(high_ref[...], w_low) + mm16(low_ref[...], w_high)
 
 
 def sum_body(r_ref, out_ref):
@@ -158,19 +170,19 @@
         out_ref[i] = total
 
 
-def core_two_body(image_ref, high_ref, low_ref, k4t_ref, out_ref, turned_ref):
+def core_two_body(image_ref, high_ref, low_ref, twice_ref, f3_ref, out_ref, turned_ref):
     flat = image_ref[...].T
-    bt = jnp.concatenate([flat[:64], flat[64:]], axis=1)
-    turned_ref[...] = bt
-    z = first_mode(bt, high_ref, low_ref)
-    for b, comb in enumerate(fourth_mode(z, k4t_ref[...])):
-        for c in range(4):
-            out_ref[pl.ds(c * 8 + b, 8, stride=32), :] = comb[c * 8 : (c + 1) * 8]
-
-
-def core_three_body(r_ref, twice_ref, f3_ref, out_ref):
-    data = jnp.concatenate([r_ref[:, c * 8 : (c + 1) * 8, :].reshape(64, 128) for c in range(4)], axis=1)
-    y = mm(twice_ref[...], data, 0, 0)
+    turned_ref[...] = jnp.concatenate([flat[:64], flat[64:]], axis=1)
+    bt_high, bt_low = halves(flat)
+    z = mm16(jnp.concatenate([bt_high, bt_low], axis=0), high_ref[...])
+    z = z[:128] + z[128:] + mm16(bt_high, low_ref[...])
+    z = jnp.concatenate(
+        [z[:64, t * 128 : t * 128 + 64] + z[64:, t * 128 + 64 : t * 128 + 128] for t in range(8)], axis=1
+    ).T
+    pieces = [
+        jnp.concatenate([z[t * 64 + n * 8 : t * 64 + n * 8 + 8] for t in range(8)], axis=0) for n in range(8)
+    ]
+    y = mm(twice_ref[...], jnp.concatenate(pieces, axis=1), 0, 0)
     upper = lax.broadcasted_iota(jnp.int32, (8, 128), 0) < 4
     for f in range(0, 32, 2):
         scale = [jnp.where(upper, f3_ref[c, f], f3_ref[c, f + 1]) for c in range(4)]
@@ -204,35 +216,39 @@
         split_body, [((1024, 1024), BF16)] * 2, (HBM,),
         scratch=(pltpu.VMEM((8192, 128), F32), pltpu.SemaphoreType.DMA((8,))), mib=48, flops=10**8,
     )(x)
-    block, k4t = call(start_body, [((320, 128), F32), ((64, 128), F32)], (VMEM,) * 5, mib=12, flops=10**9)(
+    me = lax.axis_index(ROW).astype(jnp.int32).reshape(1)
+    (block,) = call(start_body, [((320, 128), F32)], (VMEM,) * 5, mib=12, flops=10**9)(
         high, low, factor_init.T, factor_four.T, factor_two
     )
+    blocks = call(
+        pack_body, [((512, 128), F32)] * 8, (VMEM,) * 3 + (SMEM,),
+        scratch=(pltpu.VMEM((1024, 512), BF16),) * 2, mib=16, flops=3 * 10**9,
+    )(high, low, factor_four.T, me)
     block = trade(block.reshape(8, 40, 128), ROW)
-    block, whole_two, twice = call(
-        second_body, [((256, 128), F32), ((64, 32), F32), ((64, 64), F32)], (VMEM, VMEM), flops=10**7
-    )(block, factor_three)
+    block, f2, twice = call(
+        second_body, [((256, 128), F32), ((64, 32), F32), ((64, 64), F32)], (VMEM, VMEM, SMEM), flops=10**7
+    )(block, factor_three, me)
+    blocks = [blocks[0]] + [
+        lax.ppermute(blocks[t], ROW, [(i, (i + t) % 8) for i in range(8)]) for t in range(1, 8)
+    ]
     block = trade(block.reshape(32, 8, 128), COL)
     (block,) = call(third_body, [((128, 128), F32)], (VMEM,), flops=10**7)(block.reshape(256, 128))
     block = trade(block.reshape(32, 4, 128), COL)
-    (block,) = call(back_body, [((8, 32, 128), F32)], (VMEM, VMEM), flops=10**7)(block.reshape(128, 128), whole_two)
-    block = trade(block, ROW)
-    (image,) = call(image_body, [((512, 128), F32)], (VMEM,) * 4, mib=12, flops=10**9)(
-        block.reshape(256, 128), k4t, high, low
-    )
+    image, high, low = call(
+        image_body, [((512, 128), F32), ((512, 1024), BF16), ((512, 1024), BF16)], (VMEM,) * 10, mib=12, flops=10**9
+    )(block.reshape(128, 128), f2, *blocks)
     image = trade(image.reshape(32, 16, 128), PLANE)
     (image,) = call(sum_body, [((8, 16, 128), F32)], (VMEM,), flops=10**6)(image)
     image = trade(image, "z")
     (image,) = call(sum_body, [((32, 16, 128), F32)], (VMEM,), flops=10**6)(image)
     image = trade(image, PLANE)
     block, turned = call(
-        core_two_body, [((256, 128), F32), ((64, 1024), F32)], (VMEM,) * 4, mib=12, flops=10**9
-    )(image.reshape(512, 128), high, low, k4t)
-    block = trade(block.reshape(8, 32, 128), ROW)
+        core_two_body, [((1024, 128), F32), ((64, 1024), F32)], (VMEM,) * 4 + (SMEM,), mib=12, flops=10**9
+    )(image.reshape(512, 128), high, low, twice, factor_three)
     square = mm(turned, turned, 1, 1)
     lower = jnp.linalg.cholesky(square)
     linv = jax.scipy.linalg.solve_triangular(lower, jnp.eye(64, dtype=F32), lower=True)
     basis = mm(linv, turned)
-    (block,) = call(core_three_body, [((1024, 128), F32)], (VMEM, VMEM, SMEM), flops=10**7)(block, twice, factor_three)
     block = trade(block.reshape(256, 4, 128), ROW + COL)
     (core,) = call(core_body, [((64, 64), F32)], (VMEM, VMEM), scratch=(pltpu.VMEM((64, 128), F32),), flops=10**7)(
         block.reshape(1024, 128), linv

time: 140 us -> 136 us (0.971)
  the two profiles are of different devices: /device:TPU:32 before, /device:TPU:1 now
where the time goes in v4:
time: 136 us
  blocking collectives  42.6 us (31%)
  starting transfers between devices  38.5 us (28%)
  waiting for transfers between devices  20.1 us (15%)
  Pallas kernels  15.9 us (12%)
  other arithmetic  12.1 us (9%)
  local copies, waits for them, and re-layouts  4.03 us (3%)
  matrix products  1.66 us (1%)
    all_to_all x3, blocking collectives, trade(): return lax.all_to_all(block, axis, split_axis=0, concat_axis=0, tiled=True)  42.6 us
    all_to_all x4, starting transfers between devices, trade(): return lax.all_to_all(block, axis, split_axis=0, concat_axis=0, tiled=True)  28.9 us
    all_to_all x4, waiting for transfers between devices, trade(): return lax.all_to_all(block, axis, split_axis=0, concat_axis=0, tiled=True)  12.1 us
    ppermute x7, starting transfers between devices, shards(): lax.ppermute(blocks[t], ROW, [(i, (i + t) % 8) for i in range(8)])  9.63 us
    ppermute x7, waiting for transfers between devices, shards(): lax.ppermute(blocks[t], ROW, [(i, (i + t) % 8) for i in range(8)])  7.99 us
    another operation x3, other arithmetic, shards(): lower = jnp.linalg.cholesky(square)  6.52 us
    another operation x2, other arithmetic, shards(): jax.scipy.linalg.solve_triangular(lower, jnp.eye(64, dtype=F32), lower=True)  5.55 us
    pallas_call x1, Pallas kernels, shards(): call(pack_body, [((512, 128), F32)] * 8, (VMEM,) * 3 + (SMEM,), scratch=(...  4.49 us
  transfers between devices with their start and end apart: 11, of which 6 were waited for; matrix products, arithmetic and copies ran while one was open for 10% of the time, Pallas kernels for 5%

profile of v4, /device:TPU:1, one launch (start us, length us, event | category | flops | bytes accessed | tf_op | source)
XLA Modules:
  0.0 135.7 jit_solution(17957037193061847043)
XLA Ops:
  0.7 2.4 %shard_map.68 = (bf16[1024,1024]{1,0:T(8,128)(2,1)S(1)}, bf16[1024,1024]{1,0:T(8,128)(2,1)S(1)}) custom-call(f32[8192,128]{1,0:T(8,128)} %bitcast.39), custom_call_target="tpu_custom_call" | custom-call | flops 100000000 | bytes 1048576 | tf_op jit(solution)/shard_map/pallas_call | solution.py:215
  3.1 1.9 %shard_map.69 = f32[320,128]{1,0:T(8,128)} custom-call(bf16[1024,1024]{1,0:T(8,128)(2,1)S(1)} %get-tuple-element.20.high_ref, bf16[1024,1024]{1,0:T(8,128)(2,1)S(1)} %get-tuple-element.21.low_ref, f32[64,1024]{1,0:T(8,128)S(1)} %bitcast.35, f32[16,32]{1,0:T(8,128)S(1)} %bitcast.37, f32[8,32]{1,0:T(8,128)S(1)} %copy-done.4), custom_call_target="tpu_custom_call" | custom-call | flops 1000000000 | bytes 1048576 | tf_op jit(solution)/shard_map/pallas_call | solution.py:220
  5.0 6.5 %all-to-all-start = ((f32[8,40,128]{2,1,0:T(8,128)}), f32[8,40,128]{2,1,0:T(8,128)S(1)}, u32[]{:S(2)}, u32[]{:S(2)}) async-start(f32[8,40,128]{2,1,0:T(8,128)} %bitcast.3), calls=%async_computation | async-start | bytes 327680 | tf_op jit(solution)/shard_map/all_to_all | solution.py:210
  11.5 1.6 %copy-done.1 = bf16[1024,1024]{1,0:T(8,128)(2,1)S(1)} copy-done((bf16[1024,1024]{1,0:T(8,128)(2,1)S(1)}, bf16[1024,1024]{1,0:T(8,128)(2,1)}, u32[]{:S(2)}) %copy-start.1) | copy-done | bytes 2097176
  13.1 4.5 %shard_map.72 = (f32[512,128]{1,0:T(8,128)S(1)}, f32[512,128]{1,0:T(8,128)}, f32[512,128]{1,0:T(8,128)}, f32[512,128]{1,0:T(8,128)S(1)}, f32[512,128]{1,0:T(8,12...) custom-call(bf16[1024,1024]{1,0:T(8,128)(2,1)S(1)} %get-tuple-element.20.high_ref, ...), custom_call_target="tpu_custom_call" | custom-call | flops 3000000000 | bytes 1048576 | tf_op jit(solution)/shard_map/pallas_call | solution.py:223
  18.9 1.6 %collective-permute-start = (f32[512,128]{1,0:T(8,128)}, f32[512,128]{1,0:T(8,128)S(1)}, u32[]{:S(2)}, u32[]{:S(2)}) collective-permute-start(f32[512,128]{1,0:T(8,128)} %get-tuple-element.25), channel_id=1, source_target_pairs={{0,32},{32,64},{64,96},{96,128},{128,160},{160,192},{192,224},{224... | collective-permute-start | bytes 786440 | tf_op jit(solution)/shard_map/ppermute | solution.py:232
  20.6 1.2 collective-permute-start.1
  21.8 0.9 shard_map.70
  22.7 10.5 %all-to-all-start.1 = ((f32[32,8,128]{2,1,0:T(8,128)}), f32[32,8,128]{2,1,0:T(8,128)S(1)}, u32[]{:S(2)}, u32[]{:S(2)}) async-start(f32[32,8,128]{2,1,0:T(8,128)} %bitcast.5), calls=%async_computation.1 | async-start | bytes 262144 | tf_op jit(solution)/shard_map/all_to_all | solution.py:210
  33.2 2.0 %collective-permute-start.2 = (f32[512,128]{1,0:T(8,128)}, f32[512,128]{1,0:T(8,128)S(1)}, u32[]{:S(2)}, u32[]{:S(2)}) collective-permute-start(f32[512,128]{1,0:T(8,128)} %copy-done.6), channel_id=1, source_target_pairs={{0,96},{32,128},{64,160},{96,192},{128,224},{160,0},{192,32},{224,... | collective-permute-start | bytes 786440 | tf_op jit(solution)/shard_map/ppermute | solution.py:232
  35.8 1.4 %collective-permute-start.4 = (f32[512,128]{1,0:T(8,128)S(1)}, f32[512,128]{1,0:T(8,128)S(1)}, u32[]{:S(2)}, u32[]{:S(2)}) collective-permute-start(f32[512,128]{1,0:T(8,128)S(1)} %get-tuple-element.29), channel_id=1, source_target_pairs={{0,160},{32,192},{64,224},{96,0},{128,32},{160,64},{192,96},{224,1... | collective-permute-start | bytes 786440 | tf_op jit(solution)/shard_map/ppermute | solution.py:232
  37.2 0.9 collective-permute-start.5
  38.0 2.0 %collective-permute-start.6 = (f32[512,128]{1,0:T(8,128)S(1)}, f32[512,128]{1,0:T(8,128)S(1)}, u32[]{:S(2)}, u32[]{:S(2)}) collective-permute-start(f32[512,128]{1,0:T(8,128)S(1)} %get-tuple-element.31), channel_id=1, source_target_pairs={{0,224},{32,0},{64,32},{96,64},{128,96},{160,128},{192,160},{224,1... | collective-permute-start | bytes 786440 | tf_op jit(solution)/shard_map/ppermute | solution.py:232
  40.0 3.2 %all-to-all-done.1 = f32[32,8,128]{2,1,0:T(8,128)S(1)} async-done(((f32[32,8,128]{2,1,0:T(8,128)}), f32[32,8,128]{2,1,0:T(8,128)S(1)}, u32[]{:S(2)}, u32[]{:S(2)}) %all-to-all-start.1) | async-done | bytes 131104 | tf_op jit(solution)/shard_map/all_to_all | solution.py:210
  43.2 1.1 shard_map.71
  44.3 6.3 %all-to-all-start.2 = ((f32[32,4,128]{2,1,0:T(4,128)}), f32[32,4,128]{2,1,0:T(4,128)S(1)}, u32[]{:S(2)}, u32[]{:S(2)}) async-start(f32[32,4,128]{2,1,0:T(4,128)} %bitcast.7), calls=%async_computation.2 | async-start | bytes 131072 | tf_op jit(solution)/shard_map/all_to_all | solution.py:210
  50.7 1.2 collective-permute-done.4.refs_5_
  51.9 5.6 %collective-permute-done.5.refs_6_ = f32[512,128]{1,0:T(8,128)S(1)} collective-permute-done((f32[512,128]{1,0:T(8,128)S(1)}, f32[512,128]{1,0:T(8,128)S(1)}, u32[]{:S(2)}, u32[]{:S(2)}) %collective-permute-start.5) | collective-permute-done | bytes 262176 | tf_op jit(solution)/shard_map/ppermute | solution.py:232
  57.5 1.2 collective-permute-done.6.refs_7_
  58.7 0.9 all-to-all-done.2
  59.5 0.9 copy-done.8
  60.5 1.4 %shard_map.73 = (f32[512,128]{1,0:T(8,128)S(1)}, bf16[512,1024]{1,0:T(8,128)(2,1)S(1)}, bf16[512,1024]{1,0:T(8,128)(2,1)S(1)}) custom-call(f32[128,128]{1,0:T(8,128)S(1)} %bitcast.36, f32[64,32]{1,0:T(8,128)S(1)} %get-tuple-element.23.f2_ref, f32[512,128]{1,0:T(8,128)S(1)} %copy-done.8, f32[512,128]{1,0:T(8,128)S(1)} %collective-permute-done.refs_1_, ...), custom_call_target="tpu_custom_call" | custom-call | flops 1000000000 | bytes 1048576 | tf_op jit(solution)/shard_map/pallas_call | solution.py:237
  61.9 15.0 %all_to_all.35.r_ref = f32[32,16,128]{2,1,0:T(8,128)S(1)} all-to-all(f32[32,16,128]{2,1,0:T(8,128)S(1)} %bitcast.33), channel_id=1, replica_groups=mesh['x'=4,'k'=2,'y'=4,'z'=8] {'x','k','y'}, dimensions={0} | all-to-all | bytes 524288 | tf_op jit(solution)/shard_map/all_to_all | solution.py:210
  77.0 13.5 %all_to_all.36.r_ref = f32[8,16,128]{2,1,0:T(8,128)S(1)} all-to-all(f32[8,16,128]{2,1,0:T(8,128)S(1)} %shard_map.74), channel_id=1, replica_groups=mesh['x'=4,'k'=2,'y'=4,'z'=8] {'z'}, dimensions={0} | all-to-all | bytes 131072 | tf_op jit(solution)/shard_map/all_to_all | solution.py:210
  90.5 14.1 %all_to_all.37 = f32[32,16,128]{2,1,0:T(8,128)S(1)} all-to-all(f32[32,16,128]{2,1,0:T(8,128)S(1)} %shard_map.75), channel_id=1, replica_groups=mesh['x'=4,'k'=2,'y'=4,'z'=8] {'x','k','y'}, dimensions={0} | all-to-all | bytes 524288 | tf_op jit(solution)/shard_map/all_to_all | solution.py:210
  104.5 2.8 %shard_map.76 = (f32[1024,128]{1,0:T(8,128)}, f32[64,1024]{1,0:T(8,128)S(1)}) custom-call(f32[512,128]{1,0:T(8,128)S(1)} %bitcast.34, bf16[512,1024]{1,0:T(8,128)(2,1)S(1)} %get-tuple-element.33.high_ref, bf16[512,1024]{1,0:T(8,128)(2,1)S(1)} %get-tuple-element.34.low_ref, f32[64,64]{1,0:T(8,128)S(1)} %get-tuple-element.35.twice_ref, f32[4,32]{1,0:T(4,128)S(1)} %copy-done.5), custom_call_target="tpu_custom_call" | custom-call | flops 1000000000 | bytes 1048576 | tf_op jit(solution)/shard_map/pallas_call | solution.py:245
  107.7 5.6 %all-to-all-start.6 = ((f32[256,4,128]{2,1,0:T(4,128)}), f32[256,4,128]{2,1,0:T(4,128)S(1)}, u32[]{:S(2)}, u32[]{:S(2)}) async-start(f32[256,4,128]{2,1,0:T(4,128)} %bitcast.14), calls=%async_computation.6 | async-start | bytes 1048576 | tf_op jit(solution)/shard_map/all_to_all | solution.py:210
  113.4 5.8 %cholesky.17 = f32[64,64]{1,0:T(8,128)S(1)} custom-call(f32[64,64]{1,0:T(8,128)S(1)} %fusion.3), custom_call_target="Cholesky" | custom-call | tf_op jit(solution)/shard_map/jit(cholesky)/cholesky | solution.py:249
  120.6 4.9 %custom-call.7 = f32[1,64,64]{1,2,0:T(8,128)S(1)} custom-call(f32[1,64,64]{2,1,0:T(8,128)S(1)} %fusion), custom_call_target="InvertDiagBlocksLowerTriangular" | custom-call | tf_op jit(solution)/shard_map/jit(_solve_triangular)/triangular_solve | solution.py:250
  125.7 1.1 fusion.5
  126.8 8.1 %all-to-all-done.6 = f32[256,4,128]{2,1,0:T(4,128)S(1)} async-done(((f32[256,4,128]{2,1,0:T(4,128)}), f32[256,4,128]{2,1,0:T(4,128)S(1)}, u32[]{:S(2)}, u32[]{:S(2)}) %all-to-all-start.6) | async-done | bytes 524320 | tf_op jit(solution)/shard_map/all_to_all | solution.py:210
  134.8 0.9 shard_map.77
  (31 shorter events, 4.1 us)
Async XLA Ops:
  0.6 2.5 %copy-start.2 = (f32[1024,64]{0,1:T(8,128)S(1)}, f32[1024,64]{0,1:T(8,128)}, u32[]{:S(2)}) copy-start(f32[1024,64]{0,1:T(8,128)} %param.9) | copy-start | bytes 786436
  0.6 2.5 %copy-start.3 = (f32[32,16]{0,1:T(8,128)S(1)}, f32[32,16]{0,1:T(8,128)}, u32[]{:S(2)}) copy-start(f32[32,16]{0,1:T(8,128)} %param.8) | copy-start | bytes 6148
  0.7 2.5 %copy-start.4 = (f32[8,32]{1,0:T(8,128)S(1)}, f32[8,32]{1,0:T(8,128)}, u32[]{:S(2)}) copy-start(f32[8,32]{1,0:T(8,128)} %f2_ref.1) | copy-start | bytes 3076
  3.1 1.9 %copy-start = (bf16[1024,1024]{1,0:T(8,128)(2,1)}, bf16[1024,1024]{1,0:T(8,128)(2,1)S(1)}, u32[]{:S(2)}) copy-start(bf16[1024,1024]{1,0:T(8,128)(2,1)S(1)} %get-tuple-element.21.low_ref) | copy-start | bytes 6291460
  5.0 16.8 %all-to-all-start = ((f32[8,40,128]{2,1,0:T(8,128)}), f32[8,40,128]{2,1,0:T(8,128)S(1)}, u32[]{:S(2)}, u32[]{:S(2)}) async-start(f32[8,40,128]{2,1,0:T(8,128)} %bitcast.3), calls=%async_computation | async-start | bytes 327680 | tf_op jit(solution)/shard_map/all_to_all | solution.py:210
  11.5 1.6 %copy-start.1 = (bf16[1024,1024]{1,0:T(8,128)(2,1)S(1)}, bf16[1024,1024]{1,0:T(8,128)(2,1)}, u32[]{:S(2)}) copy-start(bf16[1024,1024]{1,0:T(8,128)(2,1)} %copy-done) | copy-start | bytes 6291460
  13.1 8.7 %copy-start.5 = (f32[4,32]{1,0:T(4,128)S(1)}, f32[4,32]{1,0:T(4,128)}, u32[]{:S(2)}) copy-start(f32[4,32]{1,0:T(4,128)} %f3_ref.3) | copy-start | bytes 1540
  17.6 0.7 copy-start.6
  18.2 0.7 copy-start.7
  18.9 18.2 %collective-permute-start = (f32[512,128]{1,0:T(8,128)}, f32[512,128]{1,0:T(8,128)S(1)}, u32[]{:S(2)}, u32[]{:S(2)}) collective-permute-start(f32[512,128]{1,0:T(8,128)} %get-tuple-element.25), channel_id=1, source_target_pairs={{0,32},{32,64},{64,96},{96,128},{128,160},{160,192},{192,224},{224... | collective-permute-start | bytes 786440 | tf_op jit(solution)/shard_map/ppermute | solution.py:232
  20.6 17.4 %collective-permute-start.1 = (f32[512,128]{1,0:T(8,128)}, f32[512,128]{1,0:T(8,128)S(1)}, u32[]{:S(2)}, u32[]{:S(2)}) collective-permute-start(f32[512,128]{1,0:T(8,128)} %get-tuple-element.26), channel_id=1, source_target_pairs={{0,64},{32,96},{64,128},{96,160},{128,192},{160,224},{192,0},{224,... | collective-permute-start | bytes 786440 | tf_op jit(solution)/shard_map/ppermute | solution.py:232
  22.7 20.5 %all-to-all-start.1 = ((f32[32,8,128]{2,1,0:T(8,128)}), f32[32,8,128]{2,1,0:T(8,128)S(1)}, u32[]{:S(2)}, u32[]{:S(2)}) async-start(f32[32,8,128]{2,1,0:T(8,128)} %bitcast.5), calls=%async_computation.1 | async-start | bytes 262144 | tf_op jit(solution)/shard_map/all_to_all | solution.py:210
  33.2 17.4 %collective-permute-start.2 = (f32[512,128]{1,0:T(8,128)}, f32[512,128]{1,0:T(8,128)S(1)}, u32[]{:S(2)}, u32[]{:S(2)}) collective-permute-start(f32[512,128]{1,0:T(8,128)} %copy-done.6), channel_id=1, source_target_pairs={{0,96},{32,128},{64,160},{96,192},{128,224},{160,0},{192,32},{224,... | collective-permute-start | bytes 786440 | tf_op jit(solution)/shard_map/ppermute | solution.py:232
  35.2 15.5 %collective-permute-start.3 = (f32[512,128]{1,0:T(8,128)S(1)}, f32[512,128]{1,0:T(8,128)S(1)}, u32[]{:S(2)}, u32[]{:S(2)}) collective-permute-start(f32[512,128]{1,0:T(8,128)S(1)} %get-tuple-element.28), channel_id=1, source_target_pairs={{0,128},{32,160},{64,192},{96,224},{128,0},{160,32},{192,64},{224,... | collective-permute-start | bytes 786440 | tf_op jit(solution)/shard_map/ppermute | solution.py:232
  35.8 16.1 %collective-permute-start.4 = (f32[512,128]{1,0:T(8,128)S(1)}, f32[512,128]{1,0:T(8,128)S(1)}, u32[]{:S(2)}, u32[]{:S(2)}) collective-permute-start(f32[512,128]{1,0:T(8,128)S(1)} %get-tuple-element.29), channel_id=1, source_target_pairs={{0,160},{32,192},{64,224},{96,0},{128,32},{160,64},{192,96},{224,1... | collective-permute-start | bytes 786440 | tf_op jit(solution)/shard_map/ppermute | solution.py:232
  37.2 20.3 %collective-permute-start.5 = (f32[512,128]{1,0:T(8,128)S(1)}, f32[512,128]{1,0:T(8,128)S(1)}, u32[]{:S(2)}, u32[]{:S(2)}) collective-permute-start(f32[512,128]{1,0:T(8,128)S(1)} %get-tuple-element.30), channel_id=1, source_target_pairs={{0,192},{32,224},{64,0},{96,32},{128,64},{160,96},{192,128},{224,1... | collective-permute-start | bytes 786440 | tf_op jit(solution)/shard_map/ppermute | solution.py:232
  38.0 20.7 %collective-permute-start.6 = (f32[512,128]{1,0:T(8,128)S(1)}, f32[512,128]{1,0:T(8,128)S(1)}, u32[]{:S(2)}, u32[]{:S(2)}) collective-permute-start(f32[512,128]{1,0:T(8,128)S(1)} %get-tuple-element.31), channel_id=1, source_target_pairs={{0,224},{32,0},{64,32},{96,64},{128,96},{160,128},{192,160},{224,1... | collective-permute-start | bytes 786440 | tf_op jit(solution)/shard_map/ppermute | solution.py:232
  44.3 15.2 %all-to-all-start.2 = ((f32[32,4,128]{2,1,0:T(4,128)}), f32[32,4,128]{2,1,0:T(4,128)S(1)}, u32[]{:S(2)}, u32[]{:S(2)}) async-start(f32[32,4,128]{2,1,0:T(4,128)} %bitcast.7), calls=%async_computation.2 | async-start | bytes 131072 | tf_op jit(solution)/shard_map/all_to_all | solution.py:210
  59.5 1.0 copy-start.8
  107.7 27.1 %all-to-all-start.6 = ((f32[256,4,128]{2,1,0:T(4,128)}), f32[256,4,128]{2,1,0:T(4,128)S(1)}, u32[]{:S(2)}, u32[]{:S(2)}) async-start(f32[256,4,128]{2,1,0:T(4,128)} %bitcast.14), calls=%async_computation.6 | async-start | bytes 1048576 | tf_op jit(solution)/shard_map/all_to_all | solution.py:210

commit v5 on v4

--- a/solution.py
+++ b/solution.py
@@ -5,6 +5,7 @@
 from jax.experimental.pallas import tpu as pltpu
 from jax.sharding import Mesh
 from jax.sharding import PartitionSpec as P
+
 
 ROW = ("x", "k")
 COL = ("y", "z")
@@ -64,7 +65,9 @@
     ]
 
 
-def split_body(x_ref, high_ref, low_ref, held, sems):
+def split_body(x_ref, me_ref, high_ref, low_ref, held, sems):
+    del me_ref
+
     def copy(i):
         part = pl.ds(i * 1024, 1024)
         return pltpu.make_async_copy(x_ref.at[part], held.at[part], sems.at[i])
@@ -86,7 +89,8 @@
     return major[:64] + major[64:] + mm16(bt_high, low_ref[...])
 
 
-def start_body(high_ref, low_ref, bt_ref, f4t_ref, f2_ref, out_ref):
+def start_body(high_ref, low_ref, bt_ref, f4t_ref, f2_ref, own_ref, out_ref):
+    del own_ref
     k4t = fourth_matrix(f4t_ref[...])
     tail = jnp.concatenate([f2_ref[...], jnp.zeros((8, 96), F32)], axis=1)
     for i in range(8):
@@ -206,31 +210,33 @@
     out_ref[...] = mm(jnp.concatenate(parts, axis=0), linv_ref[...], 1, 1)
 
 
+def turn(block, t):
+    return lax.ppermute(block, ROW, [(i, (i + t) % 8) for i in range(8)])
+
+
 def trade(block, axis):
     return lax.all_to_all(block, axis, split_axis=0, concat_axis=0, tiled=True)
 
 
 def shards(tensor, factor_two, factor_three, factor_four, factor_init):
     x = tensor.reshape(8192, 128)
+    me = lax.axis_index(ROW).astype(jnp.int32).reshape(1)
     high, low = call(
-        split_body, [((1024, 1024), BF16)] * 2, (HBM,),
+        split_body, [((1024, 1024), BF16)] * 2, (HBM, SMEM),
         scratch=(pltpu.VMEM((8192, 128), F32), pltpu.SemaphoreType.DMA((8,))), mib=48, flops=10**8,
-    )(x)
-    me = lax.axis_index(ROW).astype(jnp.int32).reshape(1)
-    (block,) = call(start_body, [((320, 128), F32)], (VMEM,) * 5, mib=12, flops=10**9)(
-        high, low, factor_init.T, factor_four.T, factor_two
-    )
+    )(x, me)
     blocks = call(
         pack_body, [((512, 128), F32)] * 8, (VMEM,) * 3 + (SMEM,),
         scratch=(pltpu.VMEM((1024, 512), BF16),) * 2, mib=16, flops=3 * 10**9,
     )(high, low, factor_four.T, me)
+    (block,) = call(start_body, [((320, 128), F32)], (VMEM,) * 6, mib=12, flops=10**9)(
+        high, low, factor_init.T, factor_four.T, factor_two, blocks[0]
+    )
     block = trade(block.reshape(8, 40, 128), ROW)
     block, f2, twice = call(
         second_body, [((256, 128), F32), ((64, 32), F32), ((64, 64), F32)], (VMEM, VMEM, SMEM), flops=10**7
     )(block, factor_three, me)
-    blocks = [blocks[0]] + [
-        lax.ppermute(blocks[t], ROW, [(i, (i + t) % 8) for i in range(8)]) for t in range(1, 8)
-    ]
+    blocks = [blocks[0]] + [turn(blocks[t], t) for t in range(1, 8)]
     block = trade(block.reshape(32, 8, 128), COL)
     (block,) = call(third_body, [((128, 128), F32)], (VMEM,), flops=10**7)(block.reshape(256, 128))
     block = trade(block.reshape(32, 4, 128), COL)

time: 136 us -> 136 us (level)
  local copies, waits for them, and re-layouts: 4.03 us -> 0.09 us
  starting transfers between devices: 38.5 us -> 40 us
  waiting for transfers between devices: 20.1 us -> 21.6 us
    unnamed x18 -> x8, local copies, waits for them, and re-layouts: 3.95 us -> 0.02 us
  transfers between devices with their start and end apart: 11 -> 11, of which waited for: 6 -> 8; matrix products, arithmetic and copies ran while one was open for 10% -> 10% of each run, Pallas kernels for 5% -> 2%
where the time goes in v5:
time: 136 us; the launch traced here: 135 us
  blocking collectives  42.2 us (31%)
  starting transfers between devices  40 us (29%)
  waiting for transfers between devices  21.6 us (16%)
  Pallas kernels  16.8 us (12%)
  other arithmetic  12.1 us (9%)
  matrix products  1.66 us (1%)
    all_to_all x3, blocking collectives, trade(): return lax.all_to_all(block, axis, split_axis=0, concat_axis=0, tiled=True)  42.2 us
    all_to_all x4, starting transfers between devices, trade(): return lax.all_to_all(block, axis, split_axis=0, concat_axis=0, tiled=True)  30.1 us
    all_to_all x4, waiting for transfers between devices, trade(): return lax.all_to_all(block, axis, split_axis=0, concat_axis=0, tiled=True)  13.4 us
    ppermute x7, starting transfers between devices, turn(): return lax.ppermute(block, ROW, [(i, (i + t) % 8) for i in range(8)])  9.95 us
    ppermute x7, waiting for transfers between devices, turn(): return lax.ppermute(block, ROW, [(i, (i + t) % 8) for i in range(8)])  8.26 us
    another operation x3, other arithmetic, shards(): lower = jnp.linalg.cholesky(square)  6.52 us
    another operation x2, other arithmetic, shards(): jax.scipy.linalg.solve_triangular(lower, jnp.eye(64, dtype=F32), lower=True)  5.55 us
    pallas_call x1, Pallas kernels, shards(): call(pack_body, [((512, 128), F32)] * 8, (VMEM,) * 3 + (SMEM,), scratch=(...  4.42 us
  transfers between devices with their start and end apart: 11, of which 8 were waited for; matrix products, arithmetic and copies ran while one was open for 10% of the time, Pallas kernels for 2%

profile of v5, /device:TPU:1, one launch (start us, length us, event | category | flops | bytes accessed | tf_op | source)
XLA Modules:
  0.0 135.2 jit_solution(17381743913519204661)
XLA Ops:
  0.6 2.4 %shard_map.68 = (bf16[1024,1024]{1,0:T(8,128)(2,1)S(1)}, bf16[1024,1024]{1,0:T(8,128)(2,1)S(1)}) custom-call(f32[8192,128]{1,0:T(8,128)} %bitcast.39, s32[1]{0:T(128)} %bitcast.1.me_ref), custom_call_target="tpu_custom_call" | custom-call | flops 100000000 | bytes 1048576 | tf_op jit(solution)/shard_map/pallas_call | solution.py:224
  3.1 4.4 %shard_map.69 = (f32[512,128]{1,0:T(8,128)S(1)}, f32[512,128]{1,0:T(8,128)}, f32[512,128]{1,0:T(8,128)S(1)}, f32[512,128]{1,0:T(8,128)S(1)}, f32[512,128]{1,0:T(...) custom-call(bf16[1024,1024]{1,0:T(8,128)(2,1)S(1)} %get-tuple-element.20.high_ref, ...), custom_call_target="tpu_custom_call" | custom-call | flops 3000000000 | bytes 1048576 | tf_op jit(solution)/shard_map/pallas_call | solution.py:228
  7.5 1.9 %shard_map.70 = f32[320,128]{1,0:T(8,128)} custom-call(bf16[1024,1024]{1,0:T(8,128)(2,1)S(1)} %get-tuple-element.20.high_ref, bf16[1024,1024]{1,0:T(8,128)(2,1)S(1)} %get-tuple-element.21.low_ref, f32[64,1024]{1,0:T(8,128)S(1)} %bitcast.33, f32[16,32]{1,0:T(8,128)S(1)} %bitcast.38, f32[8,32]{1,0:T(8,128)S(1)} %copy-done.2, ...), custom_call_target="tpu_custom_call" | custom-call | flops 1000000000 | bytes 1048576 | tf_op jit(solution)/shard_map/pallas_call | solution.py:232
  9.4 6.5 %all-to-all-start = ((f32[8,40,128]{2,1,0:T(8,128)}), f32[8,40,128]{2,1,0:T(8,128)S(1)}, u32[]{:S(2)}, u32[]{:S(2)}) async-start(f32[8,40,128]{2,1,0:T(8,128)} %bitcast.4), calls=%async_computation | async-start | bytes 327680 | tf_op jit(solution)/shard_map/all_to_all | solution.py:218
  15.9 1.6 %collective-permute-start = (f32[512,128]{1,0:T(8,128)}, f32[512,128]{1,0:T(8,128)S(1)}, u32[]{:S(2)}, u32[]{:S(2)}) collective-permute-start(f32[512,128]{1,0:T(8,128)} %get-tuple-element.25), channel_id=1, source_target_pairs={{0,32},{32,64},{64,96},{96,128},{128,160},{160,192},{192,224},{224... | collective-permute-start | bytes 786440 | tf_op jit(solution)/shard_map/ppermute | solution.py:214
  17.5 1.2 collective-permute-start.1
  18.7 3.1 %all-to-all-done.r_ref = f32[8,40,128]{2,1,0:T(8,128)S(1)} async-done(((f32[8,40,128]{2,1,0:T(8,128)}), f32[8,40,128]{2,1,0:T(8,128)S(1)}, u32[]{:S(2)}, u32[]{:S(2)}) %all-to-all-start) | async-done | bytes 163872 | tf_op jit(solution)/shard_map/all_to_all | solution.py:218
  21.8 0.9 shard_map.71
  22.7 10.5 %all-to-all-start.1 = ((f32[32,8,128]{2,1,0:T(8,128)}), f32[32,8,128]{2,1,0:T(8,128)S(1)}, u32[]{:S(2)}, u32[]{:S(2)}) async-start(f32[32,8,128]{2,1,0:T(8,128)} %bitcast.5), calls=%async_computation.1 | async-start | bytes 262144 | tf_op jit(solution)/shard_map/all_to_all | solution.py:218
  33.2 1.2 collective-permute-start.2
  34.5 3.1 %collective-permute-start.3 = (f32[512,128]{1,0:T(8,128)S(1)}, f32[512,128]{1,0:T(8,128)S(1)}, u32[]{:S(2)}, u32[]{:S(2)}) collective-permute-start(f32[512,128]{1,0:T(8,128)S(1)} %get-tuple-element.28), channel_id=1, source_target_pairs={{0,128},{32,160},{64,192},{96,224},{128,0},{160,32},{192,64},{224,... | collective-permute-start | bytes 786440 | tf_op jit(solution)/shard_map/ppermute | solution.py:214
  37.6 0.7 collective-permute-start.5
  38.2 2.1 %collective-permute-start.6 = (f32[512,128]{1,0:T(8,128)S(1)}, f32[512,128]{1,0:T(8,128)S(1)}, u32[]{:S(2)}, u32[]{:S(2)}) collective-permute-start(f32[512,128]{1,0:T(8,128)S(1)} %get-tuple-element.31), channel_id=1, source_target_pairs={{0,224},{32,0},{64,32},{96,64},{128,96},{160,128},{192,160},{224,1... | collective-permute-start | bytes 786440 | tf_op jit(solution)/shard_map/ppermute | solution.py:214
  40.3 2.0 %all-to-all-done.1 = f32[32,8,128]{2,1,0:T(8,128)S(1)} async-done(((f32[32,8,128]{2,1,0:T(8,128)}), f32[32,8,128]{2,1,0:T(8,128)S(1)}, u32[]{:S(2)}, u32[]{:S(2)}) %all-to-all-start.1) | async-done | bytes 131104 | tf_op jit(solution)/shard_map/all_to_all | solution.py:218
  42.4 1.1 shard_map.72
  43.5 7.5 %all-to-all-start.2 = ((f32[32,4,128]{2,1,0:T(4,128)}), f32[32,4,128]{2,1,0:T(4,128)S(1)}, u32[]{:S(2)}, u32[]{:S(2)}) async-start(f32[32,4,128]{2,1,0:T(4,128)} %bitcast.7), calls=%async_computation.2 | async-start | bytes 131072 | tf_op jit(solution)/shard_map/all_to_all | solution.py:218
  51.5 0.9 collective-permute-done.4.refs_5_
  52.5 5.6 %collective-permute-done.5.refs_6_ = f32[512,128]{1,0:T(8,128)} collective-permute-done((f32[512,128]{1,0:T(8,128)S(1)}, f32[512,128]{1,0:T(8,128)}, u32[]{:S(2)}, u32[]{:S(2)}) %collective-permute-start.5) | collective-permute-done | bytes 262176 | tf_op jit(solution)/shard_map/ppermute | solution.py:214
  58.1 1.2 collective-permute-done.6.refs_7_
  59.9 2.3 %shard_map.73 = (f32[512,128]{1,0:T(8,128)S(1)}, bf16[512,1024]{1,0:T(8,128)(2,1)S(1)}, bf16[512,1024]{1,0:T(8,128)(2,1)S(1)}) custom-call(f32[128,128]{1,0:T(8,128)S(1)} %bitcast.36, f32[64,32]{1,0:T(8,128)S(1)} %get-tuple-element.24.f2_ref, f32[512,128]{1,0:T(8,128)S(1)} %get-tuple-element.22.own_ref.refs_0_, f32[512,128]{1,0:T(8,128)S(1)} %collective-permute-done.refs_1_, ...), custom_call_target="tpu_custom_call" | custom-call | flops 1000000000 | bytes 1048576 | tf_op jit(solution)/shard_map/pallas_call | solution.py:243
  62.2 14.6 %all_to_all.35.r_ref = f32[32,16,128]{2,1,0:T(8,128)S(1)} all-to-all(f32[32,16,128]{2,1,0:T(8,128)S(1)} %bitcast.34), channel_id=1, replica_groups=mesh['x'=4,'k'=2,'y'=4,'z'=8] {'x','k','y'}, dimensions={0} | all-to-all | bytes 524288 | tf_op jit(solution)/shard_map/all_to_all | solution.py:218
  76.9 13.5 %all_to_all.36.r_ref = f32[8,16,128]{2,1,0:T(8,128)S(1)} all-to-all(f32[8,16,128]{2,1,0:T(8,128)S(1)} %shard_map.74), channel_id=1, replica_groups=mesh['x'=4,'k'=2,'y'=4,'z'=8] {'z'}, dimensions={0} | all-to-all | bytes 131072 | tf_op jit(solution)/shard_map/all_to_all | solution.py:218
  90.4 14.1 %all_to_all.37 = f32[32,16,128]{2,1,0:T(8,128)S(1)} all-to-all(f32[32,16,128]{2,1,0:T(8,128)S(1)} %shard_map.75), channel_id=1, replica_groups=mesh['x'=4,'k'=2,'y'=4,'z'=8] {'x','k','y'}, dimensions={0} | all-to-all | bytes 524288 | tf_op jit(solution)/shard_map/all_to_all | solution.py:218
  104.5 2.8 %shard_map.76 = (f32[1024,128]{1,0:T(8,128)}, f32[64,1024]{1,0:T(8,128)S(1)}) custom-call(f32[512,128]{1,0:T(8,128)S(1)} %bitcast.35, bf16[512,1024]{1,0:T(8,128)(2,1)S(1)} %get-tuple-element.33.high_ref, bf16[512,1024]{1,0:T(8,128)(2,1)S(1)} %get-tuple-element.34.low_ref, f32[64,64]{1,0:T(8,128)S(1)} %get-tuple-element.35.twice_ref, f32[4,32]{1,0:T(4,128)S(1)} %copy-done.3), custom_call_target="tpu_custom_call" | custom-call | flops 1000000000 | bytes 1048576 | tf_op jit(solution)/shard_map/pallas_call | solution.py:251
  107.2 5.6 %all-to-all-start.6 = ((f32[256,4,128]{2,1,0:T(4,128)}), f32[256,4,128]{2,1,0:T(4,128)S(1)}, u32[]{:S(2)}, u32[]{:S(2)}) async-start(f32[256,4,128]{2,1,0:T(4,128)} %bitcast.14), calls=%async_computation.6 | async-start | bytes 1048576 | tf_op jit(solution)/shard_map/all_to_all | solution.py:218
  113.3 5.8 %cholesky.17 = f32[64,64]{1,0:T(8,128)S(1)} custom-call(f32[64,64]{1,0:T(8,128)S(1)} %fusion.3), custom_call_target="Cholesky" | custom-call | tf_op jit(solution)/shard_map/jit(cholesky)/cholesky | solution.py:255
  119.2 0.6 compare_reduce_fusion
  119.8 0.7 fusion
  120.5 4.9 %custom-call.7 = f32[1,64,64]{1,2,0:T(8,128)S(1)} custom-call(f32[1,64,64]{2,1,0:T(8,128)S(1)} %fusion), custom_call_target="InvertDiagBlocksLowerTriangular" | custom-call | tf_op jit(solution)/shard_map/jit(_solve_triangular)/triangular_solve | solution.py:256
  125.6 1.1 fusion.5
  126.7 7.6 %all-to-all-done.6 = f32[256,4,128]{2,1,0:T(4,128)S(1)} async-done(((f32[256,4,128]{2,1,0:T(4,128)}), f32[256,4,128]{2,1,0:T(4,128)S(1)}, u32[]{:S(2)}, u32[]{:S(2)}) %all-to-all-start.6) | async-done | bytes 524320 | tf_op jit(solution)/shard_map/all_to_all | solution.py:218
  134.3 0.9 shard_map.77
  (21 shorter events, 2.0 us)
Async XLA Ops:
  0.6 2.4 %copy-start.1 = (f32[32,16]{0,1:T(8,128)S(1)}, f32[32,16]{0,1:T(8,128)}, u32[]{:S(2)}) copy-start(f32[32,16]{0,1:T(8,128)} %param.8) | copy-start | bytes 6148
  3.0 4.4 %copy-start = (f32[1024,64]{0,1:T(8,128)S(1)}, f32[1024,64]{0,1:T(8,128)}, u32[]{:S(2)}) copy-start(f32[1024,64]{0,1:T(8,128)} %param.9) | copy-start | bytes 786436
  3.1 4.4 %copy-start.2 = (f32[8,32]{1,0:T(8,128)S(1)}, f32[8,32]{1,0:T(8,128)}, u32[]{:S(2)}) copy-start(f32[8,32]{1,0:T(8,128)} %f2_ref.1) | copy-start | bytes 3076
  7.5 14.3 %copy-start.3 = (f32[4,32]{1,0:T(4,128)S(1)}, f32[4,32]{1,0:T(4,128)}, u32[]{:S(2)}) copy-start(f32[4,32]{1,0:T(4,128)} %f3_ref.3) | copy-start | bytes 1540
  9.4 12.4 %all-to-all-start = ((f32[8,40,128]{2,1,0:T(8,128)}), f32[8,40,128]{2,1,0:T(8,128)S(1)}, u32[]{:S(2)}, u32[]{:S(2)}) async-start(f32[8,40,128]{2,1,0:T(8,128)} %bitcast.4), calls=%async_computation | async-start | bytes 327680 | tf_op jit(solution)/shard_map/all_to_all | solution.py:218
  15.9 21.7 %collective-permute-start = (f32[512,128]{1,0:T(8,128)}, f32[512,128]{1,0:T(8,128)S(1)}, u32[]{:S(2)}, u32[]{:S(2)}) collective-permute-start(f32[512,128]{1,0:T(8,128)} %get-tuple-element.25), channel_id=1, source_target_pairs={{0,32},{32,64},{64,96},{96,128},{128,160},{160,192},{192,224},{224... | collective-permute-start | bytes 786440 | tf_op jit(solution)/shard_map/ppermute | solution.py:214
  17.5 20.7 %collective-permute-start.1 = (f32[512,128]{1,0:T(8,128)S(1)}, f32[512,128]{1,0:T(8,128)S(1)}, u32[]{:S(2)}, u32[]{:S(2)}) collective-permute-start(f32[512,128]{1,0:T(8,128)S(1)} %get-tuple-element.26), channel_id=1, source_target_pairs={{0,64},{32,96},{64,128},{96,160},{128,192},{160,224},{192,0},{224,... | collective-permute-start | bytes 786440 | tf_op jit(solution)/shard_map/ppermute | solution.py:214
  22.7 19.7 %all-to-all-start.1 = ((f32[32,8,128]{2,1,0:T(8,128)}), f32[32,8,128]{2,1,0:T(8,128)S(1)}, u32[]{:S(2)}, u32[]{:S(2)}) async-start(f32[32,8,128]{2,1,0:T(8,128)} %bitcast.5), calls=%async_computation.1 | async-start | bytes 262144 | tf_op jit(solution)/shard_map/all_to_all | solution.py:218
  33.2 18.3 %collective-permute-start.2 = (f32[512,128]{1,0:T(8,128)S(1)}, f32[512,128]{1,0:T(8,128)S(1)}, u32[]{:S(2)}, u32[]{:S(2)}) collective-permute-start(f32[512,128]{1,0:T(8,128)S(1)} %get-tuple-element.27), channel_id=1, source_target_pairs={{0,96},{32,128},{64,160},{96,192},{128,224},{160,0},{192,32},{224,... | collective-permute-start | bytes 786440 | tf_op jit(solution)/shard_map/ppermute | solution.py:214
  34.5 17.1 %collective-permute-start.3 = (f32[512,128]{1,0:T(8,128)S(1)}, f32[512,128]{1,0:T(8,128)S(1)}, u32[]{:S(2)}, u32[]{:S(2)}) collective-permute-start(f32[512,128]{1,0:T(8,128)S(1)} %get-tuple-element.28), channel_id=1, source_target_pairs={{0,128},{32,160},{64,192},{96,224},{128,0},{160,32},{192,64},{224,... | collective-permute-start | bytes 786440 | tf_op jit(solution)/shard_map/ppermute | solution.py:214
  37.6 14.9 %collective-permute-start.4 = (f32[512,128]{1,0:T(8,128)S(1)}, f32[512,128]{1,0:T(8,128)S(1)}, u32[]{:S(2)}, u32[]{:S(2)}) collective-permute-start(f32[512,128]{1,0:T(8,128)S(1)} %get-tuple-element.29), channel_id=1, source_target_pairs={{0,160},{32,192},{64,224},{96,0},{128,32},{160,64},{192,96},{224,1... | collective-permute-start | bytes 786440 | tf_op jit(solution)/shard_map/ppermute | solution.py:214
  37.6 20.5 %collective-permute-start.5 = (f32[512,128]{1,0:T(8,128)S(1)}, f32[512,128]{1,0:T(8,128)}, u32[]{:S(2)}, u32[]{:S(2)}) collective-permute-start(f32[512,128]{1,0:T(8,128)S(1)} %get-tuple-element.30), channel_id=1, source_target_pairs={{0,192},{32,224},{64,0},{96,32},{128,64},{160,96},{192,128},{224,1... | collective-permute-start | bytes 786440 | tf_op jit(solution)/shard_map/ppermute | solution.py:214
  38.2 21.0 %collective-permute-start.6 = (f32[512,128]{1,0:T(8,128)S(1)}, f32[512,128]{1,0:T(8,128)S(1)}, u32[]{:S(2)}, u32[]{:S(2)}) collective-permute-start(f32[512,128]{1,0:T(8,128)S(1)} %get-tuple-element.31), channel_id=1, source_target_pairs={{0,224},{32,0},{64,32},{96,64},{128,96},{160,128},{192,160},{224,1... | collective-permute-start | bytes 786440 | tf_op jit(solution)/shard_map/ppermute | solution.py:214
  43.5 16.4 %all-to-all-start.2 = ((f32[32,4,128]{2,1,0:T(4,128)}), f32[32,4,128]{2,1,0:T(4,128)S(1)}, u32[]{:S(2)}, u32[]{:S(2)}) async-start(f32[32,4,128]{2,1,0:T(4,128)} %bitcast.7), calls=%async_computation.2 | async-start | bytes 131072 | tf_op jit(solution)/shard_map/all_to_all | solution.py:218
  107.2 27.1 %all-to-all-start.6 = ((f32[256,4,128]{2,1,0:T(4,128)}), f32[256,4,128]{2,1,0:T(4,128)S(1)}, u32[]{:S(2)}, u32[]{:S(2)}) async-start(f32[256,4,128]{2,1,0:T(4,128)} %bitcast.14), calls=%async_computation.6 | async-start | bytes 1048576 | tf_op jit(solution)/shard_map/all_to_all | solution.py:218

commit v6 on v5

--- a/solution.py
+++ b/solution.py
@@ -47,24 +47,6 @@
     )
 
 
-def fourth_matrix(f4t):
-    wide = jnp.concatenate([f4t] * 4, axis=1)
-    owner = lax.broadcasted_iota(jnp.int32, (8, 128), 1) // 32
-    rows = [
-        jnp.where(owner == c, wide[lo * 8 : lo * 8 + 8], 0.0) for lo in range(2) for c in range(4)
-    ]
-    return jnp.concatenate(rows, axis=0)
-
-
-def fourth_mode(z, k4t):
-    stack = jnp.concatenate([z[:, b * 128 : (b + 1) * 128] for b in range(8)], axis=0)
-    m = mm(k4t, stack, 1, 1)
-    return [
-        jnp.concatenate([m[:32, b * 64 : b * 64 + 64], m[32:, b * 64 : b * 64 + 64]], axis=1)
-        for b in range(8)
-    ]
-
-
 def split_body(x_ref, me_ref, high_ref, low_ref, held, sems):
     del me_ref
 
@@ -83,26 +65,8 @@
             low_ref[rows, b * 128 : b * 128 + 128] = low
 
 
-def first_mode(bt, high_ref, low_ref):
-    bt_high, bt_low = halves(bt)
-    major = mm16(jnp.concatenate([bt_high, bt_low], axis=0), high_ref[...])
-    return major[:64] + major[64:] + mm16(bt_high, low_ref[...])
-
-
-def start_body(high_ref, low_ref, bt_ref, f4t_ref, f2_ref, own_ref, out_ref):
-    del own_ref
-    k4t = fourth_matrix(f4t_ref[...])
-    tail = jnp.concatenate([f2_ref[...], jnp.zeros((8, 96), F32)], axis=1)
-    for i in range(8):
-        out_ref[i * 40 + 32 : i * 40 + 40, :] = tail
-    z = first_mode(bt_ref[...], high_ref, low_ref)
-    for b, comb in enumerate(fourth_mode(z, k4t)):
-        for c in range(4):
-            out_ref[pl.ds(c * 8 + b, 8, stride=40), :] = comb[c * 8 : (c + 1) * 8]
-
-
-def pack_body(high_ref, low_ref, f4t_ref, me_ref, *refs):
-    outs, (mat_high, mat_low) = refs[:8], refs[8:]
+def pack_body(high_ref, low_ref, f4t_ref, bt_ref, f2_ref, me_ref, *refs):
+    outs, (first_ref, mat_high, mat_low) = refs[:8], refs[8:]
     lane = lax.broadcasted_iota(jnp.int32, (16, 512), 1)
     index = lax.broadcasted_iota(jnp.int32, (16, 512), 0)
     owner = lane // 8 % 2 * 8 + (me_ref[0] + lane // 64) % 8
@@ -113,10 +77,16 @@
     for n in range(32):
         mat_high[n * 32 : n * 32 + 32, :] = jnp.where(spot == n, wide_high.astype(F32), 0.0).astype(BF16)
         mat_low[n * 32 : n * 32 + 32, :] = jnp.where(spot == n, wide_low.astype(F32), 0.0).astype(BF16)
+    bt_high, bt_low = halves(bt_ref[...])
+    both = jnp.concatenate([bt_high, bt_low], axis=0)
+    tail = jnp.concatenate([f2_ref[...], jnp.zeros((8, 96), F32)], axis=1)
+    for i in range(8):
+        first_ref[i, 32:40, :] = tail
+    z = jnp.zeros((64, 512), F32)
     for t in range(4):
         parts = []
-        for start in (t * 128, 512 + t * 128):
-            rows = slice(start, start + 128)
+        spans = [slice(start, start + 128) for start in (t * 128, 512 + t * 128)]
+        for rows in spans:
             parts.append(
                 mm16(high_ref[rows, :], mat_high[...])
                 + mm16(high_ref[rows, :], mat_low[...])
@@ -125,26 +95,34 @@
         for n, out in enumerate(outs):
             lanes = slice(n * 64, n * 64 + 64)
             out[t * 128 : t * 128 + 128, :] = jnp.concatenate([p[:, lanes] for p in parts], axis=1)
-
-
-def second_body(r_ref, f3_ref, me_ref, out_ref, f2_ref, twice_ref):
+        p_high, p_low = halves(jnp.concatenate(parts, axis=0))
+        major = mm16(jnp.concatenate([both[:, rows] for rows in spans], axis=1), p_high)
+        z = z + major[:64] + major[64:] + mm16(jnp.concatenate([bt_high[:, rows] for rows in spans], axis=1), p_low)
+    z = z.T
+    for n in range(8):
+        for c in range(4):
+            base = n * 64 + c * 16
+            first_ref[(me_ref[0] + n) % 8, c * 8 : c * 8 + 8, :] = jnp.concatenate(
+                [z[base : base + 8], z[base + 8 : base + 16]], axis=1
+            )
+
+
+def second_body(r_ref, f3_ref, me_ref, out_ref, f2_ref):
     f2 = r_ref[:, 32:40, :].reshape(64, 128)[:, :32]
     data = jnp.concatenate([r_ref[:, c * 8 : (c + 1) * 8, :].reshape(64, 128) for c in range(4)], axis=1)
     y = mm(f2, data, 0, 0)
-    f3 = jnp.concatenate([f3_ref[...], jnp.zeros((4, 96), F32)], axis=1)
+    f3 = jnp.concatenate([f3_ref[c : c + 1, :] for c in range(4)], axis=1)
     for c in range(4):
-        out_ref[pl.ds(c, 32, stride=8), :] = y[:, c * 128 : (c + 1) * 128]
-        out_ref[pl.ds(4 + c, 32, stride=8), :] = jnp.broadcast_to(f3[c : c + 1], (32, 128))
+        out_ref[pl.ds(c, 32, stride=5), :] = y[:, c * 128 : (c + 1) * 128]
+    out_ref[pl.ds(4, 32, stride=5), :] = jnp.broadcast_to(f3, (32, 128))
     turned = jnp.concatenate([r_ref[(me_ref[0] - t + 8) % 8, 32:40, :] for t in range(8)], axis=0)[:, :32]
     f2_ref[...] = turned
-    g = lax.broadcasted_iota(jnp.int32, (32, 64), 0)
-    slot = lax.broadcasted_iota(jnp.int32, (32, 64), 1)
-    twice_ref[...] = mm(turned, jnp.where(slot // 8 * 4 + slot % 4 == g, 1.0, 0.0).astype(F32))
 
 
 def third_body(r_ref, out_ref):
-    data = jnp.concatenate([r_ref[pl.ds(c, 32, stride=8), :] for c in range(4)], axis=0)
-    f3 = jnp.concatenate([r_ref[pl.ds(4 + c, 32, stride=8), :] for c in range(4)], axis=0)[:, :32]
+    data = jnp.concatenate([r_ref[pl.ds(c, 32, stride=5), :] for c in range(4)], axis=0)
+    f3 = r_ref[pl.ds(4, 32, stride=5), :]
+    f3 = jnp.concatenate([f3[:, c * 32 : c * 32 + 32] for c in range(4)], axis=0)
     q = mm(f3, mm(f3, data, 0, 0))
     for c in range(4):
         out_ref[pl.ds(c, 32, stride=4), :] = q[c * 32 : (c + 1) * 32]
@@ -174,7 +152,10 @@
         out_ref[i] = total
 
 
-def core_two_body(image_ref, high_ref, low_ref, twice_ref, f3_ref, out_ref, turned_ref):
+def core_two_body(image_ref, high_ref, low_ref, f2_ref, f3_ref, out_ref, turned_ref):
+    g = lax.broadcasted_iota(jnp.int32, (32, 64), 0)
+    slot = lax.broadcasted_iota(jnp.int32, (32, 64), 1)
+    twice = mm(f2_ref[...], jnp.where(slot // 8 * 4 + slot % 4 == g, 1.0, 0.0).astype(F32))
     flat = image_ref[...].T
     turned_ref[...] = jnp.concatenate([flat[:64], flat[64:]], axis=1)
     bt_high, bt_low = halves(flat)
@@ -186,7 +167,7 @@
     pieces = [
         jnp.concatenate([z[t * 64 + n * 8 : t * 64 + n * 8 + 8] for t in range(8)], axis=0) for n in range(8)
     ]
-    y = mm(twice_ref[...], jnp.concatenate(pieces, axis=1), 0, 0)
+    y = mm(twice, jnp.concatenate(pieces, axis=1), 0, 0)
     upper = lax.broadcasted_iota(jnp.int32, (8, 128), 0) < 4
     for f in range(0, 32, 2):
         scale = [jnp.where(upper, f3_ref[c, f], f3_ref[c, f + 1]) for c in range(4)]
@@ -225,20 +206,17 @@
         split_body, [((1024, 1024), BF16)] * 2, (HBM, SMEM),
         scratch=(pltpu.VMEM((8192, 128), F32), pltpu.SemaphoreType.DMA((8,))), mib=48, flops=10**8,
     )(x, me)
-    blocks = call(
-        pack_body, [((512, 128), F32)] * 8, (VMEM,) * 3 + (SMEM,),
+    *blocks, block = call(
+        pack_body, [((512, 128), F32)] * 8 + [((8, 40, 128), F32)], (VMEM,) * 5 + (SMEM,),
         scratch=(pltpu.VMEM((1024, 512), BF16),) * 2, mib=16, flops=3 * 10**9,
-    )(high, low, factor_four.T, me)
-    (block,) = call(start_body, [((320, 128), F32)], (VMEM,) * 6, mib=12, flops=10**9)(
-        high, low, factor_init.T, factor_four.T, factor_two, blocks[0]
-    )
-    block = trade(block.reshape(8, 40, 128), ROW)
-    block, f2, twice = call(
-        second_body, [((256, 128), F32), ((64, 32), F32), ((64, 64), F32)], (VMEM, VMEM, SMEM), flops=10**7
+    )(high, low, factor_four.T, factor_init.T, factor_two, me)
+    block = trade(block, ROW)
+    block, f2 = call(
+        second_body, [((160, 128), F32), ((64, 32), F32)], (VMEM, VMEM, SMEM), flops=10**7
     )(block, factor_three, me)
     blocks = [blocks[0]] + [turn(blocks[t], t) for t in range(1, 8)]
-    block = trade(block.reshape(32, 8, 128), COL)
-    (block,) = call(third_body, [((128, 128), F32)], (VMEM,), flops=10**7)(block.reshape(256, 128))
+    block = trade(block.reshape(32, 1, 640), COL)
+    (block,) = call(third_body, [((128, 128), F32)], (VMEM,), flops=10**7)(block.reshape(160, 128))
     block = trade(block.reshape(32, 4, 128), COL)
     image, high, low = call(
         image_body, [((512, 128), F32), ((512, 1024), BF16), ((512, 1024), BF16)], (VMEM,) * 10, mib=12, flops=10**9
@@ -250,7 +228,7 @@
     image = trade(image, PLANE)
     block, turned = call(
         core_two_body, [((1024, 128), F32), ((64, 1024), F32)], (VMEM,) * 4 + (SMEM,), mib=12, flops=10**9
-    )(image.reshape(512, 128), high, low, twice, factor_three)
+    )(image.reshape(512, 128), high, low, f2, factor_three)
     square = mm(turned, turned, 1, 1)
     lower = jnp.linalg.cholesky(square)
     linv = jax.scipy.linalg.solve_triangular(lower, jnp.eye(64, dtype=F32), lower=True)

time: 136 us -> 139 us (1.022)
  the two profiles are of different devices: /device:TPU:1 before, /device:TPU:32 now
where the time goes in v6:
time: 139 us; the launch traced here: 136 us
  blocking collectives  54.6 us (39%)
  starting transfers between devices  31.5 us (23%)
  waiting for transfers between devices  19.3 us (14%)
  Pallas kernels  14.5 us (10%)
  other arithmetic  12.1 us (9%)
  local copies, waits for them, and re-layouts  1.74 us (1%)
  matrix products  1.66 us (1%)
    all_to_all x4, blocking collectives, trade(): return lax.all_to_all(block, axis, split_axis=0, concat_axis=0, tiled=True)  54.6 us
    all_to_all x3, starting transfers between devices, trade(): return lax.all_to_all(block, axis, split_axis=0, concat_axis=0, tiled=True)  24.3 us
    all_to_all x3, waiting for transfers between devices, trade(): return lax.all_to_all(block, axis, split_axis=0, concat_axis=0, tiled=True)  11.7 us
    ppermute x7, waiting for transfers between devices, turn(): return lax.ppermute(block, ROW, [(i, (i + t) % 8) for i in range(8)])  7.58 us
    ppermute x7, starting transfers between devices, turn(): return lax.ppermute(block, ROW, [(i, (i + t) % 8) for i in range(8)])  7.25 us
    another operation x3, other arithmetic, shards(): lower = jnp.linalg.cholesky(square)  6.52 us
    another operation x2, other arithmetic, shards(): jax.scipy.linalg.solve_triangular(lower, jnp.eye(64, dtype=F32), lower=True)  5.55 us
    pallas_call x1, Pallas kernels, shards(): call(pack_body, [((512, 128), F32)] * 8 + [((8, 40, 128), F32)], (VMEM,)...  4.89 us
  transfers between devices with their start and end apart: 10, of which 6 were waited for; matrix products, arithmetic and copies ran while one was open for 10% of the time, Pallas kernels for 2%

profile of v6, /device:TPU:32, one launch (start us, length us, event | category | flops | bytes accessed | tf_op | source)
XLA Modules:
  0.0 136.2 jit_solution(6007507567141191249)
XLA Ops:
  0.7 2.4 %shard_map.68 = (bf16[1024,1024]{1,0:T(8,128)(2,1)S(1)}, bf16[1024,1024]{1,0:T(8,128)(2,1)S(1)}) custom-call(f32[8192,128]{1,0:T(8,128)} %bitcast.37, s32[1]{0:T(128)} %bitcast.1.me_ref), custom_call_target="tpu_custom_call" | custom-call | flops 100000000 | bytes 1048576 | tf_op jit(solution)/shard_map/pallas_call | solution.py:205
  3.1 4.9 %shard_map.69 = (f32[512,128]{1,0:T(8,128)S(1)}, f32[512,128]{1,0:T(8,128)S(1)}, f32[512,128]{1,0:T(8,128)S(1)}, f32[512,128]{1,0:T(8,128)S(1)}, f32[512,128]{1,...) custom-call(bf16[1024,1024]{1,0:T(8,128)(2,1)S(1)} %get-tuple-elemen, ...), custom_call_target="tpu_custom_call" | custom-call | flops 3000000000 | bytes 1048576 | tf_op jit(solution)/shard_map/pallas_call | solution.py:209
  8.0 0.7 copy-done.4
  8.7 1.5 %collective-permute-start.1 = (f32[512,128]{1,0:T(8,128)S(1)}, f32[512,128]{1,0:T(8,128)S(1)}, u32[]{:S(2)}, u32[]{:S(2)}) collective-permute-start(f32[512,128]{1,0:T(8,128)S(1)} %get-tuple-element.27), channel_id=1, source_target_pairs={{0,64},{32,96},{64,128},{96,160},{128,192},{160,224},{192,0},{224,... | collective-permute-start | bytes 786440 | tf_op jit(solution)/shard_map/ppermute | solution.py:195
  10.2 13.2 %all_to_all.35.r_ref = f32[8,40,128]{2,1,0:T(8,128)S(1)} all-to-all(f32[8,40,128]{2,1,0:T(8,128)S(1)} %get-tuple-element.22), channel_id=1, replica_groups=mesh['x'=4,'k'=2,'y'=4,'z'=8] {'x','k'}, dimensions={0} | all-to-all | bytes 327680 | tf_op jit(solution)/shard_map/all_to_all | solution.py:199
  23.4 0.9 shard_map.70
  24.3 11.4 %all-to-all-start.1 = ((f32[32,1,640]{2,1,0:T(1,128)}), f32[32,1,640]{2,1,0:T(1,128)S(1)}, u32[]{:S(2)}, u32[]{:S(2)}) async-start(f32[32,1,640]{2,1,0:T(1,128)} %bitcast.4), calls=%async_computation.1 | async-start | bytes 163840 | tf_op jit(solution)/shard_map/all_to_all | solution.py:199
  35.8 1.6 %collective-permute-start.3 = (f32[512,128]{1,0:T(8,128)S(1)}, f32[512,128]{1,0:T(8,128)S(1)}, u32[]{:S(2)}, u32[]{:S(2)}) collective-permute-start(f32[512,128]{1,0:T(8,128)S(1)} %get-tuple-element.29), channel_id=1, source_target_pairs={{0,128},{32,160},{64,192},{96,224},{128,0},{160,32},{192,64},{224,... | collective-permute-start | bytes 786440 | tf_op jit(solution)/shard_map/ppermute | solution.py:195
  37.4 2.9 %collective-permute-start.4 = (f32[512,128]{1,0:T(8,128)S(1)}, f32[512,128]{1,0:T(8,128)S(1)}, u32[]{:S(2)}, u32[]{:S(2)}) collective-permute-start(f32[512,128]{1,0:T(8,128)S(1)} %get-tuple-element.30), channel_id=1, source_target_pairs={{0,160},{32,192},{64,224},{96,0},{128,32},{160,64},{192,96},{224,1... | collective-permute-start | bytes 786440 | tf_op jit(solution)/shard_map/ppermute | solution.py:195
  40.2 0.9 collective-permute-start.5
  41.5 3.6 %all-to-all-done.1 = f32[32,1,640]{2,1,0:T(1,128)S(1)} async-done(((f32[32,1,640]{2,1,0:T(1,128)}), f32[32,1,640]{2,1,0:T(1,128)S(1)}, u32[]{:S(2)}, u32[]{:S(2)}) %all-to-all-start.1) | async-done | bytes 81952 | tf_op jit(solution)/shard_map/all_to_all | solution.py:199
  45.1 1.2 shard_map.71
  46.3 6.2 %all-to-all-start.2 = ((f32[32,4,128]{2,1,0:T(4,128)}), f32[32,4,128]{2,1,0:T(4,128)S(1)}, u32[]{:S(2)}, u32[]{:S(2)}) async-start(f32[32,4,128]{2,1,0:T(4,128)} %bitcast.6), calls=%async_computation.2 | async-start | bytes 131072 | tf_op jit(solution)/shard_map/all_to_all | solution.py:199
  52.5 0.7 collective-permute-done.4.refs_5_
  53.2 4.7 %collective-permute-done.5.refs_6_ = f32[512,128]{1,0:T(8,128)S(1)} collective-permute-done((f32[512,128]{1,0:T(8,128)S(1)}, f32[512,128]{1,0:T(8,128)S(1)}, u32[]{:S(2)}, u32[]{:S(2)}) %collective-permute-start.5) | collective-permute-done | bytes 262176 | tf_op jit(solution)/shard_map/ppermute | solution.py:195
  57.8 2.2 %collective-permute-done.6.refs_7_ = f32[512,128]{1,0:T(8,128)S(1)} collective-permute-done((f32[512,128]{1,0:T(8,128)S(1)}, f32[512,128]{1,0:T(8,128)S(1)}, u32[]{:S(2)}, u32[]{:S(2)}) %collective-permute-start.6) | collective-permute-done | bytes 262176 | tf_op jit(solution)/shard_map/ppermute | solution.py:195
  60.1 1.5 %all-to-all-done.2 = f32[32,4,128]{2,1,0:T(4,128)S(1)} async-done(((f32[32,4,128]{2,1,0:T(4,128)}), f32[32,4,128]{2,1,0:T(4,128)S(1)}, u32[]{:S(2)}, u32[]{:S(2)}) %all-to-all-start.2) | async-done | bytes 65568 | tf_op jit(solution)/shard_map/all_to_all | solution.py:199
  61.6 0.9 copy-done.5
  62.6 1.4 %shard_map.72 = (f32[512,128]{1,0:T(8,128)S(1)}, bf16[512,1024]{1,0:T(8,128)(2,1)S(1)}, bf16[512,1024]{1,0:T(8,128)(2,1)S(1)}) custom-call(f32[128,128]{1,0:T(8,128)S(1)} %bitcast.34, f32[64,32]{1,0:T(8,128)S(1)} %get-tuple-element.24.f2_ref, f32[512,128]{1,0:T(8,128)S(1)} %copy-done.5, f32[512,128]{1,0:T(8,128)S(1)} %collective-permute-done.refs_1_, ...), custom_call_target="tpu_custom_call" | custom-call | flops 1000000000 | bytes 1048576 | tf_op jit(solution)/shard_map/pallas_call | solution.py:221
  64.0 14.6 %all_to_all.36.r_ref = f32[32,16,128]{2,1,0:T(8,128)S(1)} all-to-all(f32[32,16,128]{2,1,0:T(8,128)S(1)} %bitcast.32), channel_id=1, replica_groups=mesh['x'=4,'k'=2,'y'=4,'z'=8] {'x','k','y'}, dimensions={0} | all-to-all | bytes 524288 | tf_op jit(solution)/shard_map/all_to_all | solution.py:199
  78.6 14.1 %all_to_all.37.r_ref = f32[8,16,128]{2,1,0:T(8,128)S(1)} all-to-all(f32[8,16,128]{2,1,0:T(8,128)S(1)} %shard_map.73), channel_id=1, replica_groups=mesh['x'=4,'k'=2,'y'=4,'z'=8] {'z'}, dimensions={0} | all-to-all | bytes 131072 | tf_op jit(solution)/shard_map/all_to_all | solution.py:199
  92.7 12.7 %all_to_all.38 = f32[32,16,128]{2,1,0:T(8,128)S(1)} all-to-all(f32[32,16,128]{2,1,0:T(8,128)S(1)} %shard_map.74), channel_id=1, replica_groups=mesh['x'=4,'k'=2,'y'=4,'z'=8] {'x','k','y'}, dimensions={0} | all-to-all | bytes 524288 | tf_op jit(solution)/shard_map/all_to_all | solution.py:199
  105.4 2.7 %shard_map.75 = (f32[1024,128]{1,0:T(8,128)}, f32[64,1024]{1,0:T(8,128)S(1)}) custom-call(f32[512,128]{1,0:T(8,128)S(1)} %bitcast.33, bf16[512,1024]{1,0:T(8,128)(2,1)S(1)} %get-tuple-element.34.high_ref, bf16[512,1024]{1,0:T(8,128)(2,1)S(1)} %get-tuple-element.35.low_ref, f32[64,32]{1,0:T(8,128)S(1)} %get-tuple-element.24.f2_ref, f32[4,32]{1,0:T(4,128)S(1)} %copy-done), custom_call_target="tpu_custom_call" | custom-call | flops 1000000000 | bytes 1048576 | tf_op jit(solution)/shard_map/pallas_call | solution.py:229
  108.2 6.7 %all-to-all-start.6 = ((f32[256,4,128]{2,1,0:T(4,128)}), f32[256,4,128]{2,1,0:T(4,128)S(1)}, u32[]{:S(2)}, u32[]{:S(2)}) async-start(f32[256,4,128]{2,1,0:T(4,128)} %bitcast.13), calls=%async_computation.6 | async-start | bytes 1048576 | tf_op jit(solution)/shard_map/all_to_all | solution.py:199
  114.9 0.4 fusion.4
  115.4 5.8 %cholesky.17 = f32[64,64]{1,0:T(8,128)S(1)} custom-call(f32[64,64]{1,0:T(8,128)S(1)} %fusion.3), custom_call_target="Cholesky" | custom-call | tf_op jit(solution)/shard_map/jit(cholesky)/cholesky | solution.py:233
  121.3 0.6 compare_reduce_fusion
  121.9 0.7 fusion
  122.6 4.9 %custom-call.7 = f32[1,64,64]{1,2,0:T(8,128)S(1)} custom-call(f32[1,64,64]{2,1,0:T(8,128)S(1)} %fusion), custom_call_target="InvertDiagBlocksLowerTriangular" | custom-call | tf_op jit(solution)/shard_map/jit(_solve_triangular)/triangular_solve | solution.py:234
  127.7 1.1 fusion.5
  128.8 6.5 %all-to-all-done.6 = f32[256,4,128]{2,1,0:T(4,128)S(1)} async-done(((f32[256,4,128]{2,1,0:T(4,128)}), f32[256,4,128]{2,1,0:T(4,128)S(1)}, u32[]{:S(2)}, u32[]{:S(2)}) %all-to-all-start.6) | async-done | bytes 524320 | tf_op jit(solution)/shard_map/all_to_all | solution.py:199
  135.3 0.9 shard_map.76
  (23 shorter events, 0.8 us)
Async XLA Ops:
  0.6 2.4 %copy-start.1 = (f32[1024,64]{0,1:T(8,128)S(1)}, f32[1024,64]{0,1:T(8,128)}, u32[]{:S(2)}) copy-start(f32[1024,64]{0,1:T(8,128)} %param.9) | copy-start | bytes 786436
  0.6 2.4 %copy-start.2 = (f32[32,16]{0,1:T(8,128)S(1)}, f32[32,16]{0,1:T(8,128)}, u32[]{:S(2)}) copy-start(f32[32,16]{0,1:T(8,128)} %param.8) | copy-start | bytes 6148
  0.7 2.4 %copy-start.3 = (f32[8,32]{1,0:T(8,128)S(1)}, f32[8,32]{1,0:T(8,128)}, u32[]{:S(2)}) copy-start(f32[8,32]{1,0:T(8,128)} %f2_ref.1) | copy-start | bytes 3076
  3.1 20.3 %copy-start = (f32[4,32]{1,0:T(4,128)S(1)}, f32[4,32]{1,0:T(4,128)}, u32[]{:S(2)}) copy-start(f32[4,32]{1,0:T(4,128)} %f3_ref.3) | copy-start | bytes 1540
  8.0 0.7 copy-start.4
  8.7 31.5 %collective-permute-start = (f32[512,128]{1,0:T(8,128)S(1)}, f32[512,128]{1,0:T(8,128)S(1)}, u32[]{:S(2)}, u32[]{:S(2)}) collective-permute-start(f32[512,128]{1,0:T(8,128)S(1)} %get-tuple-element.26), channel_id=1, source_target_pairs={{0,32},{32,64},{64,96},{96,128},{128,160},{160,192},{192,224},{224... | collective-permute-start | bytes 786440 | tf_op jit(solution)/shard_map/ppermute | solution.py:195
  8.7 32.4 %collective-permute-start.1 = (f32[512,128]{1,0:T(8,128)S(1)}, f32[512,128]{1,0:T(8,128)S(1)}, u32[]{:S(2)}, u32[]{:S(2)}) collective-permute-start(f32[512,128]{1,0:T(8,128)S(1)} %get-tuple-element.27), channel_id=1, source_target_pairs={{0,64},{32,96},{64,128},{96,160},{128,192},{160,224},{192,0},{224,... | collective-permute-start | bytes 786440 | tf_op jit(solution)/shard_map/ppermute | solution.py:195
  24.3 20.8 %all-to-all-start.1 = ((f32[32,1,640]{2,1,0:T(1,128)}), f32[32,1,640]{2,1,0:T(1,128)S(1)}, u32[]{:S(2)}, u32[]{:S(2)}) async-start(f32[32,1,640]{2,1,0:T(1,128)} %bitcast.4), calls=%async_computation.1 | async-start | bytes 163840 | tf_op jit(solution)/shard_map/all_to_all | solution.py:199
  35.7 16.8 %collective-permute-start.2 = (f32[512,128]{1,0:T(8,128)S(1)}, f32[512,128]{1,0:T(8,128)S(1)}, u32[]{:S(2)}, u32[]{:S(2)}) collective-permute-start(f32[512,128]{1,0:T(8,128)S(1)} %get-tuple-element.28), channel_id=1, source_target_pairs={{0,96},{32,128},{64,160},{96,192},{128,224},{160,0},{192,32},{224,... | collective-permute-start | bytes 786440 | tf_op jit(solution)/shard_map/ppermute | solution.py:195
  35.8 16.7 %collective-permute-start.3 = (f32[512,128]{1,0:T(8,128)S(1)}, f32[512,128]{1,0:T(8,128)S(1)}, u32[]{:S(2)}, u32[]{:S(2)}) collective-permute-start(f32[512,128]{1,0:T(8,128)S(1)} %get-tuple-element.29), channel_id=1, source_target_pairs={{0,128},{32,160},{64,192},{96,224},{128,0},{160,32},{192,64},{224,... | collective-permute-start | bytes 786440 | tf_op jit(solution)/shard_map/ppermute | solution.py:195
  37.4 15.8 %collective-permute-start.4 = (f32[512,128]{1,0:T(8,128)S(1)}, f32[512,128]{1,0:T(8,128)S(1)}, u32[]{:S(2)}, u32[]{:S(2)}) collective-permute-start(f32[512,128]{1,0:T(8,128)S(1)} %get-tuple-element.30), channel_id=1, source_target_pairs={{0,160},{32,192},{64,224},{96,0},{128,32},{160,64},{192,96},{224,1... | collective-permute-start | bytes 786440 | tf_op jit(solution)/shard_map/ppermute | solution.py:195
  40.2 17.6 %collective-permute-start.5 = (f32[512,128]{1,0:T(8,128)S(1)}, f32[512,128]{1,0:T(8,128)S(1)}, u32[]{:S(2)}, u32[]{:S(2)}) collective-permute-start(f32[512,128]{1,0:T(8,128)S(1)} %get-tuple-element.31), channel_id=1, source_target_pairs={{0,192},{32,224},{64,0},{96,32},{128,64},{160,96},{192,128},{224,1... | collective-permute-start | bytes 786440 | tf_op jit(solution)/shard_map/ppermute | solution.py:195
  41.2 18.9 %collective-permute-start.6 = (f32[512,128]{1,0:T(8,128)S(1)}, f32[512,128]{1,0:T(8,128)S(1)}, u32[]{:S(2)}, u32[]{:S(2)}) collective-permute-start(f32[512,128]{1,0:T(8,128)S(1)} %get-tuple-element.32), channel_id=1, source_target_pairs={{0,224},{32,0},{64,32},{96,64},{128,96},{160,128},{192,160},{224,1... | collective-permute-start | bytes 786440 | tf_op jit(solution)/shard_map/ppermute | solution.py:195
  46.3 15.3 %all-to-all-start.2 = ((f32[32,4,128]{2,1,0:T(4,128)}), f32[32,4,128]{2,1,0:T(4,128)S(1)}, u32[]{:S(2)}, u32[]{:S(2)}) async-start(f32[32,4,128]{2,1,0:T(4,128)} %bitcast.6), calls=%async_computation.2 | async-start | bytes 131072 | tf_op jit(solution)/shard_map/all_to_all | solution.py:199
  61.6 1.0 copy-start.5
  108.2 27.2 %all-to-all-start.6 = ((f32[256,4,128]{2,1,0:T(4,128)}), f32[256,4,128]{2,1,0:T(4,128)S(1)}, u32[]{:S(2)}, u32[]{:S(2)}) async-start(f32[256,4,128]{2,1,0:T(4,128)} %bitcast.13), calls=%async_computation.6 | async-start | bytes 1048576 | tf_op jit(solution)/shard_map/all_to_all | solution.py:199

commit v7 on v6

--- a/solution.py
+++ b/solution.py
@@ -83,9 +83,9 @@
     for i in range(8):
         first_ref[i, 32:40, :] = tail
     z = jnp.zeros((64, 512), F32)
-    for t in range(4):
+    for t in range(2):
         parts = []
-        spans = [slice(start, start + 128) for start in (t * 128, 512 + t * 128)]
+        spans = [slice(start, start + 256) for start in (t * 256, 512 + t * 256)]
         for rows in spans:
             parts.append(
                 mm16(high_ref[rows, :], mat_high[...])
@@ -94,7 +94,7 @@
             )
         for n, out in enumerate(outs):
             lanes = slice(n * 64, n * 64 + 64)
-            out[t * 128 : t * 128 + 128, :] = jnp.concatenate([p[:, lanes] for p in parts], axis=1)
+            out[t * 256 : t * 256 + 256, :] = jnp.concatenate([p[:, lanes] for p in parts], axis=1)
         p_high, p_low = halves(jnp.concatenate(parts, axis=0))
         major = mm16(jnp.concatenate([both[:, rows] for rows in spans], axis=1), p_high)
         z = z + major[:64] + major[64:] + mm16(jnp.concatenate([bt_high[:, rows] for rows in spans], axis=1), p_low)

time: 139 us -> 138 us (level)
  no operation moved by 1% of the time
where the time goes in v7:
time: 138 us; the launch traced here: 136 us
  blocking collectives  54.4 us (39%)
  starting transfers between devices  31.5 us (23%)
  waiting for transfers between devices  19.3 us (14%)
  Pallas kernels  14.1 us (10%)
  other arithmetic  12.1 us (9%)
  local copies, waits for them, and re-layouts  1.74 us (1%)
  matrix products  1.66 us (1%)
    all_to_all x4, blocking collectives, trade(): return lax.all_to_all(block, axis, split_axis=0, concat_axis=0, tiled=True)  54.4 us
    all_to_all x3, starting transfers between devices, trade(): return lax.all_to_all(block, axis, split_axis=0, concat_axis=0, tiled=True)  24.3 us
    all_to_all x3, waiting for transfers between devices, trade(): return lax.all_to_all(block, axis, split_axis=0, concat_axis=0, tiled=True)  11.7 us
    ppermute x7, waiting for transfers between devices, turn(): return lax.ppermute(block, ROW, [(i, (i + t) % 8) for i in range(8)])  7.58 us
    ppermute x7, starting transfers between devices, turn(): return lax.ppermute(block, ROW, [(i, (i + t) % 8) for i in range(8)])  7.25 us
    another operation x3, other arithmetic, shards(): lower = jnp.linalg.cholesky(square)  6.52 us
    another operation x2, other arithmetic, shards(): jax.scipy.linalg.solve_triangular(lower, jnp.eye(64, dtype=F32), lower=True)  5.55 us
    pallas_call x1, Pallas kernels, shards(): call(pack_body, [((512, 128), F32)] * 8 + [((8, 40, 128), F32)], (VMEM,)...  4.55 us
  transfers between devices with their start and end apart: 10, of which 6 were waited for; matrix products, arithmetic and copies ran while one was open for 10% of the time, Pallas kernels for 2%

profile of v7, /device:TPU:32, one launch (start us, length us, event | category | flops | bytes accessed | tf_op | source)
XLA Modules:
  0.0 135.7 jit_solution(10531197758831593938)
XLA Ops:
  0.7 2.4 %shard_map.68 = (bf16[1024,1024]{1,0:T(8,128)(2,1)S(1)}, bf16[1024,1024]{1,0:T(8,128)(2,1)S(1)}) custom-call(f32[8192,128]{1,0:T(8,128)} %bitcast.37, s32[1]{0:T(128)} %bitcast.1.me_ref), custom_call_target="tpu_custom_call" | custom-call | flops 100000000 | bytes 1048576 | tf_op jit(solution)/shard_map/pallas_call | solution.py:205
  3.1 4.5 %shard_map.69 = (f32[512,128]{1,0:T(8,128)S(1)}, f32[512,128]{1,0:T(8,128)S(1)}, f32[512,128]{1,0:T(8,128)S(1)}, f32[512,128]{1,0:T(8,128)S(1)}, f32[512,128]{1,...) custom-call(bf16[1024,1024]{1,0:T(8,128)(2,1)S(1)} %get-tuple-elemen, ...), custom_call_target="tpu_custom_call" | custom-call | flops 3000000000 | bytes 1048576 | tf_op jit(solution)/shard_map/pallas_call | solution.py:209
  7.7 0.7 copy-done.4
  8.4 1.5 %collective-permute-start.1 = (f32[512,128]{1,0:T(8,128)S(1)}, f32[512,128]{1,0:T(8,128)S(1)}, u32[]{:S(2)}, u32[]{:S(2)}) collective-permute-start(f32[512,128]{1,0:T(8,128)S(1)} %get-tuple-element.27), channel_id=1, source_target_pairs={{0,64},{32,96},{64,128},{96,160},{128,192},{160,224},{192,0},{224,... | collective-permute-start | bytes 786440 | tf_op jit(solution)/shard_map/ppermute | solution.py:195
  9.9 13.2 %all_to_all.35.r_ref = f32[8,40,128]{2,1,0:T(8,128)S(1)} all-to-all(f32[8,40,128]{2,1,0:T(8,128)S(1)} %get-tuple-element.22), channel_id=1, replica_groups=mesh['x'=4,'k'=2,'y'=4,'z'=8] {'x','k'}, dimensions={0} | all-to-all | bytes 327680 | tf_op jit(solution)/shard_map/all_to_all | solution.py:199
  23.1 0.9 shard_map.70
  24.0 11.4 %all-to-all-start.1 = ((f32[32,1,640]{2,1,0:T(1,128)}), f32[32,1,640]{2,1,0:T(1,128)S(1)}, u32[]{:S(2)}, u32[]{:S(2)}) async-start(f32[32,1,640]{2,1,0:T(1,128)} %bitcast.4), calls=%async_computation.1 | async-start | bytes 163840 | tf_op jit(solution)/shard_map/all_to_all | solution.py:199
  35.4 1.6 %collective-permute-start.3 = (f32[512,128]{1,0:T(8,128)S(1)}, f32[512,128]{1,0:T(8,128)S(1)}, u32[]{:S(2)}, u32[]{:S(2)}) collective-permute-start(f32[512,128]{1,0:T(8,128)S(1)} %get-tuple-element.29), channel_id=1, source_target_pairs={{0,128},{32,160},{64,192},{96,224},{128,0},{160,32},{192,64},{224,... | collective-permute-start | bytes 786440 | tf_op jit(solution)/shard_map/ppermute | solution.py:195
  37.0 2.9 %collective-permute-start.4 = (f32[512,128]{1,0:T(8,128)S(1)}, f32[512,128]{1,0:T(8,128)S(1)}, u32[]{:S(2)}, u32[]{:S(2)}) collective-permute-start(f32[512,128]{1,0:T(8,128)S(1)} %get-tuple-element.30), channel_id=1, source_target_pairs={{0,160},{32,192},{64,224},{96,0},{128,32},{160,64},{192,96},{224,1... | collective-permute-start | bytes 786440 | tf_op jit(solution)/shard_map/ppermute | solution.py:195
  39.9 0.9 collective-permute-start.5
  41.1 3.6 %all-to-all-done.1 = f32[32,1,640]{2,1,0:T(1,128)S(1)} async-done(((f32[32,1,640]{2,1,0:T(1,128)}), f32[32,1,640]{2,1,0:T(1,128)S(1)}, u32[]{:S(2)}, u32[]{:S(2)}) %all-to-all-start.1) | async-done | bytes 81952 | tf_op jit(solution)/shard_map/all_to_all | solution.py:199
  44.8 1.2 shard_map.71
  45.9 6.2 %all-to-all-start.2 = ((f32[32,4,128]{2,1,0:T(4,128)}), f32[32,4,128]{2,1,0:T(4,128)S(1)}, u32[]{:S(2)}, u32[]{:S(2)}) async-start(f32[32,4,128]{2,1,0:T(4,128)} %bitcast.6), calls=%async_computation.2 | async-start | bytes 131072 | tf_op jit(solution)/shard_map/all_to_all | solution.py:199
  52.1 0.7 collective-permute-done.4.refs_5_
  52.8 4.7 %collective-permute-done.5.refs_6_ = f32[512,128]{1,0:T(8,128)S(1)} collective-permute-done((f32[512,128]{1,0:T(8,128)S(1)}, f32[512,128]{1,0:T(8,128)S(1)}, u32[]{:S(2)}, u32[]{:S(2)}) %collective-permute-start.5) | collective-permute-done | bytes 262176 | tf_op jit(solution)/shard_map/ppermute | solution.py:195
  57.5 2.2 %collective-permute-done.6.refs_7_ = f32[512,128]{1,0:T(8,128)S(1)} collective-permute-done((f32[512,128]{1,0:T(8,128)S(1)}, f32[512,128]{1,0:T(8,128)S(1)}, u32[]{:S(2)}, u32[]{:S(2)}) %collective-permute-start.6) | collective-permute-done | bytes 262176 | tf_op jit(solution)/shard_map/ppermute | solution.py:195
  59.7 1.5 %all-to-all-done.2 = f32[32,4,128]{2,1,0:T(4,128)S(1)} async-done(((f32[32,4,128]{2,1,0:T(4,128)}), f32[32,4,128]{2,1,0:T(4,128)S(1)}, u32[]{:S(2)}, u32[]{:S(2)}) %all-to-all-start.2) | async-done | bytes 65568 | tf_op jit(solution)/shard_map/all_to_all | solution.py:199
  61.3 0.9 copy-done.5
  62.2 1.4 %shard_map.72 = (f32[512,128]{1,0:T(8,128)S(1)}, bf16[512,1024]{1,0:T(8,128)(2,1)S(1)}, bf16[512,1024]{1,0:T(8,128)(2,1)S(1)}) custom-call(f32[128,128]{1,0:T(8,128)S(1)} %bitcast.34, f32[64,32]{1,0:T(8,128)S(1)} %get-tuple-element.24.f2_ref, f32[512,128]{1,0:T(8,128)S(1)} %copy-done.5, f32[512,128]{1,0:T(8,128)S(1)} %collective-permute-done.refs_1_, ...), custom_call_target="tpu_custom_call" | custom-call | flops 1000000000 | bytes 1048576 | tf_op jit(solution)/shard_map/pallas_call | solution.py:221
  63.6 14.6 %all_to_all.36.r_ref = f32[32,16,128]{2,1,0:T(8,128)S(1)} all-to-all(f32[32,16,128]{2,1,0:T(8,128)S(1)} %bitcast.32), channel_id=1, replica_groups=mesh['x'=4,'k'=2,'y'=4,'z'=8] {'x','k','y'}, dimensions={0} | all-to-all | bytes 524288 | tf_op jit(solution)/shard_map/all_to_all | solution.py:199
  78.2 13.9 %all_to_all.37.r_ref = f32[8,16,128]{2,1,0:T(8,128)S(1)} all-to-all(f32[8,16,128]{2,1,0:T(8,128)S(1)} %shard_map.73), channel_id=1, replica_groups=mesh['x'=4,'k'=2,'y'=4,'z'=8] {'z'}, dimensions={0} | all-to-all | bytes 131072 | tf_op jit(solution)/shard_map/all_to_all | solution.py:199
  92.2 12.7 %all_to_all.38 = f32[32,16,128]{2,1,0:T(8,128)S(1)} all-to-all(f32[32,16,128]{2,1,0:T(8,128)S(1)} %shard_map.74), channel_id=1, replica_groups=mesh['x'=4,'k'=2,'y'=4,'z'=8] {'x','k','y'}, dimensions={0} | all-to-all | bytes 524288 | tf_op jit(solution)/shard_map/all_to_all | solution.py:199
  104.9 2.7 %shard_map.75 = (f32[1024,128]{1,0:T(8,128)}, f32[64,1024]{1,0:T(8,128)S(1)}) custom-call(f32[512,128]{1,0:T(8,128)S(1)} %bitcast.33, bf16[512,1024]{1,0:T(8,128)(2,1)S(1)} %get-tuple-element.34.high_ref, bf16[512,1024]{1,0:T(8,128)(2,1)S(1)} %get-tuple-element.35.low_ref, f32[64,32]{1,0:T(8,128)S(1)} %get-tuple-element.24.f2_ref, f32[4,32]{1,0:T(4,128)S(1)} %copy-done), custom_call_target="tpu_custom_call" | custom-call | flops 1000000000 | bytes 1048576 | tf_op jit(solution)/shard_map/pallas_call | solution.py:229
  107.6 6.8 %all-to-all-start.6 = ((f32[256,4,128]{2,1,0:T(4,128)}), f32[256,4,128]{2,1,0:T(4,128)S(1)}, u32[]{:S(2)}, u32[]{:S(2)}) async-start(f32[256,4,128]{2,1,0:T(4,128)} %bitcast.13), calls=%async_computation.6 | async-start | bytes 1048576 | tf_op jit(solution)/shard_map/all_to_all | solution.py:199
  114.4 0.4 fusion.4
  114.8 5.8 %cholesky.17 = f32[64,64]{1,0:T(8,128)S(1)} custom-call(f32[64,64]{1,0:T(8,128)S(1)} %fusion.3), custom_call_target="Cholesky" | custom-call | tf_op jit(solution)/shard_map/jit(cholesky)/cholesky | solution.py:233
  120.7 0.6 compare_reduce_fusion
  121.4 0.7 fusion
  122.0 4.9 %custom-call.7 = f32[1,64,64]{1,2,0:T(8,128)S(1)} custom-call(f32[1,64,64]{2,1,0:T(8,128)S(1)} %fusion), custom_call_target="InvertDiagBlocksLowerTriangular" | custom-call | tf_op jit(solution)/shard_map/jit(_solve_triangular)/triangular_solve | solution.py:234
  127.2 1.1 fusion.5
  128.2 6.5 %all-to-all-done.6 = f32[256,4,128]{2,1,0:T(4,128)S(1)} async-done(((f32[256,4,128]{2,1,0:T(4,128)}), f32[256,4,128]{2,1,0:T(4,128)S(1)}, u32[]{:S(2)}, u32[]{:S(2)}) %all-to-all-start.6) | async-done | bytes 524320 | tf_op jit(solution)/shard_map/all_to_all | solution.py:199
  134.8 0.9 shard_map.76
  (23 shorter events, 0.8 us)
Async XLA Ops:
  0.6 2.4 %copy-start.1 = (f32[1024,64]{0,1:T(8,128)S(1)}, f32[1024,64]{0,1:T(8,128)}, u32[]{:S(2)}) copy-start(f32[1024,64]{0,1:T(8,128)} %param.9) | copy-start | bytes 786436
  0.6 2.4 %copy-start.2 = (f32[32,16]{0,1:T(8,128)S(1)}, f32[32,16]{0,1:T(8,128)}, u32[]{:S(2)}) copy-start(f32[32,16]{0,1:T(8,128)} %param.8) | copy-start | bytes 6148
  0.7 2.4 %copy-start.3 = (f32[8,32]{1,0:T(8,128)S(1)}, f32[8,32]{1,0:T(8,128)}, u32[]{:S(2)}) copy-start(f32[8,32]{1,0:T(8,128)} %f2_ref.1) | copy-start | bytes 3076
  3.1 20.0 %copy-start = (f32[4,32]{1,0:T(4,128)S(1)}, f32[4,32]{1,0:T(4,128)}, u32[]{:S(2)}) copy-start(f32[4,32]{1,0:T(4,128)} %f3_ref.3) | copy-start | bytes 1540
  7.7 0.7 copy-start.4
  8.4 31.5 %collective-permute-start = (f32[512,128]{1,0:T(8,128)S(1)}, f32[512,128]{1,0:T(8,128)S(1)}, u32[]{:S(2)}, u32[]{:S(2)}) collective-permute-start(f32[512,128]{1,0:T(8,128)S(1)} %get-tuple-element.26), channel_id=1, source_target_pairs={{0,32},{32,64},{64,96},{96,128},{128,160},{160,192},{192,224},{224... | collective-permute-start | bytes 786440 | tf_op jit(solution)/shard_map/ppermute | solution.py:195
  8.4 32.4 %collective-permute-start.1 = (f32[512,128]{1,0:T(8,128)S(1)}, f32[512,128]{1,0:T(8,128)S(1)}, u32[]{:S(2)}, u32[]{:S(2)}) collective-permute-start(f32[512,128]{1,0:T(8,128)S(1)} %get-tuple-element.27), channel_id=1, source_target_pairs={{0,64},{32,96},{64,128},{96,160},{128,192},{160,224},{192,0},{224,... | collective-permute-start | bytes 786440 | tf_op jit(solution)/shard_map/ppermute | solution.py:195
  24.0 20.8 %all-to-all-start.1 = ((f32[32,1,640]{2,1,0:T(1,128)}), f32[32,1,640]{2,1,0:T(1,128)S(1)}, u32[]{:S(2)}, u32[]{:S(2)}) async-start(f32[32,1,640]{2,1,0:T(1,128)} %bitcast.4), calls=%async_computation.1 | async-start | bytes 163840 | tf_op jit(solution)/shard_map/all_to_all | solution.py:199
  35.4 16.8 %collective-permute-start.2 = (f32[512,128]{1,0:T(8,128)S(1)}, f32[512,128]{1,0:T(8,128)S(1)}, u32[]{:S(2)}, u32[]{:S(2)}) collective-permute-start(f32[512,128]{1,0:T(8,128)S(1)} %get-tuple-element.28), channel_id=1, source_target_pairs={{0,96},{32,128},{64,160},{96,192},{128,224},{160,0},{192,32},{224,... | collective-permute-start | bytes 786440 | tf_op jit(solution)/shard_map/ppermute | solution.py:195
  35.4 16.7 %collective-permute-start.3 = (f32[512,128]{1,0:T(8,128)S(1)}, f32[512,128]{1,0:T(8,128)S(1)}, u32[]{:S(2)}, u32[]{:S(2)}) collective-permute-start(f32[512,128]{1,0:T(8,128)S(1)} %get-tuple-element.29), channel_id=1, source_target_pairs={{0,128},{32,160},{64,192},{96,224},{128,0},{160,32},{192,64},{224,... | collective-permute-start | bytes 786440 | tf_op jit(solution)/shard_map/ppermute | solution.py:195
  37.0 15.8 %collective-permute-start.4 = (f32[512,128]{1,0:T(8,128)S(1)}, f32[512,128]{1,0:T(8,128)S(1)}, u32[]{:S(2)}, u32[]{:S(2)}) collective-permute-start(f32[512,128]{1,0:T(8,128)S(1)} %get-tuple-element.30), channel_id=1, source_target_pairs={{0,160},{32,192},{64,224},{96,0},{128,32},{160,64},{192,96},{224,1... | collective-permute-start | bytes 786440 | tf_op jit(solution)/shard_map/ppermute | solution.py:195
  39.9 17.6 %collective-permute-start.5 = (f32[512,128]{1,0:T(8,128)S(1)}, f32[512,128]{1,0:T(8,128)S(1)}, u32[]{:S(2)}, u32[]{:S(2)}) collective-permute-start(f32[512,128]{1,0:T(8,128)S(1)} %get-tuple-element.31), channel_id=1, source_target_pairs={{0,192},{32,224},{64,0},{96,32},{128,64},{160,96},{192,128},{224,1... | collective-permute-start | bytes 786440 | tf_op jit(solution)/shard_map/ppermute | solution.py:195
  40.8 18.9 %collective-permute-start.6 = (f32[512,128]{1,0:T(8,128)S(1)}, f32[512,128]{1,0:T(8,128)S(1)}, u32[]{:S(2)}, u32[]{:S(2)}) collective-permute-start(f32[512,128]{1,0:T(8,128)S(1)} %get-tuple-element.32), channel_id=1, source_target_pairs={{0,224},{32,0},{64,32},{96,64},{128,96},{160,128},{192,160},{224,1... | collective-permute-start | bytes 786440 | tf_op jit(solution)/shard_map/ppermute | solution.py:195
  45.9 15.3 %all-to-all-start.2 = ((f32[32,4,128]{2,1,0:T(4,128)}), f32[32,4,128]{2,1,0:T(4,128)S(1)}, u32[]{:S(2)}, u32[]{:S(2)}) async-start(f32[32,4,128]{2,1,0:T(4,128)} %bitcast.6), calls=%async_computation.2 | async-start | bytes 131072 | tf_op jit(solution)/shard_map/all_to_all | solution.py:199
  61.3 1.0 copy-start.5
  107.6 27.2 %all-to-all-start.6 = ((f32[256,4,128]{2,1,0:T(4,128)}), f32[256,4,128]{2,1,0:T(4,128)S(1)}, u32[]{:S(2)}, u32[]{:S(2)}) async-start(f32[256,4,128]{2,1,0:T(4,128)} %bitcast.13), calls=%async_computation.6 | async-start | bytes 1048576 | tf_op jit(solution)/shard_map/all_to_all | solution.py:199
